TPU v7x, 32 devices: a whole 2x2x4 slice. The times are simulated.
32 devices in a mesh: gz: 4 (over z), gy: 4 (over y, x), gx: 2 (over core).
Axes of the slice: x: 2, y: 2, z: 4, core: 2. Of those that a mesh axis runs over, the one named last changes fastest.
Arguments:
- fine_now: float32 [3, 16, 64, 512], P(None, 'gz', 'gy', 'gx'), may hold values from -6 to 6
- fine_prev: float32 [3, 16, 64, 512], P(None, 'gz', 'gy', 'gx'), may hold values from -6 to 6
- stiffness: float32 [9, 16, 64, 512], P(None, 'gz', 'gy', 'gx'), may hold values from 0 to 6, as said below
- metric: float32 [16, 64, 512], P('gz', 'gy', 'gx'), may hold values from 0.7 to 1.4
- density: float32 [16, 64, 512], P('gz', 'gy', 'gx'), may hold values from 1 to 2
- coarse_now: float32 [3, 32, 32, 256], P(None, 'gz', 'gy', 'gx'), may hold values from -6 to 6
- coarse_prev: float32 [3, 32, 32, 256], P(None, 'gz', 'gy', 'gx'), may hold values from -6 to 6
- coarse_stiffness: float32 [9, 32, 32, 256], P(None, 'gz', 'gy', 'gx'), may hold values from 0 to 24, as said below
- coarse_density: float32 [32, 32, 256], P('gz', 'gy', 'gx'), may hold values from 1.5 to 3
Outputs:
- fine_next: float32 [3, 16, 64, 512], P(None, 'gz', 'gy', 'gx')
- coarse_next: float32 [3, 32, 32, 256], P(None, 'gz', 'gy', 'gx')
Inputs may be any that keep to these rules, and one draw needn't show every extreme that they name: `stiffness`: channels 0 to 5 lie in [2, 6] and channels 6 to 8 in [0, 0.9]. `coarse_stiffness`: channels 0 to 5 lie in [8, 24] and channels 6 to 8 in [0, 3.6].
All inputs are finite; a program needn't handle non-finite values.
Results may differ from a plain program's by a relative error of at most 0.00002.
Values sent between devices are 32-bit elements; how exact they have to be, the bound alone decides.
No kernel may reach another device: no remote copies, remote signals or barrier semaphores. Data moves between devices by JAX's collectives and lax.ppermute only.
A program may use at most 64 MiB of HBM per device.

v0:
```python
import jax
import jax.numpy as jnp
from jax import lax
from jax.sharding import PartitionSpec as P

ITERS = 3


TIME_STEP = 0.2


def with_halo(cells, sides, width):
    for axis, dim in sides:
        count = lax.axis_size(axis)
        ends = count - 1
        head = lax.slice_in_dim(cells, 0, width, axis=dim)
        tail = lax.slice_in_dim(cells, cells.shape[dim] - width, cells.shape[dim], axis=dim)
        cells = jnp.concatenate(
            [
                lax.ppermute(tail, axis, [(i, (i + 1) % count) for i in range(ends)]),
                cells,
                lax.ppermute(head, axis, [((i + 1) % count, i) for i in range(ends)]),
            ],
            axis=dim,
        )
    return cells


def passed_along(shard, axis, by):
    length = lax.axis_size(axis)
    pairs = [(i, i + by) for i in range(length) if 0 <= i + by < length]
    return lax.ppermute(shard, axis, pairs)


def along_x(volume, inverse_step):
    return (volume[..., 1:-1, 1:-1, 2:] - volume[..., 1:-1, 1:-1, :-2]) * inverse_step


def along_y(volume, inverse_step):
    return (volume[..., 1:-1, 2:, 1:-1] - volume[..., 1:-1, :-2, 1:-1]) * inverse_step


def along_z(volume, inverse_step, stretch):
    return (volume[..., 2:, 1:-1, 1:-1] - volume[..., :-2, 1:-1, 1:-1]) * inverse_step * stretch


def stresses(padded, stiffness, stretch, inverse_step):
    disp_x, disp_y, disp_z = (padded[0], padded[1], padded[2])
    normal_x = along_x(disp_x, inverse_step)
    normal_y = along_y(disp_y, inverse_step)
    normal_z = along_z(disp_z, inverse_step, stretch)
    stress_xx = stiffness[0] * normal_x + stiffness[6] * normal_y + stiffness[7] * normal_z
    stress_yy = stiffness[6] * normal_x + stiffness[1] * normal_y + stiffness[8] * normal_z
    stress_zz = stiffness[7] * normal_x + stiffness[8] * normal_y + stiffness[2] * normal_z
    stress_yz = stiffness[3] * (
        along_z(disp_y, inverse_step, stretch) + along_y(disp_z, inverse_step)
    )
    stress_xz = stiffness[4] * (
        along_z(disp_x, inverse_step, stretch) + along_x(disp_z, inverse_step)
    )
    stress_xy = stiffness[5] * (along_y(disp_x, inverse_step) + along_x(disp_y, inverse_step))
    return jnp.stack([stress_xx, stress_yy, stress_zz, stress_yz, stress_xz, stress_xy])


def divergence(stress, stretch, inverse_step):
    total_x = (
        along_x(stress[0], inverse_step)
        + along_y(stress[5], inverse_step)
        + along_z(stress[4], inverse_step, stretch)
    )
    total_y = (
        along_x(stress[5], inverse_step)
        + along_y(stress[1], inverse_step)
        + along_z(stress[3], inverse_step, stretch)
    )
    total_z = (
        along_x(stress[4], inverse_step)
        + along_y(stress[3], inverse_step)
        + along_z(stress[2], inverse_step, stretch)
    )
    return jnp.stack([total_x, total_y, total_z])


def prolong_axis(padded, axis):
    length = padded.shape[axis] - 2
    centre = lax.slice_in_dim(padded, 1, length + 1, axis=axis)
    before = lax.slice_in_dim(padded, 0, length, axis=axis)
    behind = lax.slice_in_dim(padded, 2, length + 2, axis=axis)
    even_cells = 0.75 * centre + 0.25 * before
    odd_cells = 0.75 * centre + 0.25 * behind
    new_shape = list(centre.shape)
    new_shape[axis] = 2 * length
    return jnp.stack([even_cells, odd_cells], axis + 1).reshape(new_shape)


def prolong(padded):
    return prolong_axis(prolong_axis(padded, 1), 2)


def restrict(surface):
    row_pairs = surface.reshape(surface.shape[0], surface.shape[1] // 2, 2, surface.shape[2])
    summed = row_pairs[:, :, 0] + row_pairs[:, :, 1]
    col_pairs = summed.reshape(summed.shape[0], summed.shape[1], summed.shape[2] // 2, 2)
    return (col_pairs[..., 0] + col_pairs[..., 1]) * 0.25


def extend_edges(padded):
    plane_y = lax.axis_index("gy")
    plane_x = lax.axis_index("gx")
    upper_rim = jnp.where(plane_y == 0, padded[:, 1:2], padded[:, 0:1])
    bottom = jnp.where(plane_y == lax.axis_size("gy") - 1, padded[:, -2:-1], padded[:, -1:])
    row_fixed = jnp.concatenate([upper_rim, padded[:, 1:-1], bottom], 1)
    left_rim = jnp.where(plane_x == 0, row_fixed[:, :, 1:2], row_fixed[:, :, 0:1])
    right_rim = jnp.where(
        plane_x == lax.axis_size("gx") - 1, row_fixed[:, :, -2:-1], row_fixed[:, :, -1:]
    )
    return jnp.concatenate([left_rim, row_fixed[:, :, 1:-1], right_rim], 2)


def advance(now, prev, stiffness, density, stretch_own, inverse_step, is_fine):
    if is_fine:
        padded = with_halo(now, (("gz", 1), ("gy", 2), ("gx", 3)), 1)
        stress = with_halo(
            stresses(padded, stiffness, stretch_own, inverse_step),
            (("gz", 1), ("gy", 2), ("gx", 3)),
            1,
        )
    else:
        padded = with_halo(now, (("gz", 1), ("gy", 2), ("gx", 3)), 1)
        stress = with_halo(
            stresses(padded, stiffness, stretch_own, inverse_step),
            (("gz", 1), ("gy", 2), ("gx", 3)),
            1,
        )
    internal = divergence(stress, stretch_own, inverse_step)
    return 2.0 * now - prev + TIME_STEP * TIME_STEP * internal / density


def per_device(
    fine_now,
    fine_prev,
    stiffness,
    metric,
    density,
    coarse_now,
    coarse_prev,
    coarse_stiffness,
    coarse_density,
):
    plane_z = lax.axis_index("gz")
    count_z = lax.axis_size("gz")
    layers = fine_now.shape[1]
    layer_index = plane_z * layers + jnp.arange(layers)
    stretch_own = jnp.where((layer_index < count_z * layers // 2)[:, None, None], metric, 1.0)
    fine_step = advance(fine_now, fine_prev, stiffness, density, stretch_own, 0.5, True)
    coarse_step = advance(
        coarse_now, coarse_prev, coarse_stiffness, coarse_density, 1.0, 0.25, False
    )
    fine_start = fine_step[:, -1]
    above = fine_step[:, -2]
    fine_coef = jnp.stack([stiffness[4, -1], stiffness[3, -1], stiffness[2, -1]])
    coarse_start = coarse_step[:, 0]
    below = coarse_step[:, 1]
    coarse_coef = jnp.stack(
        [coarse_stiffness[4, 0], coarse_stiffness[3, 0], coarse_stiffness[2, 0]]
    )
    coarse_iter = coarse_start
    fine_iter = fine_start
    for repeat in range(ITERS):
        lowered = passed_along(restrict(fine_iter), "gz", -3)
        traction = coarse_coef * (below - coarse_iter) * 0.25
        raised = passed_along(traction, "gz", 3)
        padded = with_halo(raised, (("gy", 1), ("gx", 2)), 1)
        fine_later = above + prolong(extend_edges(padded)) / fine_coef
        coarse_iter = 0.5 * (coarse_start + lowered)
        fine_iter = fine_later
    fine_next = fine_step.at[:, -1].set(
        jnp.where(plane_z == count_z - 1, fine_iter, fine_step[:, -1])
    )
    coarse_next = coarse_step.at[:, 0].set(jnp.where(plane_z == 0, coarse_iter, coarse_step[:, 0]))
    return (fine_next, coarse_next)


def solution(mesh):
    placed = (
        P(None, "gz", "gy", "gx"),
        P(None, "gz", "gy", "gx"),
        P(None, "gz", "gy", "gx"),
        P("gz", "gy", "gx"),
        P("gz", "gy", "gx"),
        P(None, "gz", "gy", "gx"),
        P(None, "gz", "gy", "gx"),
        P(None, "gz", "gy", "gx"),
        P("gz", "gy", "gx"),
    )
    return jax.shard_map(
        per_device,
        mesh=mesh,
        in_specs=placed,
        out_specs=(P(None, "gz", "gy", "gx"), P(None, "gz", "gy", "gx")),
        check_vma=False,
    )
```

profile of v0, /device:TPU:2, one launch (start us, length us, event | category | flops | bytes accessed | tf_op | source)
XLA Modules:
  0.0 181.4 jit_solution(43520599597370198)
XLA Ops:
  1.4 3.5 %collective-permute-start.12 = (f32[3,1,8,128]{3,2,1,0:T(8,128)S(1)}, f32[3,1,8,128]{3,2,1,0:T(8,128)S(1)}, u32[]{:S(2)}, u32[]{:S(2)}) collective-permute-start(f32[3,1,8,128]{3,2,1,0:T(8,128)S(1)} %get-tuple-element.96), channel_id=1, source_target_pairs={{0,8},{8,16},{16,24},{1,9},{9,17},{17,25},{2,10},{10,18},{18,26},{... | collective-permute-start | bytes 36872 | tf_op jit(solution)/shard_map/ppermute | solution.py:20
  7.0 4.5 %collective-permute-start = (f32[3,1,16,256]{3,2,1,0:T(8,128)S(1)}, f32[3,1,16,256]{3,2,1,0:T(8,128)S(1)}, u32[]{:S(2)}, u32[]{:S(2)}) collective-permute-start(f32[3,1,16,256]{3,2,1,0:T(8,128)S(1)} %get-tuple-element.89), channel_id=1, source_target_pairs={{0,8},{8,16},{16,24},{1,9},{9,17},{17,25},{2,10},{10,18},{18,26},{... | collective-permute-start | bytes 147464 | tf_op jit(solution)/shard_map/ppermute | solution.py:20
  16.0 3.4 %collective-permute-start.14 = (f32[3,10,1,128]{3,2,1,0:T(1,128)S(1)}, f32[3,10,1,128]{3,2,1,0:T(1,128)S(1)}, u32[]{:S(2)}, u32[]{:S(2)}) collective-permute-start(f32[3,10,1,128]{3,2,1,0:T(1,128)S(1)} %get-tuple-element.94), channel_id=1, source_target_pairs={{0,2},{2,4},{4,6},{1,3},{3,5},{5,7},{8,10},{10,12},{12,14},{9,11},... | collective-permute-start | bytes 46088 | tf_op jit(solution)/shard_map/ppermute | solution.py:20
  19.4 2.4 %collective-permute-start.15 = (f32[3,10,1,128]{3,2,1,0:T(1,128)S(1)}, f32[3,10,1,128]{3,2,1,0:T(1,128)S(1)}, u32[]{:S(2)}, u32[]{:S(2)}) collective-permute-start(f32[3,10,1,128]{3,2,1,0:T(1,128)S(1)} %get-tuple-element.93), channel_id=1, source_target_pairs={{2,0},{4,2},{6,4},{3,1},{5,3},{7,5},{10,8},{12,10},{14,12},{11,9},... | collective-permute-start | bytes 46088 | tf_op jit(solution)/shard_map/ppermute | solution.py:22
  22.0 3.9 %collective-permute-done.15 = f32[3,10,1,128]{3,2,1,0:T(1,128)S(1)} collective-permute-done((f32[3,10,1,128]{3,2,1,0:T(1,128)S(1)}, f32[3,10,1,128]{3,2,1,0:T(1,128)S(1)}, u32[]{:S(2)}, u32[]{:S(2)}) %collective-permute-start.15) | collective-permute-done | bytes 15392 | tf_op jit(solution)/shard_map/ppermute | solution.py:22
  28.8 2.0 %collective-permute-done.17 = f32[3,10,10,1]{3,0,2,1:T(4,128)S(1)} collective-permute-done((f32[3,10,10,1]{3,0,2,1:T(4,128)S(1)}, f32[3,10,10,1]{3,0,2,1:T(4,128)S(1)}, u32[]{:S(2)}, u32[]{:S(2)}) %collective-permute-start.17) | collective-permute-done | bytes 1232 | tf_op jit(solution)/shard_map/ppermute | solution.py:22
  32.6 4.5 %collective-permute-start.18 = (f32[6,1,8,128]{3,2,1,0:T(8,128)S(1)}, f32[6,1,8,128]{3,2,1,0:T(8,128)S(1)}, u32[]{:S(2)}, u32[]{:S(2)}) collective-permute-start(f32[6,1,8,128]{3,2,1,0:T(8,128)S(1)} %get-tuple-element.86), channel_id=1, source_target_pairs={{0,8},{8,16},{16,24},{1,9},{9,17},{17,25},{2,10},{10,18},{18,26},{... | collective-permute-start | bytes 73736 | tf_op jit(solution)/shard_map/ppermute | solution.py:20
  38.5 2.5 %collective-permute-start.2 = (f32[3,6,1,256]{3,2,1,0:T(1,128)S(1)}, f32[3,6,1,256]{3,2,1,0:T(1,128)S(1)}, u32[]{:S(2)}, u32[]{:S(2)}) collective-permute-start(f32[3,6,1,256]{3,2,1,0:T(1,128)S(1)} %get-tuple-element.76), channel_id=1, source_target_pairs={{0,2},{2,4},{4,6},{1,3},{3,5},{5,7},{8,10},{10,12},{12,14},{9,11},... | collective-permute-start | bytes 55304 | tf_op jit(solution)/shard_map/ppermute | solution.py:20
  41.1 3.3 %collective-permute-start.3 = (f32[3,6,1,256]{3,2,1,0:T(1,128)S(1)}, f32[3,6,1,256]{3,2,1,0:T(1,128)S(1)}, u32[]{:S(2)}, u32[]{:S(2)}) collective-permute-start(f32[3,6,1,256]{3,2,1,0:T(1,128)S(1)} %get-tuple-element.77), channel_id=1, source_target_pairs={{2,0},{4,2},{6,4},{3,1},{5,3},{7,5},{10,8},{12,10},{14,12},{11,9},... | collective-permute-start | bytes 55304 | tf_op jit(solution)/shard_map/ppermute | solution.py:22
  44.5 3.1 %collective-permute-done.3 = f32[3,6,1,256]{3,2,1,0:T(1,128)S(1)} collective-permute-done((f32[3,6,1,256]{3,2,1,0:T(1,128)S(1)}, f32[3,6,1,256]{3,2,1,0:T(1,128)S(1)}, u32[]{:S(2)}, u32[]{:S(2)}) %collective-permute-start.3) | collective-permute-done | bytes 18464 | tf_op jit(solution)/shard_map/ppermute | solution.py:22
  50.5 1.9 %collective-permute-start.20 = (f32[6,10,1,128]{3,2,1,0:T(1,128)S(1)}, f32[6,10,1,128]{3,2,1,0:T(1,128)S(1)}, u32[]{:S(2)}, u32[]{:S(2)}) collective-permute-start(f32[6,10,1,128]{3,2,1,0:T(1,128)S(1)} %get-tuple-element.81), channel_id=1, source_target_pairs={{0,2},{2,4},{4,6},{1,3},{3,5},{5,7},{8,10},{10,12},{12,14},{9,11},... | collective-permute-start | bytes 92168 | tf_op jit(solution)/shard_map/ppermute | solution.py:20
  52.4 4.1 %collective-permute-start.21 = (f32[6,10,1,128]{3,2,1,0:T(1,128)S(1)}, f32[6,10,1,128]{3,2,1,0:T(1,128)S(1)}, u32[]{:S(2)}, u32[]{:S(2)}) collective-permute-start(f32[6,10,1,128]{3,2,1,0:T(1,128)S(1)} %get-tuple-element.80), channel_id=1, source_target_pairs={{2,0},{4,2},{6,4},{3,1},{5,3},{7,5},{10,8},{12,10},{14,12},{11,9},... | collective-permute-start | bytes 92168 | tf_op jit(solution)/shard_map/ppermute | solution.py:22
  57.7 1.7 collective-permute-done.21
  59.6 2.0 %collective-permute-start.22 = (f32[6,10,10,1]{3,0,2,1:T(8,128)S(1)}, f32[6,10,10,1]{3,0,2,1:T(8,128)S(1)}, u32[]{:S(2)}, u32[]{:S(2)}) collective-permute-start(f32[6,10,10,1]{3,0,2,1:T(8,128)S(1)} %get-tuple-element.63), channel_id=1, source_target_pairs={{0,1},{2,3},{4,5},{6,7},{8,9},{10,11},{12,13},{14,15},{16,17},{18,... | collective-permute-start | bytes 7208 | tf_op jit(solution)/shard_map/ppermute | solution.py:20
  63.1 2.2 %collective-permute-done.23 = f32[6,10,10,1]{3,0,2,1:T(8,128)S(1)} collective-permute-done((f32[6,10,10,1]{3,0,2,1:T(8,128)S(1)}, f32[6,10,10,1]{3,0,2,1:T(8,128)S(1)}, u32[]{:S(2)}, u32[]{:S(2)}) %collective-permute-start.23) | collective-permute-done | bytes 2432 | tf_op jit(solution)/shard_map/ppermute | solution.py:22
  65.3 2.0 %pad_maximum_fusion.11 = (f32[1,10,10,130]{3,0,2,1:T(1,128)S(1)}, f32[1,10,10,130]{3,0,2,1:T(1,128)S(1)}, f32[1,10,10,130]{3,0,2,1:T(1,128)S(1)}, f32[1,10,10,13...) fusion(f32[6,10,10,1]{3,0,2,1:T(8,128)S(1)} %collective-permute-done.23, ...), kind=kLoop, calls=%fused_computation.34 | loop fusion | flops 156000 | bytes 624000 | tf_op jit(solution)/shard_map/slice | solution.py:67
  68.3 6.6 %collective-permute-start.24 = (f32[3,8,128]{2,1,0:T(8,128)S(1)}, f32[3,8,128]{2,1,0:T(8,128)S(1)}, u32[]{:S(2)}, u32[]{:S(2)}) collective-permute-start(f32[3,8,128]{2,1,0:T(8,128)S(1)} %multiply_multiply_fusion.2), channel_id=1, source_target_pairs={{0,24},{1,25},{2,26},{3,27},{4,28},{5,29},{6,30},{7,31}} | collective-permute-start | bytes 36872 | tf_op jit(solution)/shard_map/ppermute | solution.py:32
  76.3 1.9 %collective-permute-start.25 = (f32[3,1,128]{2,1,0:T(1,128)S(1)}, f32[3,1,128]{2,1,0:T(1,128)S(1)}, u32[]{:S(2)}, u32[]{:S(2)}) collective-permute-start(f32[3,1,128]{2,1,0:T(1,128)S(1)} %get-tuple-element.132), channel_id=1, source_target_pairs={{0,2},{2,4},{4,6},{1,3},{3,5},{5,7},{8,10},{10,12},{12,14},{9,11},... | collective-permute-start | bytes 4616 | tf_op jit(solution)/shard_map/ppermute | solution.py:20
  79.5 3.9 %collective-permute-start.26 = (f32[3,1,128]{2,1,0:T(1,128)S(1)}, f32[3,1,128]{2,1,0:T(1,128)S(1)}, u32[]{:S(2)}, u32[]{:S(2)}) collective-permute-start(f32[3,1,128]{2,1,0:T(1,128)S(1)} %get-tuple-element.131), channel_id=1, source_target_pairs={{2,0},{4,2},{6,4},{3,1},{5,3},{7,5},{10,8},{12,10},{14,12},{11,9},... | collective-permute-start | bytes 4616 | tf_op jit(solution)/shard_map/ppermute | solution.py:22
  83.5 2.4 %collective-permute-done.26 = f32[3,1,128]{2,1,0:T(1,128)S(1)} collective-permute-done((f32[3,1,128]{2,1,0:T(1,128)S(1)}, f32[3,1,128]{2,1,0:T(1,128)S(1)}, u32[]{:S(2)}, u32[]{:S(2)}) %collective-permute-start.26) | collective-permute-done | bytes 1568 | tf_op jit(solution)/shard_map/ppermute | solution.py:22
  91.0 5.0 %collective-permute-done.7 = f32[6,1,16,256]{3,2,1,0:T(8,128)S(1)} collective-permute-done((f32[6,1,16,256]{3,2,1,0:T(8,128)S(1)}, f32[6,1,16,256]{3,2,1,0:T(8,128)S(1)}, u32[]{:S(2)}, u32[]{:S(2)}) %collective-permute-start.7) | collective-permute-done | bytes 98336 | tf_op jit(solution)/shard_map/ppermute | solution.py:22
  96.0 1.9 %collective-permute-start.8 = (f32[6,6,1,256]{3,2,1,0:T(1,128)S(1)}, f32[6,6,1,256]{3,2,1,0:T(1,128)S(1)}, u32[]{:S(2)}, u32[]{:S(2)}) collective-permute-start(f32[6,6,1,256]{3,2,1,0:T(1,128)S(1)} %get-tuple-element.59), channel_id=1, source_target_pairs={{0,2},{2,4},{4,6},{1,3},{3,5},{5,7},{8,10},{10,12},{12,14},{9,11},... | collective-permute-start | bytes 110600 | tf_op jit(solution)/shard_map/ppermute | solution.py:20
  98.0 3.9 %collective-permute-start.9 = (f32[6,6,1,256]{3,2,1,0:T(1,128)S(1)}, f32[6,6,1,256]{3,2,1,0:T(1,128)S(1)}, u32[]{:S(2)}, u32[]{:S(2)}) collective-permute-start(f32[6,6,1,256]{3,2,1,0:T(1,128)S(1)} %get-tuple-element.60), channel_id=1, source_target_pairs={{2,0},{4,2},{6,4},{3,1},{5,3},{7,5},{10,8},{12,10},{14,12},{11,9},... | collective-permute-start | bytes 110600 | tf_op jit(solution)/shard_map/ppermute | solution.py:22
  102.0 2.7 %collective-permute-done.9 = f32[6,6,1,256]{3,2,1,0:T(1,128)S(1)} collective-permute-done((f32[6,6,1,256]{3,2,1,0:T(1,128)S(1)}, f32[6,6,1,256]{3,2,1,0:T(1,128)S(1)}, u32[]{:S(2)}, u32[]{:S(2)}) %collective-permute-start.9) | collective-permute-done | bytes 36896 | tf_op jit(solution)/shard_map/ppermute | solution.py:22
  105.9 2.1 %collective-permute-start.10 = (f32[6,6,18,1]{3,2,1,0:T(8,128)}, f32[6,6,18,1]{3,2,1,0:T(8,128)}, u32[]{:S(2)}, u32[]{:S(2)}) collective-permute-start(f32[6,6,18,1]{3,2,1,0:T(8,128)} %get-tuple-element.48), channel_id=1, source_target_pairs={{0,1},{2,3},{4,5},{6,7},{8,9},{10,11},{12,13},{14,15},{16,17},{18,... | collective-permute-start | bytes 7784 | tf_op jit(solution)/shard_map/ppermute | solution.py:20
  108.0 1.5 collective-permute-start.11
  110.1 1.8 copy.291
  111.9 2.8 %reshape.170 = f32[3,8,2,256]{3,2,1,0:T(2,128)} reshape(f32[3,16,128,2]{3,2,1,0:T(8,128)S(1)} %copy.291) | data formatting | bytes 98304 | tf_op jit(solution)/shard_map/reshape | solution.py:93
  114.6 2.1 %pad_maximum_fusion = f32[6,6,18,258]{3,2,1,0:T(8,128)S(1)} fusion(f32[6,6,18,1]{3,2,1,0:T(8,128)} %collective-permute-done.11, f32[6,6,1,256]{3,2,1,0:T(1,128)} %copy-done.20, f32[6,1,16,256]{3,2,1,0:T(8,128)} %copy-done.6, f32[6,4,16,256]{3,2,1,0:T(8,128)S(1)} %constant_dynamic-update-slice_fusion.3, f32[6,1,16,256]{3,2,1,0:T(8,128)} %copy-done.5, ...), kind=kLoop, calls=%fused_computation | loop fusion | flops 1003104 | bytes 1337472 | tf_op jit(solution)/shard_map/concatenate | solution.py:18
  118.9 1.3 collective-permute-start.29
  120.3 6.1 %collective-permute-done.29 = f32[3,8,128]{2,1,0:T(8,128)S(1)} collective-permute-done((f32[3,8,128]{2,1,0:T(8,128)S(1)}, f32[3,8,128]{2,1,0:T(8,128)S(1)}, u32[]{:S(2)}, u32[]{:S(2)}) %collective-permute-start.29) | collective-permute-done | bytes 12320 | tf_op jit(solution)/shard_map/ppermute | solution.py:32
  127.1 1.6 collective-permute-start.30
  128.7 1.4 collective-permute-done.30
  130.1 1.9 %collective-permute-start.31 = (f32[3,1,128]{2,1,0:T(1,128)S(1)}, f32[3,1,128]{2,1,0:T(1,128)S(1)}, u32[]{:S(2)}, u32[]{:S(2)}) collective-permute-start(f32[3,1,128]{2,1,0:T(1,128)S(1)} %get-tuple-element.130), channel_id=1, source_target_pairs={{0,2},{2,4},{4,6},{1,3},{3,5},{5,7},{8,10},{10,12},{12,14},{9,11},... | collective-permute-start | bytes 4616 | tf_op jit(solution)/shard_map/ppermute | solution.py:20
  132.0 3.9 %collective-permute-start.32 = (f32[3,1,128]{2,1,0:T(1,128)S(1)}, f32[3,1,128]{2,1,0:T(1,128)S(1)}, u32[]{:S(2)}, u32[]{:S(2)}) collective-permute-start(f32[3,1,128]{2,1,0:T(1,128)S(1)} %get-tuple-element.129), channel_id=1, source_target_pairs={{2,0},{4,2},{6,4},{3,1},{5,3},{7,5},{10,8},{12,10},{14,12},{11,9},... | collective-permute-start | bytes 4616 | tf_op jit(solution)/shard_map/ppermute | solution.py:22
  136.0 2.4 %collective-permute-done.32 = f32[3,1,128]{2,1,0:T(1,128)S(1)} collective-permute-done((f32[3,1,128]{2,1,0:T(1,128)S(1)}, f32[3,1,128]{2,1,0:T(1,128)S(1)}, u32[]{:S(2)}, u32[]{:S(2)}) %collective-permute-start.32) | collective-permute-done | bytes 1568 | tf_op jit(solution)/shard_map/ppermute | solution.py:22
  141.1 1.8 collective-permute-done.34
  144.8 1.3 collective-permute-start.35
  146.1 6.1 %collective-permute-done.35 = f32[3,8,128]{2,1,0:T(8,128)S(1)} collective-permute-done((f32[3,8,128]{2,1,0:T(8,128)S(1)}, f32[3,8,128]{2,1,0:T(8,128)S(1)}, u32[]{:S(2)}, u32[]{:S(2)}) %collective-permute-start.35) | collective-permute-done | bytes 12320 | tf_op jit(solution)/shard_map/ppermute | solution.py:32
  152.9 1.6 collective-permute-start.36
  154.5 1.4 collective-permute-done.36
  155.9 1.9 %collective-permute-start.37 = (f32[3,1,128]{2,1,0:T(1,128)S(1)}, f32[3,1,128]{2,1,0:T(1,128)S(1)}, u32[]{:S(2)}, u32[]{:S(2)}) collective-permute-start(f32[3,1,128]{2,1,0:T(1,128)S(1)} %get-tuple-element.128), channel_id=1, source_target_pairs={{0,2},{2,4},{4,6},{1,3},{3,5},{5,7},{8,10},{10,12},{12,14},{9,11},... | collective-permute-start | bytes 4616 | tf_op jit(solution)/shard_map/ppermute | solution.py:20
  157.8 3.9 %collective-permute-start.38 = (f32[3,1,128]{2,1,0:T(1,128)S(1)}, f32[3,1,128]{2,1,0:T(1,128)S(1)}, u32[]{:S(2)}, u32[]{:S(2)}) collective-permute-start(f32[3,1,128]{2,1,0:T(1,128)S(1)} %get-tuple-element.127), channel_id=1, source_target_pairs={{2,0},{4,2},{6,4},{3,1},{5,3},{7,5},{10,8},{12,10},{14,12},{11,9},... | collective-permute-start | bytes 4616 | tf_op jit(solution)/shard_map/ppermute | solution.py:22
  161.8 2.4 %collective-permute-done.38 = f32[3,1,128]{2,1,0:T(1,128)S(1)} collective-permute-done((f32[3,1,128]{2,1,0:T(1,128)S(1)}, f32[3,1,128]{2,1,0:T(1,128)S(1)}, u32[]{:S(2)}, u32[]{:S(2)}) %collective-permute-start.38) | collective-permute-done | bytes 1568 | tf_op jit(solution)/shard_map/ppermute | solution.py:22
  166.9 1.8 collective-permute-done.40
  170.5 2.2 %reshape.174 = f32[3,8,2,256]{3,2,1,0:T(2,128)S(1)} reshape(f32[3,16,128,2]{3,2,1,0:T(8,128)S(1)} %copy.308) | data formatting | bytes 98304 | tf_op jit(solution)/shard_map/reshape | solution.py:93
  173.4 1.3 collective-permute-start.41
  175.4 5.4 %collective-permute-done.41 = f32[3,8,128]{2,1,0:T(8,128)S(1)} collective-permute-done((f32[3,8,128]{2,1,0:T(8,128)S(1)}, f32[3,8,128]{2,1,0:T(8,128)S(1)}, u32[]{:S(2)}, u32[]{:S(2)}) %collective-permute-start.41) | collective-permute-done | bytes 12320 | tf_op jit(solution)/shard_map/ppermute | solution.py:32
  (256 shorter events, 43.8 us)
Async XLA Ops:
  1.4 13.6 %collective-permute-start.12 = (f32[3,1,8,128]{3,2,1,0:T(8,128)S(1)}, f32[3,1,8,128]{3,2,1,0:T(8,128)S(1)}, u32[]{:S(2)}, u32[]{:S(2)}) collective-permute-start(f32[3,1,8,128]{3,2,1,0:T(8,128)S(1)} %get-tuple-element.96), channel_id=1, source_target_pairs={{0,8},{8,16},{16,24},{1,9},{9,17},{17,25},{2,10},{10,18},{18,26},{... | collective-permute-start | bytes 36872 | tf_op jit(solution)/shard_map/ppermute | solution.py:20
  4.8 11.1 %collective-permute-start.13 = (f32[3,1,8,128]{3,2,1,0:T(8,128)S(1)}, f32[3,1,8,128]{3,2,1,0:T(8,128)S(1)}, u32[]{:S(2)}, u32[]{:S(2)}) collective-permute-start(f32[3,1,8,128]{3,2,1,0:T(8,128)S(1)} %get-tuple-element.95), channel_id=1, source_target_pairs={{8,0},{16,8},{24,16},{9,1},{17,9},{25,17},{10,2},{18,10},{26,18},{... | collective-permute-start | bytes 36872 | tf_op jit(solution)/shard_map/ppermute | solution.py:22
  7.0 31.5 %collective-permute-start = (f32[3,1,16,256]{3,2,1,0:T(8,128)S(1)}, f32[3,1,16,256]{3,2,1,0:T(8,128)S(1)}, u32[]{:S(2)}, u32[]{:S(2)}) collective-permute-start(f32[3,1,16,256]{3,2,1,0:T(8,128)S(1)} %get-tuple-element.89), channel_id=1, source_target_pairs={{0,8},{8,16},{16,24},{1,9},{9,17},{17,25},{2,10},{10,18},{18,26},{... | collective-permute-start | bytes 147464 | tf_op jit(solution)/shard_map/ppermute | solution.py:20
  11.5 27.0 %collective-permute-start.1 = (f32[3,1,16,256]{3,2,1,0:T(8,128)S(1)}, f32[3,1,16,256]{3,2,1,0:T(8,128)S(1)}, u32[]{:S(2)}, u32[]{:S(2)}) collective-permute-start(f32[3,1,16,256]{3,2,1,0:T(8,128)S(1)} %get-tuple-element.88), channel_id=1, source_target_pairs={{8,0},{16,8},{24,16},{9,1},{17,9},{25,17},{10,2},{18,10},{26,18},{... | collective-permute-start | bytes 147464 | tf_op jit(solution)/shard_map/ppermute | solution.py:22
  13.5 54.7 %copy-start.23 = (f32[1,8,128]{2,1,0:T(8,128)}, f32[1,8,128]{2,1,0:T(8,128)S(1)}, u32[]{:S(2)}) copy-start(f32[1,8,128]{2,1,0:T(8,128)S(1)} %get-tuple-element.73) | copy-start | bytes 12292
  13.5 54.7 %copy-start.25 = (f32[1,8,128]{2,1,0:T(8,128)}, f32[1,8,128]{2,1,0:T(8,128)S(1)}, u32[]{:S(2)}) copy-start(f32[1,8,128]{2,1,0:T(8,128)S(1)} %get-tuple-element.74) | copy-start | bytes 12292
  13.5 54.7 %copy-start.27 = (f32[1,8,128]{2,1,0:T(8,128)}, f32[1,8,128]{2,1,0:T(8,128)S(1)}, u32[]{:S(2)}) copy-start(f32[1,8,128]{2,1,0:T(8,128)S(1)} %get-tuple-element.75) | copy-start | bytes 12292
  16.0 5.9 %collective-permute-start.14 = (f32[3,10,1,128]{3,2,1,0:T(1,128)S(1)}, f32[3,10,1,128]{3,2,1,0:T(1,128)S(1)}, u32[]{:S(2)}, u32[]{:S(2)}) collective-permute-start(f32[3,10,1,128]{3,2,1,0:T(1,128)S(1)} %get-tuple-element.94), channel_id=1, source_target_pairs={{0,2},{2,4},{4,6},{1,3},{3,5},{5,7},{8,10},{10,12},{12,14},{9,11},... | collective-permute-start | bytes 46088 | tf_op jit(solution)/shard_map/ppermute | solution.py:20
  19.4 6.5 %collective-permute-start.15 = (f32[3,10,1,128]{3,2,1,0:T(1,128)S(1)}, f32[3,10,1,128]{3,2,1,0:T(1,128)S(1)}, u32[]{:S(2)}, u32[]{:S(2)}) collective-permute-start(f32[3,10,1,128]{3,2,1,0:T(1,128)S(1)} %get-tuple-element.93), channel_id=1, source_target_pairs={{2,0},{4,2},{6,4},{3,1},{5,3},{7,5},{10,8},{12,10},{14,12},{11,9},... | collective-permute-start | bytes 46088 | tf_op jit(solution)/shard_map/ppermute | solution.py:22
  26.1 2.7 %collective-permute-start.16 = (f32[3,10,10,1]{3,0,2,1:T(4,128)S(1)}, f32[3,10,10,1]{3,0,2,1:T(4,128)S(1)}, u32[]{:S(2)}, u32[]{:S(2)}) collective-permute-start(f32[3,10,10,1]{3,0,2,1:T(4,128)S(1)} %get-tuple-element.82), channel_id=1, source_target_pairs={{0,1},{2,3},{4,5},{6,7},{8,9},{10,11},{12,13},{14,15},{16,17},{18,... | collective-permute-start | bytes 3608 | tf_op jit(solution)/shard_map/ppermute | solution.py:20
  27.4 3.3 %collective-permute-start.17 = (f32[3,10,10,1]{3,0,2,1:T(4,128)S(1)}, f32[3,10,10,1]{3,0,2,1:T(4,128)S(1)}, u32[]{:S(2)}, u32[]{:S(2)}) collective-permute-start(f32[3,10,10,1]{3,0,2,1:T(4,128)S(1)} %get-tuple-element.83), channel_id=1, source_target_pairs={{1,0},{3,2},{5,4},{7,6},{9,8},{11,10},{13,12},{15,14},{17,16},{19,... | collective-permute-start | bytes 3608 | tf_op jit(solution)/shard_map/ppermute | solution.py:22
  28.8 34.2 %copy-start.30 = (pred[4]{0:T(512)(128)(4,1)}, pred[4]{0:T(512)(128)(4,1)S(1)}, u32[]{:S(2)}) copy-start(pred[4]{0:T(512)(128)(4,1)S(1)} %add_compare_fusion) | copy-start | bytes 16
  32.6 11.8 %collective-permute-start.18 = (f32[6,1,8,128]{3,2,1,0:T(8,128)S(1)}, f32[6,1,8,128]{3,2,1,0:T(8,128)S(1)}, u32[]{:S(2)}, u32[]{:S(2)}) collective-permute-start(f32[6,1,8,128]{3,2,1,0:T(8,128)S(1)} %get-tuple-element.86), channel_id=1, source_target_pairs={{0,8},{8,16},{16,24},{1,9},{9,17},{17,25},{2,10},{10,18},{18,26},{... | collective-permute-start | bytes 73736 | tf_op jit(solution)/shard_map/ppermute | solution.py:20
  37.1 7.3 %collective-permute-start.19 = (f32[6,1,8,128]{3,2,1,0:T(8,128)S(1)}, f32[6,1,8,128]{3,2,1,0:T(8,128)S(1)}, u32[]{:S(2)}, u32[]{:S(2)}) collective-permute-start(f32[6,1,8,128]{3,2,1,0:T(8,128)S(1)} %get-tuple-element.87), channel_id=1, source_target_pairs={{8,0},{16,8},{24,16},{9,1},{17,9},{25,17},{10,2},{18,10},{26,18},{... | collective-permute-start | bytes 73736 | tf_op jit(solution)/shard_map/ppermute | solution.py:22
  38.5 5.9 %collective-permute-start.2 = (f32[3,6,1,256]{3,2,1,0:T(1,128)S(1)}, f32[3,6,1,256]{3,2,1,0:T(1,128)S(1)}, u32[]{:S(2)}, u32[]{:S(2)}) collective-permute-start(f32[3,6,1,256]{3,2,1,0:T(1,128)S(1)} %get-tuple-element.76), channel_id=1, source_target_pairs={{0,2},{2,4},{4,6},{1,3},{3,5},{5,7},{8,10},{10,12},{12,14},{9,11},... | collective-permute-start | bytes 55304 | tf_op jit(solution)/shard_map/ppermute | solution.py:20
  41.1 6.6 %collective-permute-start.3 = (f32[3,6,1,256]{3,2,1,0:T(1,128)S(1)}, f32[3,6,1,256]{3,2,1,0:T(1,128)S(1)}, u32[]{:S(2)}, u32[]{:S(2)}) collective-permute-start(f32[3,6,1,256]{3,2,1,0:T(1,128)S(1)} %get-tuple-element.77), channel_id=1, source_target_pairs={{2,0},{4,2},{6,4},{3,1},{5,3},{7,5},{10,8},{12,10},{14,12},{11,9},... | collective-permute-start | bytes 55304 | tf_op jit(solution)/shard_map/ppermute | solution.py:22
  47.8 8.7 %collective-permute-start.4 = (f32[3,6,18,1]{3,2,1,0:T(8,128)S(1)}, f32[3,6,18,1]{3,2,1,0:T(8,128)S(1)}, u32[]{:S(2)}, u32[]{:S(2)}) collective-permute-start(f32[3,6,18,1]{3,2,1,0:T(8,128)S(1)} %get-tuple-element.61), channel_id=1, source_target_pairs={{0,1},{2,3},{4,5},{6,7},{8,9},{10,11},{12,13},{14,15},{16,17},{18,... | collective-permute-start | bytes 3896 | tf_op jit(solution)/shard_map/ppermute | solution.py:20
  49.1 7.4 %collective-permute-start.5 = (f32[3,6,18,1]{3,2,1,0:T(8,128)S(1)}, f32[3,6,18,1]{3,2,1,0:T(8,128)S(1)}, u32[]{:S(2)}, u32[]{:S(2)}) collective-permute-start(f32[3,6,18,1]{3,2,1,0:T(8,128)S(1)} %get-tuple-element.62), channel_id=1, source_target_pairs={{1,0},{3,2},{5,4},{7,6},{9,8},{11,10},{13,12},{15,14},{17,16},{19,... | collective-permute-start | bytes 3896 | tf_op jit(solution)/shard_map/ppermute | solution.py:22
  50.5 7.1 %collective-permute-start.20 = (f32[6,10,1,128]{3,2,1,0:T(1,128)S(1)}, f32[6,10,1,128]{3,2,1,0:T(1,128)S(1)}, u32[]{:S(2)}, u32[]{:S(2)}) collective-permute-start(f32[6,10,1,128]{3,2,1,0:T(1,128)S(1)} %get-tuple-element.81), channel_id=1, source_target_pairs={{0,2},{2,4},{4,6},{1,3},{3,5},{5,7},{8,10},{10,12},{12,14},{9,11},... | collective-permute-start | bytes 92168 | tf_op jit(solution)/shard_map/ppermute | solution.py:20
  52.4 7.0 %collective-permute-start.21 = (f32[6,10,1,128]{3,2,1,0:T(1,128)S(1)}, f32[6,10,1,128]{3,2,1,0:T(1,128)S(1)}, u32[]{:S(2)}, u32[]{:S(2)}) collective-permute-start(f32[6,10,1,128]{3,2,1,0:T(1,128)S(1)} %get-tuple-element.80), channel_id=1, source_target_pairs={{2,0},{4,2},{6,4},{3,1},{5,3},{7,5},{10,8},{12,10},{14,12},{11,9},... | collective-permute-start | bytes 92168 | tf_op jit(solution)/shard_map/ppermute | solution.py:22
  59.6 3.5 %collective-permute-start.22 = (f32[6,10,10,1]{3,0,2,1:T(8,128)S(1)}, f32[6,10,10,1]{3,0,2,1:T(8,128)S(1)}, u32[]{:S(2)}, u32[]{:S(2)}) collective-permute-start(f32[6,10,10,1]{3,0,2,1:T(8,128)S(1)} %get-tuple-element.63), channel_id=1, source_target_pairs={{0,1},{2,3},{4,5},{6,7},{8,9},{10,11},{12,13},{14,15},{16,17},{18,... | collective-permute-start | bytes 7208 | tf_op jit(solution)/shard_map/ppermute | solution.py:20
  61.6 3.6 %collective-permute-start.23 = (f32[6,10,10,1]{3,0,2,1:T(8,128)S(1)}, f32[6,10,10,1]{3,0,2,1:T(8,128)S(1)}, u32[]{:S(2)}, u32[]{:S(2)}) collective-permute-start(f32[6,10,10,1]{3,0,2,1:T(8,128)S(1)} %get-tuple-element.64), channel_id=1, source_target_pairs={{1,0},{3,2},{5,4},{7,6},{9,8},{11,10},{13,12},{15,14},{17,16},{19,... | collective-permute-start | bytes 7208 | tf_op jit(solution)/shard_map/ppermute | solution.py:22
  68.3 8.0 %collective-permute-start.24 = (f32[3,8,128]{2,1,0:T(8,128)S(1)}, f32[3,8,128]{2,1,0:T(8,128)S(1)}, u32[]{:S(2)}, u32[]{:S(2)}) collective-permute-start(f32[3,8,128]{2,1,0:T(8,128)S(1)} %multiply_multiply_fusion.2), channel_id=1, source_target_pairs={{0,24},{1,25},{2,26},{3,27},{4,28},{5,29},{6,30},{7,31}} | collective-permute-start | bytes 36872 | tf_op jit(solution)/shard_map/ppermute | solution.py:32
  76.3 7.2 %collective-permute-start.25 = (f32[3,1,128]{2,1,0:T(1,128)S(1)}, f32[3,1,128]{2,1,0:T(1,128)S(1)}, u32[]{:S(2)}, u32[]{:S(2)}) collective-permute-start(f32[3,1,128]{2,1,0:T(1,128)S(1)} %get-tuple-element.132), channel_id=1, source_target_pairs={{0,2},{2,4},{4,6},{1,3},{3,5},{5,7},{8,10},{10,12},{12,14},{9,11},... | collective-permute-start | bytes 4616 | tf_op jit(solution)/shard_map/ppermute | solution.py:20
  78.2 12.8 %collective-permute-start.6 = (f32[6,1,16,256]{3,2,1,0:T(8,128)S(1)}, f32[6,1,16,256]{3,2,1,0:T(8,128)S(1)}, u32[]{:S(2)}, u32[]{:S(2)}) collective-permute-start(f32[6,1,16,256]{3,2,1,0:T(8,128)S(1)} %get-tuple-element.71), channel_id=1, source_target_pairs={{0,8},{8,16},{16,24},{1,9},{9,17},{17,25},{2,10},{10,18},{18,26},{... | collective-permute-start | bytes 294920 | tf_op jit(solution)/shard_map/ppermute | solution.py:20
  79.5 6.4 %collective-permute-start.26 = (f32[3,1,128]{2,1,0:T(1,128)S(1)}, f32[3,1,128]{2,1,0:T(1,128)S(1)}, u32[]{:S(2)}, u32[]{:S(2)}) collective-permute-start(f32[3,1,128]{2,1,0:T(1,128)S(1)} %get-tuple-element.131), channel_id=1, source_target_pairs={{2,0},{4,2},{6,4},{3,1},{5,3},{7,5},{10,8},{12,10},{14,12},{11,9},... | collective-permute-start | bytes 4616 | tf_op jit(solution)/shard_map/ppermute | solution.py:22
  86.0 3.9 %collective-permute-start.27 = (f32[3,10,1]{2,0,1:T(4,128)S(1)}, f32[3,10,1]{2,0,1:T(4,128)S(1)}, u32[]{:S(2)}, u32[]{:S(2)}) collective-permute-start(f32[3,10,1]{2,0,1:T(4,128)S(1)} %get-tuple-element.125), channel_id=1, source_target_pairs={{0,1},{2,3},{4,5},{6,7},{8,9},{10,11},{12,13},{14,15},{16,17},{18,... | collective-permute-start | bytes 368 | tf_op jit(solution)/shard_map/ppermute | solution.py:20
  87.3 3.1 %collective-permute-start.28 = (f32[3,10,1]{2,0,1:T(4,128)S(1)}, f32[3,10,1]{2,0,1:T(4,128)S(1)}, u32[]{:S(2)}, u32[]{:S(2)}) collective-permute-start(f32[3,10,1]{2,0,1:T(4,128)S(1)} %get-tuple-element.126), channel_id=1, source_target_pairs={{1,0},{3,2},{5,4},{7,6},{9,8},{11,10},{13,12},{15,14},{17,16},{19,... | collective-permute-start | bytes 368 | tf_op jit(solution)/shard_map/ppermute | solution.py:22
  88.6 7.4 %collective-permute-start.7 = (f32[6,1,16,256]{3,2,1,0:T(8,128)S(1)}, f32[6,1,16,256]{3,2,1,0:T(8,128)S(1)}, u32[]{:S(2)}, u32[]{:S(2)}) collective-permute-start(f32[6,1,16,256]{3,2,1,0:T(8,128)S(1)} %get-tuple-element.72), channel_id=1, source_target_pairs={{8,0},{16,8},{24,16},{9,1},{17,9},{25,17},{10,2},{18,10},{26,18},{... | collective-permute-start | bytes 294920 | tf_op jit(solution)/shard_map/ppermute | solution.py:22
  96.0 5.9 %collective-permute-start.8 = (f32[6,6,1,256]{3,2,1,0:T(1,128)S(1)}, f32[6,6,1,256]{3,2,1,0:T(1,128)S(1)}, u32[]{:S(2)}, u32[]{:S(2)}) collective-permute-start(f32[6,6,1,256]{3,2,1,0:T(1,128)S(1)} %get-tuple-element.59), channel_id=1, source_target_pairs={{0,2},{2,4},{4,6},{1,3},{3,5},{5,7},{8,10},{10,12},{12,14},{9,11},... | collective-permute-start | bytes 110600 | tf_op jit(solution)/shard_map/ppermute | solution.py:20
  98.0 6.8 %collective-permute-start.9 = (f32[6,6,1,256]{3,2,1,0:T(1,128)S(1)}, f32[6,6,1,256]{3,2,1,0:T(1,128)S(1)}, u32[]{:S(2)}, u32[]{:S(2)}) collective-permute-start(f32[6,6,1,256]{3,2,1,0:T(1,128)S(1)} %get-tuple-element.60), channel_id=1, source_target_pairs={{2,0},{4,2},{6,4},{3,1},{5,3},{7,5},{10,8},{12,10},{14,12},{11,9},... | collective-permute-start | bytes 110600 | tf_op jit(solution)/shard_map/ppermute | solution.py:22
  105.9 8.7 %collective-permute-start.10 = (f32[6,6,18,1]{3,2,1,0:T(8,128)}, f32[6,6,18,1]{3,2,1,0:T(8,128)}, u32[]{:S(2)}, u32[]{:S(2)}) collective-permute-start(f32[6,6,18,1]{3,2,1,0:T(8,128)} %get-tuple-element.48), channel_id=1, source_target_pairs={{0,1},{2,3},{4,5},{6,7},{8,9},{10,11},{12,13},{14,15},{16,17},{18,... | collective-permute-start | bytes 7784 | tf_op jit(solution)/shard_map/ppermute | solution.py:20
  108.0 6.6 %collective-permute-start.11 = (f32[6,6,18,1]{3,2,1,0:T(8,128)}, f32[6,6,18,1]{3,2,1,0:T(8,128)}, u32[]{:S(2)}, u32[]{:S(2)}) collective-permute-start(f32[6,6,18,1]{3,2,1,0:T(8,128)} %get-tuple-element.49), channel_id=1, source_target_pairs={{1,0},{3,2},{5,4},{7,6},{9,8},{11,10},{13,12},{15,14},{17,16},{19,... | collective-permute-start | bytes 7784 | tf_op jit(solution)/shard_map/ppermute | solution.py:22
  118.8 25.1 %copy-start.18 = (f32[1,1,16,256]{3,2,1,0:T(8,128)S(1)}, f32[1,1,16,256]{3,2,1,0:T(8,128)}, u32[]{:S(2)}) copy-start(f32[1,1,16,256]{3,2,1,0:T(8,128)} %copy-done.17) | copy-start | bytes 49156
  118.9 7.4 %collective-permute-start.29 = (f32[3,8,128]{2,1,0:T(8,128)S(1)}, f32[3,8,128]{2,1,0:T(8,128)S(1)}, u32[]{:S(2)}, u32[]{:S(2)}) collective-permute-start(f32[3,8,128]{2,1,0:T(8,128)S(1)} %multiply_bitcast_fusion.2), channel_id=1, source_target_pairs={{24,0},{25,1},{26,2},{27,3},{28,4},{29,5},{30,6},{31,7}} | collective-permute-start | bytes 36872 | tf_op jit(solution)/shard_map/ppermute | solution.py:32
  127.1 3.0 %collective-permute-start.30 = (f32[3,8,128]{2,1,0:T(8,128)S(1)}, f32[3,8,128]{2,1,0:T(8,128)S(1)}, u32[]{:S(2)}, u32[]{:S(2)}) collective-permute-start(f32[3,8,128]{2,1,0:T(8,128)S(1)} %multiply_multiply_fusion.1), channel_id=1, source_target_pairs={{0,24},{1,25},{2,26},{3,27},{4,28},{5,29},{6,30},{7,31}} | collective-permute-start | bytes 36872 | tf_op jit(solution)/shard_map/ppermute | solution.py:32
  130.1 5.8 %collective-permute-start.31 = (f32[3,1,128]{2,1,0:T(1,128)S(1)}, f32[3,1,128]{2,1,0:T(1,128)S(1)}, u32[]{:S(2)}, u32[]{:S(2)}) collective-permute-start(f32[3,1,128]{2,1,0:T(1,128)S(1)} %get-tuple-element.130), channel_id=1, source_target_pairs={{0,2},{2,4},{4,6},{1,3},{3,5},{5,7},{8,10},{10,12},{12,14},{9,11},... | collective-permute-start | bytes 4616 | tf_op jit(solution)/shard_map/ppermute | solution.py:20
  132.0 6.4 %collective-permute-start.32 = (f32[3,1,128]{2,1,0:T(1,128)S(1)}, f32[3,1,128]{2,1,0:T(1,128)S(1)}, u32[]{:S(2)}, u32[]{:S(2)}) collective-permute-start(f32[3,1,128]{2,1,0:T(1,128)S(1)} %get-tuple-element.129), channel_id=1, source_target_pairs={{2,0},{4,2},{6,4},{3,1},{5,3},{7,5},{10,8},{12,10},{14,12},{11,9},... | collective-permute-start | bytes 4616 | tf_op jit(solution)/shard_map/ppermute | solution.py:22
  138.5 2.6 %collective-permute-start.33 = (f32[3,10,1]{2,0,1:T(4,128)S(1)}, f32[3,10,1]{2,0,1:T(4,128)S(1)}, u32[]{:S(2)}, u32[]{:S(2)}) collective-permute-start(f32[3,10,1]{2,0,1:T(4,128)S(1)} %get-tuple-element.123), channel_id=1, source_target_pairs={{0,1},{2,3},{4,5},{6,7},{8,9},{10,11},{12,13},{14,15},{16,17},{18,... | collective-permute-start | bytes 368 | tf_op jit(solution)/shard_map/ppermute | solution.py:20
  139.8 3.1 %collective-permute-start.34 = (f32[3,10,1]{2,0,1:T(4,128)S(1)}, f32[3,10,1]{2,0,1:T(4,128)S(1)}, u32[]{:S(2)}, u32[]{:S(2)}) collective-permute-start(f32[3,10,1]{2,0,1:T(4,128)S(1)} %get-tuple-element.124), channel_id=1, source_target_pairs={{1,0},{3,2},{5,4},{7,6},{9,8},{11,10},{13,12},{15,14},{17,16},{19,... | collective-permute-start | bytes 368 | tf_op jit(solution)/shard_map/ppermute | solution.py:22
  144.0 25.2 %copy-start.9 = (f32[3,4,16,256]{3,2,1,0:T(8,128)}, f32[3,4,16,256]{3,2,1,0:T(8,128)S(1)}, u32[]{:S(2)}) copy-start(f32[3,4,16,256]{3,2,1,0:T(8,128)S(1)} %get-tuple-element.85) | copy-start | bytes 589828
  144.8 7.4 %collective-permute-start.35 = (f32[3,8,128]{2,1,0:T(8,128)S(1)}, f32[3,8,128]{2,1,0:T(8,128)S(1)}, u32[]{:S(2)}, u32[]{:S(2)}) collective-permute-start(f32[3,8,128]{2,1,0:T(8,128)S(1)} %multiply_bitcast_fusion.1), channel_id=1, source_target_pairs={{24,0},{25,1},{26,2},{27,3},{28,4},{29,5},{30,6},{31,7}} | collective-permute-start | bytes 36872 | tf_op jit(solution)/shard_map/ppermute | solution.py:32
  152.9 3.0 %collective-permute-start.36 = (f32[3,8,128]{2,1,0:T(8,128)S(1)}, f32[3,8,128]{2,1,0:T(8,128)S(1)}, u32[]{:S(2)}, u32[]{:S(2)}) collective-permute-start(f32[3,8,128]{2,1,0:T(8,128)S(1)} %multiply_multiply_fusion), channel_id=1, source_target_pairs={{0,24},{1,25},{2,26},{3,27},{4,28},{5,29},{6,30},{7,31}} | collective-permute-start | bytes 36872 | tf_op jit(solution)/shard_map/ppermute | solution.py:32
  155.9 5.8 %collective-permute-start.37 = (f32[3,1,128]{2,1,0:T(1,128)S(1)}, f32[3,1,128]{2,1,0:T(1,128)S(1)}, u32[]{:S(2)}, u32[]{:S(2)}) collective-permute-start(f32[3,1,128]{2,1,0:T(1,128)S(1)} %get-tuple-element.128), channel_id=1, source_target_pairs={{0,2},{2,4},{4,6},{1,3},{3,5},{5,7},{8,10},{10,12},{12,14},{9,11},... | collective-permute-start | bytes 4616 | tf_op jit(solution)/shard_map/ppermute | solution.py:20
  157.8 6.4 %collective-permute-start.38 = (f32[3,1,128]{2,1,0:T(1,128)S(1)}, f32[3,1,128]{2,1,0:T(1,128)S(1)}, u32[]{:S(2)}, u32[]{:S(2)}) collective-permute-start(f32[3,1,128]{2,1,0:T(1,128)S(1)} %get-tuple-element.127), channel_id=1, source_target_pairs={{2,0},{4,2},{6,4},{3,1},{5,3},{7,5},{10,8},{12,10},{14,12},{11,9},... | collective-permute-start | bytes 4616 | tf_op jit(solution)/shard_map/ppermute | solution.py:22
  164.3 2.6 %collective-permute-start.39 = (f32[3,10,1]{2,0,1:T(4,128)S(1)}, f32[3,10,1]{2,0,1:T(4,128)S(1)}, u32[]{:S(2)}, u32[]{:S(2)}) collective-permute-start(f32[3,10,1]{2,0,1:T(4,128)S(1)} %get-tuple-element.121), channel_id=1, source_target_pairs={{0,1},{2,3},{4,5},{6,7},{8,9},{10,11},{12,13},{14,15},{16,17},{18,... | collective-permute-start | bytes 368 | tf_op jit(solution)/shard_map/ppermute | solution.py:20
  165.6 3.1 %collective-permute-start.40 = (f32[3,10,1]{2,0,1:T(4,128)S(1)}, f32[3,10,1]{2,0,1:T(4,128)S(1)}, u32[]{:S(2)}, u32[]{:S(2)}) collective-permute-start(f32[3,10,1]{2,0,1:T(4,128)S(1)} %get-tuple-element.122), channel_id=1, source_target_pairs={{1,0},{3,2},{5,4},{7,6},{9,8},{11,10},{13,12},{15,14},{17,16},{19,... | collective-permute-start | bytes 368 | tf_op jit(solution)/shard_map/ppermute | solution.py:22
  173.4 7.4 %collective-permute-start.41 = (f32[3,8,128]{2,1,0:T(8,128)S(1)}, f32[3,8,128]{2,1,0:T(8,128)S(1)}, u32[]{:S(2)}, u32[]{:S(2)}) collective-permute-start(f32[3,8,128]{2,1,0:T(8,128)S(1)} %multiply_bitcast_fusion), channel_id=1, source_target_pairs={{24,0},{25,1},{26,2},{27,3},{28,4},{29,5},{30,6},{31,7}} | collective-permute-start | bytes 36872 | tf_op jit(solution)/shard_map/ppermute | solution.py:32
  (26 other events, 142.4 us)
where the time goes:
time: 185 us; the launch traced here: 181 us
  starting transfers between devices  93.5 us (51%)
  waiting for transfers between devices  53.5 us (29%)
  local copies, waits for them, and re-layouts  19.8 us (11%)
  other arithmetic  12.3 us (7%)
  between operations  2.31 us (1%)
    ppermute x18, starting transfers between devices, with_halo(): lax.ppermute(head, axis, [((i + 1) % count, i) for i in range(ends)])  39.9 us
    ppermute x18, starting transfers between devices, with_halo(): lax.ppermute(tail, axis, [(i, (i + 1) % count) for i in range(ends)])  39.9 us
    ppermute x18, waiting for transfers between devices, with_halo(): lax.ppermute(head, axis, [((i + 1) % count, i) for i in range(ends)])  31.9 us
    ppermute x6, waiting for transfers between devices, passed_along(): return lax.ppermute(shard, axis, pairs)  21.6 us
    ppermute x6, starting transfers between devices, passed_along(): return lax.ppermute(shard, axis, pairs)  13.8 us
    reshape x6, local copies, waits for them, and re-layouts, prolong_axis(): return jnp.stack([even_cells, odd_cells], axis + 1).reshape(new_shape)  5.17 us
    concatenate x9, other arithmetic, with_halo(): jnp.concatenate([lax.ppermute(tail, axis, [(i, (i + 1) % count) for i in...  4.03 us
    unnamed x93, local copies, waits for them, and re-layouts  3.77 us
  transfers between devices with their start and end apart: 42, of which 19 were waited for; matrix products, arithmetic and copies ran while one was open for 7% of the time, Pallas kernels for 0%

commit v1 on v0

v1 whole, which is shorter than its diff:
```python
import numpy as np
import jax
import jax.numpy as jnp
from jax import lax
from jax.sharding import PartitionSpec as P

ITERS = 3
TIME_STEP = 0.2
HALO = 2


def pair_tables(count):
    even = [(i, i + 1) for i in range(0, count - 1, 2)]
    odd = [(i, i + 1) for i in range(1, count - 1, 2)]
    both = lambda some: some + [(b, a) for a, b in some]
    return both(even), both(odd)


def swap_both(to_prev, to_next, axis):
    count = lax.axis_size(axis)
    is_even = lax.axis_index(axis) % 2 == 0
    first, second = pair_tables(count)
    got_first = lax.ppermute(jnp.where(is_even, to_next, to_prev), axis, first)
    zero = jnp.zeros_like(got_first)
    if second:
        got_second = lax.ppermute(jnp.where(is_even, to_prev, to_next), axis, second)
    else:
        got_second = zero
    return (
        jnp.where(is_even, got_second, got_first),
        jnp.where(is_even, got_first, got_second),
    )


def flat(parts):
    return jnp.concatenate([part.reshape(-1) for part in parts])


def split(buffer, shapes):
    out = []
    at = 0
    for shape in shapes:
        size = int(np.prod(shape))
        out.append(buffer[at : at + size].reshape(shape))
        at += size
    return out


def edge(cells, dim, low, width=1):
    if low:
        return lax.slice_in_dim(cells, 0, width, axis=dim)
    return lax.slice_in_dim(cells, cells.shape[dim] - width, cells.shape[dim], axis=dim)


def faces(blocks, axis, dim):
    low = [edge(b, dim, True) for b in blocks]
    high = [edge(b, dim, False) for b in blocks]
    shapes = [f.shape for f in low]
    from_prev, from_next = swap_both(flat(low), flat(high), axis)
    return list(zip(split(from_prev, shapes), split(from_next, shapes)))


def diff(cells, around, dim, inverse_step):
    wide = jnp.concatenate([around[0], cells, around[1]], axis=dim)
    length = cells.shape[dim]
    return (
        lax.slice_in_dim(wide, 2, length + 2, axis=dim) - lax.slice_in_dim(wide, 0, length, axis=dim)
    ) * inverse_step


def stresses(disp, halos, stiffness, stretch, inverse_step):
    dx = diff(disp, halos[2], 3, inverse_step)
    dy = diff(disp, halos[1], 2, inverse_step)
    dz = diff(disp, halos[0], 1, inverse_step) * stretch
    c = stiffness
    xx = c[0] * dx[0] + c[6] * dy[1] + c[7] * dz[2]
    yy = c[6] * dx[0] + c[1] * dy[1] + c[8] * dz[2]
    zz = c[7] * dx[0] + c[8] * dy[1] + c[2] * dz[2]
    yz = c[3] * (dz[1] + dy[2])
    xz = c[4] * (dz[0] + dx[2])
    xy = c[5] * (dy[0] + dx[1])
    return (jnp.stack([xx, xy, xz]), jnp.stack([xy, yy, yz]), jnp.stack([xz, yz, zz]))


def transfer_matrices(rows, halo):
    coarse = rows + 2 * halo
    fine = 2 * rows + 4 * (halo - 1)
    up = np.zeros((fine, coarse), np.float32)
    for f in range(fine):
        c = f - 2 * (halo - 1)
        up[f, c // 2 + halo] += 0.75
        up[f, c // 2 - 1 + 2 * (c % 2) + halo] += 0.25
    return up


def prolong(plane, rows, cols, halo):
    left = transfer_matrices(rows, halo)
    right = transfer_matrices(cols, halo)
    half = jnp.einsum("fy,cyx->cfx", left, plane, precision=lax.Precision.HIGHEST)
    return jnp.einsum("cfx,gx->cfg", half, right, precision=lax.Precision.HIGHEST)


def restrict(plane):
    rows, cols = plane.shape[1] // 2, plane.shape[2] // 2
    left = np.kron(np.eye(rows, dtype=np.float32), np.full((1, 2), 0.5, np.float32))
    right = np.kron(np.eye(cols, dtype=np.float32), np.full((1, 2), 0.5, np.float32))
    half = jnp.einsum("fy,cyx->cfx", left, plane, precision=lax.Precision.HIGHEST)
    return jnp.einsum("cfx,gx->cfg", half, right, precision=lax.Precision.HIGHEST)


def clamp(plane, halo):
    for axis, dim in (("gy", 1), ("gx", 2)):
        spot = lax.axis_index(axis)
        size = plane.shape[dim]
        where = lax.broadcasted_iota(jnp.int32, plane.shape, dim)
        first = lax.slice_in_dim(plane, halo, halo + 1, axis=dim)
        last = lax.slice_in_dim(plane, size - halo - 1, size - halo, axis=dim)
        plane = jnp.where((spot == 0) & (where < halo), first, plane)
        plane = jnp.where(
            (spot == lax.axis_size(axis) - 1) & (where >= size - halo), last, plane
        )
    return plane


def trim(plane, width):
    return plane[:, width : plane.shape[1] - width, width : plane.shape[2] - width]


def widen(coarse, fine):
    for axis, dim in (("gx", 2), ("gy", 1)):
        low = [edge(p, dim, True, HALO) for p in (coarse, fine)]
        high = [edge(p, dim, False, HALO) for p in (coarse, fine)]
        shapes = [f.shape for f in low]
        prev, after = swap_both(flat(low), flat(high), axis)
        prev, after = split(prev, shapes), split(after, shapes)
        coarse = jnp.concatenate([prev[0], coarse, after[0]], axis=dim)
        fine = jnp.concatenate([prev[1], fine, after[1]], axis=dim)
    return coarse, fine


def per_device(
    fine_now,
    fine_prev,
    stiffness,
    metric,
    density,
    coarse_now,
    coarse_prev,
    coarse_stiffness,
    coarse_density,
):
    plane_z = lax.axis_index("gz")
    count_z = lax.axis_size("gz")
    layers = fine_now.shape[1]
    layer_index = plane_z * layers + jnp.arange(layers)
    stretch = jnp.where((layer_index < count_z * layers // 2)[:, None, None], metric, 1.0)

    axes = (("gz", 1), ("gy", 2), ("gx", 3))
    around = [faces([fine_now, coarse_now], axis, dim) for axis, dim in axes]
    sf = stresses(fine_now, [a[0] for a in around], stiffness, stretch, 0.5)
    sc = stresses(coarse_now, [a[1] for a in around], coarse_stiffness, 1.0, 0.25)
    by_axis = (2, 1, 0)
    around = [
        faces([sf[k], sc[k]], axis, dim) for k, (axis, dim) in zip(by_axis, axes)
    ]

    def advance(now, prev, density, stress, halos, stretch, inverse_step):
        internal = (
            diff(stress[0], halos[2], 3, inverse_step)
            + diff(stress[1], halos[1], 2, inverse_step)
            + diff(stress[2], halos[0], 1, inverse_step) * stretch
        )
        return 2.0 * now - prev + TIME_STEP * TIME_STEP * internal / density

    fine_step = advance(fine_now, fine_prev, density, sf, [a[0] for a in around], stretch, 0.5)
    coarse_step = advance(
        coarse_now, coarse_prev, coarse_density, sc, [a[1] for a in around], 1.0, 0.25
    )

    rows, cols = coarse_now.shape[2], coarse_now.shape[3]
    is_top = plane_z == count_z - 1
    above = fine_step[:, -2]
    kf = jnp.stack([stiffness[4, -1], stiffness[3, -1], stiffness[2, -1]])
    start_r = restrict(fine_step[:, -1])
    kc = jnp.stack([coarse_stiffness[4, 0], coarse_stiffness[3, 0], coarse_stiffness[2, 0]])
    coarse = jnp.concatenate([coarse_step[:, 0], coarse_step[:, 1], kc], 0)
    from_top = flat([above, kf, start_r])
    from_low = flat([coarse])
    from_low = jnp.concatenate(
        [from_low, jnp.zeros((from_top.shape[0] - from_low.shape[0],), jnp.float32)]
    )
    got = lax.ppermute(
        jnp.where(is_top, from_top, from_low), "gz", [(0, count_z - 1), (count_z - 1, 0)]
    )
    top = jnp.where(is_top, from_top, got)
    low = jnp.where(is_top, got, from_low)
    above, kf, start_r = split(top, [above.shape, kf.shape, start_r.shape])
    coarse = split(low, [coarse.shape])[0]
    coarse, fine = widen(jnp.concatenate([coarse, start_r]), jnp.concatenate([above, kf]))
    start, below, kc, start_r = (coarse[3 * i : 3 * i + 3] for i in range(4))
    above, kf = fine[:3], fine[3:]
    kf = jnp.where(kf > 0, kf, 1.0)

    traction = clamp(kc * (below - start) * 0.25, HALO)
    fine_1 = above + prolong(traction, rows, cols, HALO) / kf
    coarse_2 = 0.5 * (trim(start, 1) + restrict(fine_1))
    traction = clamp(trim(kc, 1) * (trim(below, 1) - coarse_2) * 0.25, 1)
    fine_3 = trim(above, HALO) + prolong(traction, rows, cols, 1) / trim(kf, HALO)
    coarse_1 = 0.5 * (trim(start, 1) + trim(start_r, 1))
    traction = clamp(trim(kc, 1) * (trim(below, 1) - coarse_1) * 0.25, 1)
    fine_2 = trim(above, HALO) + prolong(traction, rows, cols, 1) / trim(kf, HALO)
    coarse_3 = 0.5 * (trim(start, HALO) + restrict(fine_2))

    fine_next = fine_step.at[:, -1].set(jnp.where(is_top, fine_3, fine_step[:, -1]))
    coarse_next = coarse_step.at[:, 0].set(
        jnp.where(plane_z == 0, coarse_3, coarse_step[:, 0])
    )
    return (fine_next, coarse_next)


def solution(mesh):
    block = P(None, "gz", "gy", "gx")
    field = P("gz", "gy", "gx")
    return jax.shard_map(
        per_device,
        mesh=mesh,
        in_specs=(block, block, block, field, field, block, block, block, field),
        out_specs=(block, block),
        check_vma=False,
    )
```

time: 185 us -> 59.5 us (0.32)
  the two profiles are of different devices: /device:TPU:2 before, /device:TPU:0 now
where the time goes in v1:
time: 59.5 us; the launch traced here: 59.1 us
  starting transfers between devices  25.2 us (42%)
  local copies, waits for them, and re-layouts  15.5 us (26%)
  waiting for transfers between devices  9.3 us (16%)
  matrix products  4.58 us (8%)
  other arithmetic  2.55 us (4%)
  between operations  1.95 us (3%)
    ppermute x8, starting transfers between devices, swap_both(): got_first = lax.ppermute(jnp.where(is_even, to_next, to_prev), axis, first)  19.1 us
    unnamed x55, local copies, waits for them, and re-layouts  7.04 us
    ppermute x1, waiting for transfers between devices, per_device(): lax.ppermute(jnp.where(is_top, from_top, from_low), 'gz', [(0, count_z -...  5.6 us
    ppermute x8, waiting for transfers between devices, swap_both(): got_first = lax.ppermute(jnp.where(is_even, to_next, to_prev), axis, first)  3.69 us
    slice x54, local copies, waits for them, and re-layouts, split(): out.append(buffer[at:at + size].reshape(shape))  3.44 us
    ppermute x5, starting transfers between devices, swap_both(): lax.ppermute(jnp.where(is_even, to_prev, to_next), axis, second)  3.26 us
    ppermute x1, starting transfers between devices, per_device(): lax.ppermute(jnp.where(is_top, from_top, from_low), 'gz', [(0, count_z -...  2.82 us
    reshape x17, local copies, waits for them, and re-layouts, flat(): return jnp.concatenate([part.reshape(-1) for part in parts])  1.72 us
  transfers between devices with their start and end apart: 14, of which 5 were waited for; matrix products, arithmetic and copies ran while one was open for 6% of the time, Pallas kernels for 0%

profile of v1, /device:TPU:0, one launch (start us, length us, event | category | flops | bytes accessed | tf_op | source)
XLA Modules:
  0.0 59.1 jit_solution(14877858664358762992)
XLA Ops:
  0.6 0.8 %fusion.102 = (f32[3,1,16,256]{3,2,1,0:T(8,128)S(1)}, f32[3,1,16,256]{3,2,1,0:T(8,128)S(1)}) fusion(f32[3,4,16,256]{3,2,1,0:T(8,128)} %param.25), kind=kLoop, calls=%fused_computation.307 | loop fusion | bytes 196608 | tf_op jit(solution)/shard_map/slice | solution.py:52
  1.6 0.8 %copy-done.1 = f32[3,8,8,128]{3,2,1,0:T(8,128)S(1)} copy-done((f32[3,8,8,128]{3,2,1,0:T(8,128)S(1)}, f32[3,8,8,128]{3,2,1,0:T(8,128)}, u32[]{:S(2)}) %copy-start.1) | copy-done | bytes 98328
  2.4 3.1 %collective-permute-start.3 = (f32[15360]{0:T(1024)S(1)}, f32[15360]{0:T(1024)S(1)}, u32[]{:S(2)}, u32[]{:S(2)}) collective-permute-start(f32[15360]{0:T(1024)S(1)} %get-tuple-element.80), channel_id=1, source_target_pairs={{0,8},{16,24},{8,0},{24,16},{1,9},{17,25},{9,1},{25,17},{2,10},{18... | collective-permute-start | bytes 184328 | tf_op jit(solution)/shard_map/ppermute | solution.py:23
  5.5 0.7 %collective-permute-start.4 = (f32[15360]{0:T(1024)S(1)}, f32[15360]{0:T(1024)S(1)}, u32[]{:S(2)}, u32[]{:S(2)}) collective-permute-start(f32[15360]{0:T(1024)S(1)} %get-tuple-element.81), channel_id=1, source_target_pairs={{8,16},{16,8},{9,17},{17,9},{10,18},{18,10},{11,19},{19,11},{12,20... | collective-permute-start | bytes 184328 | tf_op jit(solution)/shard_map/ppermute | solution.py:26
  6.3 1.6 %collective-permute-start.1 = (f32[6144]{0:T(1024)S(1)}, f32[6144]{0:T(1024)S(1)}, u32[]{:S(2)}, u32[]{:S(2)}) collective-permute-start(f32[6144]{0:T(1024)S(1)} %get-tuple-element.119), channel_id=1, source_target_pairs={{0,2},{4,6},{2,0},{6,4},{1,3},{5,7},{3,1},{7,5},{8,10},{12,14},{10... | collective-permute-start | bytes 73736 | tf_op jit(solution)/shard_map/ppermute | solution.py:23
  7.8 0.7 %collective-permute-start.2 = (f32[6144]{0:T(1024)S(1)}, f32[6144]{0:T(1024)S(1)}, u32[]{:S(2)}, u32[]{:S(2)}) collective-permute-start(f32[6144]{0:T(1024)S(1)} %get-tuple-element.120), channel_id=1, source_target_pairs={{2,4},{4,2},{3,5},{5,3},{10,12},{12,10},{11,13},{13,11},{18,20},{2... | collective-permute-start | bytes 73736 | tf_op jit(solution)/shard_map/ppermute | solution.py:26
  8.5 0.2 slice_reduce_fusion
  8.7 0.2 slice_reduce_fusion.1
  9.5 0.5 copy-done.11
  10.1 0.4 collective-permute-done
  11.1 0.2 copy.79
  11.4 0.2 copy.80
  11.9 0.2 fusion.25
  12.4 0.8 %copy-done.5 = f32[9,8,8,128]{3,2,1,0:T(8,128)S(1)} copy-done((f32[9,8,8,128]{3,2,1,0:T(8,128)S(1)}, f32[9,8,8,128]{3,2,1,0:T(8,128)}, u32[]{:S(2)}) %copy-start.5) | copy-done | bytes 294936
  14.0 0.2 copy.92
  14.3 0.2 copy.94
  14.7 0.2 collective-permute-start.5
  15.0 4.3 %collective-permute-start.6 = (f32[6144]{0:T(1024)S(1)}, f32[6144]{0:T(1024)S(1)}, u32[]{:S(2)}, u32[]{:S(2)}) collective-permute-start(f32[6144]{0:T(1024)S(1)} %get-tuple-element.115), channel_id=1, source_target_pairs={{0,2},{4,6},{2,0},{6,4},{1,3},{5,7},{3,1},{7,5},{8,10},{12,14},{10... | collective-permute-start | bytes 73736 | tf_op jit(solution)/shard_map/ppermute | solution.py:23
  19.3 0.7 %collective-permute-start.7 = (f32[6144]{0:T(1024)S(1)}, f32[6144]{0:T(1024)S(1)}, u32[]{:S(2)}, u32[]{:S(2)}) collective-permute-start(f32[6144]{0:T(1024)S(1)} %get-tuple-element.116), channel_id=1, source_target_pairs={{2,4},{4,2},{3,5},{5,3},{10,12},{12,10},{11,13},{13,11},{18,20},{2... | collective-permute-start | bytes 73736 | tf_op jit(solution)/shard_map/ppermute | solution.py:26
  20.1 4.5 %collective-permute-start.8 = (f32[15360]{0:T(1024)S(1)}, f32[15360]{0:T(1024)S(1)}, u32[]{:S(2)}, u32[]{:S(2)}) collective-permute-start(f32[15360]{0:T(1024)S(1)} %get-tuple-element.76), channel_id=1, source_target_pairs={{0,8},{16,24},{8,0},{24,16},{1,9},{17,25},{9,1},{25,17},{2,10},{18... | collective-permute-start | bytes 184328 | tf_op jit(solution)/shard_map/ppermute | solution.py:23
  24.5 0.7 %collective-permute-start.9 = (f32[15360]{0:T(1024)S(1)}, f32[15360]{0:T(1024)S(1)}, u32[]{:S(2)}, u32[]{:S(2)}) collective-permute-start(f32[15360]{0:T(1024)S(1)} %get-tuple-element.77), channel_id=1, source_target_pairs={{8,16},{16,8},{9,17},{17,9},{10,18},{18,10},{11,19},{19,11},{12,20... | collective-permute-start | bytes 184328 | tf_op jit(solution)/shard_map/ppermute | solution.py:26
  25.4 0.2 copy.113
  25.7 0.2 copy.114
  26.8 0.8 %copy-done.9 = f32[3,8,8,128]{3,2,1,0:T(8,128)S(1)} copy-done((f32[3,8,8,128]{3,2,1,0:T(8,128)S(1)}, f32[3,8,8,128]{3,2,1,0:T(8,128)}, u32[]{:S(2)}) %copy-start.9) | copy-done | bytes 98328
  28.0 0.8 %copy-done.8 = f32[3,4,16,256]{3,2,1,0:T(8,128)S(1)} copy-done((f32[3,4,16,256]{3,2,1,0:T(8,128)S(1)}, f32[3,4,16,256]{3,2,1,0:T(8,128)}, u32[]{:S(2)}) %copy-start.8) | copy-done | bytes 196632
  28.8 0.2 fusion.15
  29.1 0.6 %copy-done.13 = f32[8,16,1]{1,0,2:T(8,128)S(1)} copy-done((f32[8,16,1]{1,0,2:T(8,128)S(1)}, f32[8,16,1]{1,0,2:T(8,128)}, u32[]{:S(2)}) %copy-start.13) | copy-done | bytes 536
  29.9 0.2 convolution_bitcast_fusion.6
  30.2 2.8 %collective-permute-start.10 = (f32[27648]{0:T(1024)S(1)}, f32[27648]{0:T(1024)S(1)}, u32[]{:S(2)}, u32[]{:S(2)}) collective-permute-start(f32[27648]{0:T(1024)S(1)} %pad_select_fusion.1), channel_id=1, source_target_pairs={{0,24},{24,0},{1,25},{25,1},{2,26},{26,2},{3,27},{27,3},{4,28},{28... | collective-permute-start | bytes 331784 | tf_op jit(solution)/shard_map/ppermute | solution.py:192
  33.0 5.6 %collective-permute-done.10 = f32[27648]{0:T(1024)S(1)} collective-permute-done((f32[27648]{0:T(1024)S(1)}, f32[27648]{0:T(1024)S(1)}, u32[]{:S(2)}, u32[]{:S(2)}) %collective-permute-start.10) | collective-permute-done | bytes 110624 | tf_op jit(solution)/shard_map/ppermute | solution.py:192
  39.6 1.1 %collective-permute-done.11 = f32[384]{0:T(512)S(1)} collective-permute-done((f32[384]{0:T(512)S(1)}, f32[384]{0:T(512)S(1)}, u32[]{:S(2)}, u32[]{:S(2)}) %collective-permute-start.11) | collective-permute-done | bytes 1568 | tf_op jit(solution)/shard_map/ppermute | solution.py:23
  42.3 0.7 %collective-permute-start.12 = (f32[6288]{0:T(1024)S(1)}, f32[6288]{0:T(1024)S(1)}, u32[]{:S(2)}, u32[]{:S(2)}) collective-permute-start(f32[6288]{0:T(1024)S(1)} %get-tuple-element.101), channel_id=1, source_target_pairs={{2,4},{4,2},{3,5},{5,3},{10,12},{12,10},{11,13},{13,11},{18,20},{2... | collective-permute-start | bytes 75464 | tf_op jit(solution)/shard_map/ppermute | solution.py:26
  42.9 5.5 %collective-permute-start.13 = (f32[6288]{0:T(1024)S(1)}, f32[6288]{0:T(1024)S(1)}, u32[]{:S(2)}, u32[]{:S(2)}) collective-permute-start(f32[6288]{0:T(1024)S(1)} %get-tuple-element.102), channel_id=1, source_target_pairs={{0,2},{4,6},{2,0},{6,4},{1,3},{5,7},{3,1},{7,5},{8,10},{12,14},{10... | collective-permute-start | bytes 75464 | tf_op jit(solution)/shard_map/ppermute | solution.py:23
  48.4 2.1 %collective-permute-done.13 = f32[6288]{0:T(1024)S(1)} collective-permute-done((f32[6288]{0:T(1024)S(1)}, f32[6288]{0:T(1024)S(1)}, u32[]{:S(2)}, u32[]{:S(2)}) %collective-permute-start.13) | collective-permute-done | bytes 25184 | tf_op jit(solution)/shard_map/ppermute | solution.py:23
  51.6 0.2 slice_reduce_fusion.9
  51.9 0.5 copy-done.14
  52.5 0.7 %convolution_bitcast_fusion.1 = f32[3,20,132]{1,2,0:T(8,128)S(1)} fusion(f32[20,12,1]{1,0,2:T(8,128)S(1)} %copy-done.14, f32[3,12,132]{2,1,0:T(8,128)S(1)} %select_select_fusion.2, f32[3,12]{1,0:T(4,128)S(1)} %get-tuple-element.39, f32[3,12]{1,0:T(4,128)S(1)} %get-tuple-element.38, pred[132]{0:T(512)(128)(4,1)S(1)} %compare_and_fusion.2, ...), kind=kOutput, calls=%fused_computation.1 | convolution fusion | flops 1149984 | bytes 52200 | tf_op jit(solution)/shard_map/fy,cyx->cfx/dot_general | solution.py:99
  53.1 0.9 %fusion = f32[3,20,260]{2,1,0:T(8,128)S(1)} fusion(f32[3,20,132]{1,2,0:T(8,128)S(1)} %convolution_bitcast_fusion.1, f32[260,132,1]{1,0,2:T(8,128)S(1)} %copy-done.6, f32[6,20,260]{2,1,0:T(8,128)S(1)} %pad_maximum_fusion), kind=kOutput, calls=%fused_computation.3 | convolution fusion | flops 24772800 | bytes 356160 | tf_op jit(solution)/shard_map/cfx,gx->cfg/dot_general | solution.py:100
  54.1 0.2 convolution_bitcast_fusion.2
  54.3 0.4 fusion.8
  55.1 0.4 copy-done.15
  55.5 0.7 %convolution_bitcast_fusion = f32[3,16,130]{1,2,0:T(8,128)S(1)} fusion(f32[16,10,1]{1,0,2:T(8,128)S(1)} %copy-done.15, f32[3,10,130]{2,1,0:T(8,128)S(1)} %get-tuple-element.147, f32[3,10]{1,0:T(4,128)S(1)} %get-tuple-element.35, f32[3,10]{1,0:T(4,128)S(1)} %get-tuple-element.34, pred[130]{0:T(512)(128)(4,1)S(1)} %compare_and_fusion, ...), kind=kOutput, calls=%fused_computation | convolution fusion | flops 756600 | bytes 41700 | tf_op jit(solution)/shard_map/fy,cyx->cfx/dot_general | solution.py:99
  56.1 0.5 fusion.9
  56.8 0.2 fusion.97
  57.1 0.6 %copy.118 = f32[3,8,8,128]{3,2,1,0:T(8,128)} copy(f32[3,8,8,128]{3,2,0,1:T(8,128)S(1)} %fusion.97) | data formatting | bytes 196608
  57.9 0.3 convolution_bitcast_fusion.3
  58.2 0.2 fusion.4
  58.4 0.7 %copy.117 = f32[3,4,16,256]{3,2,1,0:T(8,128)} copy(f32[3,4,16,256]{3,2,0,1:T(8,128)S(1)} %fusion.4) | data formatting | bytes 393216
  (208 shorter events, 8.8 us)
Async XLA Ops:
  1.5 0.9 %copy-start.1 = (f32[3,8,8,128]{3,2,1,0:T(8,128)S(1)}, f32[3,8,8,128]{3,2,1,0:T(8,128)}, u32[]{:S(2)}) copy-start(f32[3,8,8,128]{3,2,1,0:T(8,128)} %param.30) | copy-start | bytes 294916
  1.5 4.7 %copy-start = (f32[3,4,16,256]{3,2,1,0:T(8,128)S(1)}, f32[3,4,16,256]{3,2,1,0:T(8,128)}, u32[]{:S(2)}) copy-start(f32[3,4,16,256]{3,2,1,0:T(8,128)} %param.25) | copy-start | bytes 589828
  1.5 7.9 %copy-start.2 = (f32[9,4,16,256]{3,2,1,0:T(8,128)S(1)}, f32[9,4,16,256]{3,2,1,0:T(8,128)}, u32[]{:S(2)}) copy-start(f32[9,4,16,256]{3,2,1,0:T(8,128)} %param.27) | copy-start | bytes 1769476
  2.4 9.4 %collective-permute-start.3 = (f32[15360]{0:T(1024)S(1)}, f32[15360]{0:T(1024)S(1)}, u32[]{:S(2)}, u32[]{:S(2)}) collective-permute-start(f32[15360]{0:T(1024)S(1)} %get-tuple-element.80), channel_id=1, source_target_pairs={{0,8},{16,24},{8,0},{24,16},{1,9},{17,25},{9,1},{25,17},{2,10},{18... | collective-permute-start | bytes 184328 | tf_op jit(solution)/shard_map/ppermute | solution.py:23
  5.5 6.3 %collective-permute-start.4 = (f32[15360]{0:T(1024)S(1)}, f32[15360]{0:T(1024)S(1)}, u32[]{:S(2)}, u32[]{:S(2)}) collective-permute-start(f32[15360]{0:T(1024)S(1)} %get-tuple-element.81), channel_id=1, source_target_pairs={{8,16},{16,8},{9,17},{17,9},{10,18},{18,10},{11,19},{19,11},{12,20... | collective-permute-start | bytes 184328 | tf_op jit(solution)/shard_map/ppermute | solution.py:26
  6.3 5.4 %collective-permute-start.1 = (f32[6144]{0:T(1024)S(1)}, f32[6144]{0:T(1024)S(1)}, u32[]{:S(2)}, u32[]{:S(2)}) collective-permute-start(f32[6144]{0:T(1024)S(1)} %get-tuple-element.119), channel_id=1, source_target_pairs={{0,2},{4,6},{2,0},{6,4},{1,3},{5,7},{3,1},{7,5},{8,10},{12,14},{10... | collective-permute-start | bytes 73736 | tf_op jit(solution)/shard_map/ppermute | solution.py:23
  7.8 3.8 %collective-permute-start.2 = (f32[6144]{0:T(1024)S(1)}, f32[6144]{0:T(1024)S(1)}, u32[]{:S(2)}, u32[]{:S(2)}) collective-permute-start(f32[6144]{0:T(1024)S(1)} %get-tuple-element.120), channel_id=1, source_target_pairs={{2,4},{4,2},{3,5},{5,3},{10,12},{12,10},{11,13},{13,11},{18,20},{2... | collective-permute-start | bytes 73736 | tf_op jit(solution)/shard_map/ppermute | solution.py:26
  9.1 0.8 %copy-start.11 = (f32[4,16,256]{2,1,0:T(8,128)S(1)}, f32[4,16,256]{2,1,0:T(8,128)}, u32[]{:S(2)}) copy-start(f32[4,16,256]{2,1,0:T(8,128)} %param.28) | copy-start | bytes 196612
  9.3 1.2 %collective-permute-start = (f32[384]{0:T(512)S(1)}, f32[384]{0:T(512)S(1)}, u32[]{:S(2)}, u32[]{:S(2)}) collective-permute-start(f32[384]{0:T(512)S(1)} %maximum_select_fusion), channel_id=1, source_target_pairs={{0,1},{1,0},{2,3},{3,2},{4,5},{5,4},{6,7},{7,6},{8,9},{9,8},{10,11... | collective-permute-start | bytes 4616 | tf_op jit(solution)/shard_map/ppermute | solution.py:23
  12.3 1.0 %copy-start.5 = (f32[9,8,8,128]{3,2,1,0:T(8,128)S(1)}, f32[9,8,8,128]{3,2,1,0:T(8,128)}, u32[]{:S(2)}) copy-start(f32[9,8,8,128]{3,2,1,0:T(8,128)} %param.32) | copy-start | bytes 884740
  14.7 10.5 %collective-permute-start.5 = (f32[384]{0:T(512)S(1)}, f32[384]{0:T(512)S(1)}, u32[]{:S(2)}, u32[]{:S(2)}) collective-permute-start(f32[384]{0:T(512)S(1)} %maximum_select_fusion.1), channel_id=1, source_target_pairs={{0,1},{1,0},{2,3},{3,2},{4,5},{5,4},{6,7},{7,6},{8,9},{9,8},{10,11... | collective-permute-start | bytes 4616 | tf_op jit(solution)/shard_map/ppermute | solution.py:23
  15.0 11.5 %collective-permute-start.6 = (f32[6144]{0:T(1024)S(1)}, f32[6144]{0:T(1024)S(1)}, u32[]{:S(2)}, u32[]{:S(2)}) collective-permute-start(f32[6144]{0:T(1024)S(1)} %get-tuple-element.115), channel_id=1, source_target_pairs={{0,2},{4,6},{2,0},{6,4},{1,3},{5,7},{3,1},{7,5},{8,10},{12,14},{10... | collective-permute-start | bytes 73736 | tf_op jit(solution)/shard_map/ppermute | solution.py:23
  19.3 7.2 %collective-permute-start.7 = (f32[6144]{0:T(1024)S(1)}, f32[6144]{0:T(1024)S(1)}, u32[]{:S(2)}, u32[]{:S(2)}) collective-permute-start(f32[6144]{0:T(1024)S(1)} %get-tuple-element.116), channel_id=1, source_target_pairs={{2,4},{4,2},{3,5},{5,3},{10,12},{12,10},{11,13},{13,11},{18,20},{2... | collective-permute-start | bytes 73736 | tf_op jit(solution)/shard_map/ppermute | solution.py:26
  20.1 6.7 %collective-permute-start.8 = (f32[15360]{0:T(1024)S(1)}, f32[15360]{0:T(1024)S(1)}, u32[]{:S(2)}, u32[]{:S(2)}) collective-permute-start(f32[15360]{0:T(1024)S(1)} %get-tuple-element.76), channel_id=1, source_target_pairs={{0,8},{16,24},{8,0},{24,16},{1,9},{17,25},{9,1},{25,17},{2,10},{18... | collective-permute-start | bytes 184328 | tf_op jit(solution)/shard_map/ppermute | solution.py:23
  24.5 2.2 %collective-permute-start.9 = (f32[15360]{0:T(1024)S(1)}, f32[15360]{0:T(1024)S(1)}, u32[]{:S(2)}, u32[]{:S(2)}) collective-permute-start(f32[15360]{0:T(1024)S(1)} %get-tuple-element.77), channel_id=1, source_target_pairs={{8,16},{16,8},{9,17},{17,9},{10,18},{18,10},{11,19},{19,11},{12,20... | collective-permute-start | bytes 184328 | tf_op jit(solution)/shard_map/ppermute | solution.py:26
  26.8 0.9 %copy-start.9 = (f32[3,8,8,128]{3,2,1,0:T(8,128)S(1)}, f32[3,8,8,128]{3,2,1,0:T(8,128)}, u32[]{:S(2)}) copy-start(f32[3,8,8,128]{3,2,1,0:T(8,128)} %param.31) | copy-start | bytes 294916
  26.8 0.9 %copy-start.12 = (f32[8,8,128]{2,1,0:T(8,128)S(1)}, f32[8,8,128]{2,1,0:T(8,128)}, u32[]{:S(2)}) copy-start(f32[8,8,128]{2,1,0:T(8,128)} %param.33) | copy-start | bytes 98308
  27.8 0.9 %copy-start.8 = (f32[3,4,16,256]{3,2,1,0:T(8,128)S(1)}, f32[3,4,16,256]{3,2,1,0:T(8,128)}, u32[]{:S(2)}) copy-start(f32[3,4,16,256]{3,2,1,0:T(8,128)} %param.26) | copy-start | bytes 589828
  27.9 0.9 %copy-start.10 = (f32[4,16,256]{2,1,0:T(8,128)S(1)}, f32[4,16,256]{2,1,0:T(8,128)}, u32[]{:S(2)}) copy-start(f32[4,16,256]{2,1,0:T(8,128)} %param.29) | copy-start | bytes 196612
  29.0 0.7 %copy-start.13 = (f32[8,16,1]{1,0,2:T(8,128)S(1)}, f32[8,16,1]{1,0,2:T(8,128)}, u32[]{:S(2)}) copy-start(f32[8,16,1]{1,0,2:T(8,128)} %constant.161) | copy-start | bytes 1540
  29.0 0.9 %copy-start.4 = (f32[128,256,1]{1,0,2:T(8,128)S(1)}, f32[128,256,1]{1,0,2:T(8,128)}, u32[]{:S(2)}) copy-start(f32[128,256,1]{1,0,2:T(8,128)} %constant.162) | copy-start | bytes 393220
  30.2 8.4 %collective-permute-start.10 = (f32[27648]{0:T(1024)S(1)}, f32[27648]{0:T(1024)S(1)}, u32[]{:S(2)}, u32[]{:S(2)}) collective-permute-start(f32[27648]{0:T(1024)S(1)} %pad_select_fusion.1), channel_id=1, source_target_pairs={{0,24},{24,0},{1,25},{25,1},{2,26},{26,2},{3,27},{27,3},{4,28},{28... | collective-permute-start | bytes 331784 | tf_op jit(solution)/shard_map/ppermute | solution.py:192
  39.6 1.2 %collective-permute-start.11 = (f32[384]{0:T(512)S(1)}, f32[384]{0:T(512)S(1)}, u32[]{:S(2)}, u32[]{:S(2)}) collective-permute-start(f32[384]{0:T(512)S(1)} %maximum_select_fusion.2), channel_id=1, source_target_pairs={{0,1},{1,0},{2,3},{3,2},{4,5},{5,4},{6,7},{7,6},{8,9},{9,8},{10,11... | collective-permute-start | bytes 4616 | tf_op jit(solution)/shard_map/ppermute | solution.py:23
  42.3 6.2 %collective-permute-start.12 = (f32[6288]{0:T(1024)S(1)}, f32[6288]{0:T(1024)S(1)}, u32[]{:S(2)}, u32[]{:S(2)}) collective-permute-start(f32[6288]{0:T(1024)S(1)} %get-tuple-element.101), channel_id=1, source_target_pairs={{2,4},{4,2},{3,5},{5,3},{10,12},{12,10},{11,13},{13,11},{18,20},{2... | collective-permute-start | bytes 75464 | tf_op jit(solution)/shard_map/ppermute | solution.py:26
  42.9 7.6 %collective-permute-start.13 = (f32[6288]{0:T(1024)S(1)}, f32[6288]{0:T(1024)S(1)}, u32[]{:S(2)}, u32[]{:S(2)}) collective-permute-start(f32[6288]{0:T(1024)S(1)} %get-tuple-element.102), channel_id=1, source_target_pairs={{0,2},{4,6},{2,0},{6,4},{1,3},{5,7},{3,1},{7,5},{8,10},{12,14},{10... | collective-permute-start | bytes 75464 | tf_op jit(solution)/shard_map/ppermute | solution.py:23
  51.7 0.7 %copy-start.14 = (f32[20,12,1]{1,0,2:T(8,128)S(1)}, f32[20,12,1]{1,0,2:T(8,128)}, u32[]{:S(2)}) copy-start(f32[20,12,1]{1,0,2:T(8,128)} %constant.163) | copy-start | bytes 2884
  51.9 1.2 %copy-start.6 = (f32[260,132,1]{1,0,2:T(8,128)S(1)}, f32[260,132,1]{1,0,2:T(8,128)}, u32[]{:S(2)}) copy-start(f32[260,132,1]{1,0,2:T(8,128)} %constant.164) | copy-start | bytes 411844
  53.1 0.9 %copy-start.16 = (f32[10,20,1]{1,0,2:T(8,128)S(1)}, f32[10,20,1]{1,0,2:T(8,128)}, u32[]{:S(2)}) copy-start(f32[10,20,1]{1,0,2:T(8,128)} %constant.165) | copy-start | bytes 2404
  53.1 1.2 %copy-start.7 = (f32[130,260,1]{1,0,2:T(8,128)S(1)}, f32[130,260,1]{1,0,2:T(8,128)}, u32[]{:S(2)}) copy-start(f32[130,260,1]{1,0,2:T(8,128)} %constant.166) | copy-start | bytes 405604
  54.8 0.7 %copy-start.15 = (f32[16,10,1]{1,0,2:T(8,128)S(1)}, f32[16,10,1]{1,0,2:T(8,128)}, u32[]{:S(2)}) copy-start(f32[16,10,1]{1,0,2:T(8,128)} %constant.167) | copy-start | bytes 1924
  55.1 1.1 %copy-start.3 = (f32[256,130,1]{0,1,2:T(8,128)S(1)}, f32[256,130,1]{0,1,2:T(8,128)}, u32[]{:S(2)}) copy-start(f32[256,130,1]{0,1,2:T(8,128)} %constant.168) | copy-start | bytes 399364

commit v2 on v1

v2 whole, which is shorter than its diff:
```python
import functools

import numpy as np
import jax
import jax.numpy as jnp
from jax import lax
from jax.experimental import pallas as pl
from jax.experimental.pallas import tpu as pltpu
from jax.sharding import PartitionSpec as P

ITERS = 3
TIME_STEP = 0.2
ALPHA = TIME_STEP * TIME_STEP
SUB = 8
LANE = 128
COLS = 4
SLOTS = LANE // COLS
Y_CHANNELS = (1, 3, 5, 6, 8)
Z_CHANNELS = (2, 3, 4, 7, 8)
XX, YY, ZZ, YZ, XZ, XY = range(6)


class Block:
    def __init__(self, shape, fine):
        self.layers, self.rows, self.cols = shape
        self.fine = fine
        self.inverse_step = 0.5 if fine else 0.25
        self.wide = (self.rows + SUB, self.cols + LANE)
        self.row_tiles, self.col_tiles = self.rows // SUB, self.cols // LANE
        self.planes = []
        for layer in range(self.layers):
            depth = self.depth(layer)
            for c in range(3):
                self.planes.append(("u", c, layer, 4 if depth < 4 else 2))
            for c in range(9):
                in_y, in_z = c in Y_CHANNELS, c in Z_CHANNELS
                if depth < 2:
                    count = 3 if in_y else 2
                elif depth == 2 and in_z:
                    count = 2
                else:
                    count = 1 if in_y else 0
                self.planes.append(("k", c, layer, count))
            if fine:
                self.planes.append(("m", 0, layer, 1))
            if depth < 2:
                for c in range(3):
                    self.planes.append(("p", c, layer, 2))
                self.planes.append(("d", 0, layer, 2))
        self.index = {plane[:3]: i for i, plane in enumerate(self.planes)}

    def depth(self, layer):
        return self.layers - 1 - layer if self.fine else layer

    def x_tiles(self):
        return -(-len(self.planes) // SLOTS) * (self.row_tiles + 1)


def row_table(blocks):
    table, at = {}, 0
    for count in (4, 2, 1, 3):
        for b, block in enumerate(blocks):
            for p, plane in enumerate(block.planes):
                if plane[3] == count:
                    for t in range(block.col_tiles):
                        table[b, p, t] = at
                        at += count
    return table, -(-at // SUB) * SUB


def lanes_of(t):
    return slice(LANE * t, LANE * t + LANE)


def rows_of(t):
    return slice(SUB * t, SUB * t + SUB)


def own(refs, plane, rows, lanes):
    kind, c, layer = plane[:3]
    if kind in ("m", "d"):
        return refs[kind][layer, rows, lanes]
    return refs[kind][c, layer, rows, lanes]


def is_even(axis):
    return lax.rem(lax.axis_index(axis), 2) == 0


def iota(shape, dim):
    return lax.broadcasted_iota(jnp.int32, shape, dim)


def named(refs):
    fine = dict(zip("ukmpd", refs[:5]))
    coarse = dict(zip("ukpd", refs[5:9]))
    return (fine, coarse), refs[9:]


def rows_kernel(blocks, *refs):
    sources, (first, second) = named(refs)
    table, _ = row_table(blocks)
    even = is_even("gy")
    for b, block in enumerate(blocks):
        for p, plane in enumerate(block.planes):
            count = plane[3]
            for t in range(block.col_tiles if count else 0):
                high = own(sources[b], plane, slice(block.rows - count, block.rows), lanes_of(t))
                low = own(sources[b], plane, slice(0, count), lanes_of(t))
                at = slice(table[b, p, t], table[b, p, t] + count)
                first[at, :] = lax.select(even, high, low)
                second[at, :] = lax.select(even, low, high)


def columns_kernel(blocks, both, *refs):
    sources, rest = named(refs)
    got_first, got_second = rest[:2]
    halos = rest[2:4]
    outs = rest[4:]
    table, _ = row_table(blocks)
    even = is_even("gy")
    for b, block in enumerate(blocks):
        for p, plane in enumerate(block.planes):
            count = plane[3]
            halos[b][p] = jnp.zeros((SUB, block.cols), jnp.float32)
            for t in range(block.col_tiles if count else 0):
                at = slice(table[b, p, t], table[b, p, t] + count)
                one, two = got_first[at, :], got_second[at, :]
                halos[b][p, 0:count, lanes_of(t)] = lax.select(even, one, two)
                halos[b][p, SUB - count : SUB, lanes_of(t)] = lax.select(even, two, one)
    even = is_even("gx")
    lane = iota((SUB, LANE), 1)
    slot = lax.shift_right_logical(lane, jnp.full((SUB, LANE), 2, jnp.int32))
    move = lax.select(even, jnp.int32(COLS), jnp.int32(0))
    back = COLS - move
    at = 0
    for b, block in enumerate(blocks):
        for group in range(0, len(block.planes), SLOTS):
            for rt in range(block.row_tiles + 1):
                made = [jnp.zeros((SUB, LANE), jnp.float32) for _ in outs]
                for s, plane in enumerate(block.planes[group : group + SLOTS]):
                    if rt < block.row_tiles:
                        left = own(sources[b], plane, rows_of(rt), lanes_of(0))
                        right = own(sources[b], plane, rows_of(rt), lanes_of(block.col_tiles - 1))
                    elif plane[3]:
                        left = halos[b][group + s, :, lanes_of(0)]
                        right = halos[b][group + s, :, lanes_of(block.col_tiles - 1)]
                    else:
                        continue
                    for o in range(len(outs)):
                        face = lax.select(even, right, left) if o == 0 else lax.select(even, left, right)
                        by = lax.rem(COLS * s + (move if o == 0 else back), LANE)
                        made[o] = jnp.where(slot == s, pltpu.roll(face, by, 1), made[o])
                for o, out in enumerate(outs):
                    out[at] = made[o]
                at += 1


def put(buffer, at, value):
    rows, cols = value.shape
    for rt in range(rows // SUB):
        for ct in range(cols // LANE):
            buffer[at] = value[rows_of(rt), lanes_of(ct)]
            at += 1
    return at


def take(read, at, rows, cols):
    tiles = [
        jnp.concatenate(
            [read(at + rt * (cols // LANE) + ct) for ct in range(cols // LANE)], axis=1
        )
        for rt in range(rows // SUB)
    ]
    return jnp.concatenate(tiles, axis=0), at + (rows // SUB) * (cols // LANE)


def slope(value, dim):
    size = value.shape[dim]
    return pltpu.roll(value, size - 1, dim) - pltpu.roll(value, 1, dim)


def signed(index, inner, total):
    return jnp.where(index < (inner + total) // 2, index, index - total)


def transfer(fine, coarse, halo, down):
    shape = (coarse + halo, fine + halo)
    c = signed(iota(shape, 0), coarse, coarse + halo)
    f = signed(iota(shape, 1), fine, fine + halo)
    half = jnp.right_shift(f, 1)
    if down:
        return jnp.where(half == c, 0.5, 0.0)
    other = half - 1 + 2 * jnp.bitwise_and(f, 1)
    return jnp.where(half == c, 0.75, 0.0) + jnp.where(other == c, 0.25, 0.0)


def exact_dot(a, b, dims):
    return lax.dot_general(
        a, b, (dims, ((), ())), precision=lax.Precision.HIGHEST, preferred_element_type=jnp.float32
    )


def restrict(planes, fine, coarse):
    rows = fine.wide[0]
    by_x = transfer(fine.cols, coarse.cols, LANE, True)
    by_y = transfer(fine.rows, coarse.rows, SUB, True)
    stacked = exact_dot(jnp.concatenate(planes, axis=0), by_x, ((1,), (1,)))
    return [
        exact_dot(by_y, stacked[i * rows : i * rows + rows], ((1,), (0,))) for i in range(3)
    ]


def prolong(planes, fine, coarse):
    rows = coarse.wide[0]
    by_x = transfer(fine.cols, coarse.cols, LANE, False)
    by_y = transfer(fine.rows, coarse.rows, SUB, False)
    stacked = exact_dot(jnp.concatenate(planes, axis=0), by_x, ((1,), (0,)))
    return [
        exact_dot(by_y, stacked[i * rows : i * rows + rows], ((0,), (0,))) for i in range(3)
    ]


def clamp(plane, coarse):
    for axis, dim, inner in (("gy", 0, coarse.rows), ("gx", 1, coarse.cols)):
        spot, count = lax.axis_index(axis), lax.axis_size(axis)
        index = signed(iota(plane.shape, dim), inner, plane.shape[dim])
        low = lax.slice_in_dim(plane, 0, 1, axis=dim)
        high = lax.slice_in_dim(plane, inner - 1, inner, axis=dim)
        least = lax.select(spot == 0, jnp.int32(0), jnp.int32(-plane.shape[dim]))
        most = lax.select(spot == count - 1, jnp.int32(inner - 1), jnp.int32(plane.shape[dim]))
        plane = jnp.where(index < least, low, jnp.where(index > most, high, plane))
    return plane


def interface_sizes(fine, coarse):
    wide = (coarse.wide[0] // SUB) * (coarse.wide[1] // LANE)
    inner = coarse.row_tiles * coarse.col_tiles
    return wide, inner


def z_tiles(blocks):
    faces = sum(b.row_tiles * b.col_tiles * 9 + b.row_tiles + b.col_tiles for b in blocks)
    wide, inner = interface_sizes(*blocks)
    top = 3 * wide + 3 * inner + 3 * blocks[0].row_tiles * blocks[0].col_tiles
    return max(faces, top, 9 * wide)


def widen(blocks, sources, halos, got, wides):
    even = is_even("gx")
    lane = iota((SUB, LANE), 1)
    shift = lax.select(even, jnp.int32(0), jnp.int32(COLS))
    masks = [
        jnp.bitwise_and(lane + shift, LANE - 1) < COLS,
        jnp.bitwise_and(lane + COLS - shift, LANE - 1) < COLS,
    ]
    start = 0
    for b, block in enumerate(blocks):
        rows, cols = block.rows, block.cols
        for p, plane in enumerate(block.planes):
            wide = wides[b]
            wide[p, 0:rows, 0:cols] = own(sources[b], plane, slice(0, rows), slice(0, cols))
            wide[p, rows:, 0:cols] = halos[b][p]
            s = p % SLOTS
            at = start + (p // SLOTS) * (block.row_tiles + 1)
            for rt in range(block.row_tiles + 1):
                tile = jnp.zeros((SUB, LANE), jnp.float32)
                for o, buffer in enumerate(got):
                    by = shift if o == 0 else COLS - shift
                    moved = pltpu.roll(buffer[at + rt], lax.rem(2 * LANE - COLS * s - by, LANE), 1)
                    tile = tile + jnp.where(masks[o], moved, 0.0)
                wide[p, rows_of(rt), cols:] = tile
        start += block.x_tiles()


def step_kernel(blocks, x_count, *refs):
    sources, rest = named(refs)
    halos = rest[:2]
    got = rest[2 : 2 + x_count]
    steps_out = rest[2 + x_count : 4 + x_count]
    first, second, coefs, coefs_coarse, keep = rest[4 + x_count : 9 + x_count]
    wides = rest[9 + x_count : 11 + x_count]
    stresses = rest[11 + x_count : 13 + x_count]
    starts = rest[13 + x_count : 15 + x_count]
    all_coefs = (coefs, coefs_coarse)
    spot_z, count_z = lax.axis_index("gz"), lax.axis_size("gz")
    even = is_even("gz")
    widen(blocks, sources, halos, got, wides)

    for b, block in enumerate(blocks):
        wide, stress = wides[b], stresses[b]
        layers, rows, cols, inverse = block.layers, block.rows, block.cols, block.inverse_step
        half = count_z * layers // 2

        def field(kind, c, layer):
            return wide[block.index[kind, c, layer]]

        def stretched(layer, inner=False):
            if not block.fine:
                return None
            value = field("m", 0, layer)
            if inner:
                value = value[:rows, :cols]
            return lax.select(spot_z * layers + layer < half, value, jnp.ones_like(value))

        def along_z(below, above, stretch):
            if below is None:
                value = above
            elif above is None:
                value = -below
            else:
                value = above - below
            value = value * inverse
            return value if stretch is None else value * stretch

        for layer in range(layers):
            k = [functools.partial(field, "k", c, layer) for c in range(9)]
            u = [field("u", c, layer) for c in range(3)]
            stretch = stretched(layer)
            dz = [
                along_z(
                    field("u", c, layer - 1) if layer else None,
                    field("u", c, layer + 1) if layer < layers - 1 else None,
                    stretch,
                )
                for c in range(3)
            ]
            nx = slope(u[0], 1) * inverse
            ny = slope(u[1], 0) * inverse
            nz = dz[2]
            stress[XX, layer] = k[0]() * nx + k[6]() * ny + k[7]() * nz
            stress[YY, layer] = k[6]() * nx + k[1]() * ny + k[8]() * nz
            stress[ZZ, layer] = k[7]() * nx + k[8]() * ny + k[2]() * nz
            stress[YZ, layer] = k[3]() * (dz[1] + slope(u[2], 0) * inverse)
            stress[XZ, layer] = k[4]() * (dz[0] + slope(u[2], 1) * inverse)
            stress[XY, layer] = k[5]() * ((slope(u[0], 0) + slope(u[1], 1)) * inverse)

        for side, layer in enumerate((0, layers - 1)):
            stretch = stretched(layer)
            for i, c in enumerate((4, 3, 2, 7, 8)):
                value = field("k", c, layer) * inverse
                all_coefs[b][side, i] = value if stretch is None else value * stretch

        table = ((XX, XY, XZ), (XY, YY, YZ), (XZ, YZ, ZZ))
        for layer in range(layers):
            depth = block.depth(layer)
            stretch = stretched(layer, depth >= 2)
            for c in range(3):
                part = table[c]
                height, width = (slice(0, None),) * 2 if depth < 2 else (slice(0, rows), slice(0, cols))
                dx = slope(stress[part[0], layer, height, :], 1)[:, width] * inverse
                dy = slope(stress[part[1], layer, :, width], 0)[height] * inverse
                dz = along_z(
                    stress[part[2], layer - 1, height, width] if layer else None,
                    stress[part[2], layer + 1, height, width] if layer < layers - 1 else None,
                    stretch,
                )
                if depth < 2:
                    now, prev = field("u", c, layer), field("p", c, layer)
                    density = field("d", 0, layer)
                    density = jnp.where(density > 0, density, 1.0)
                else:
                    now = sources[b]["u"][c, layer]
                    prev = sources[b]["p"][c, layer]
                    density = sources[b]["d"][layer]
                value = (2.0 * now - prev) + ALPHA * (dx + dy + dz) / density
                steps_out[b][c, layer] = value[:rows, :cols]
                if depth == 0:
                    starts[b][c] = value
                elif depth == 1 and block.fine:
                    keep[c] = value
                elif depth == 1:
                    starts[b][3 + c] = value

    fine, coarse = blocks
    for i, c in enumerate((4, 3, 2)):
        keep[3 + i] = wides[0][fine.index["k", c, fine.layers - 1]]

    at = 0
    lane = iota((SUB, LANE), 1)

    def send(tile_low, tile_high):
        nonlocal at
        first[at] = lax.select(even, tile_high, tile_low)
        second[at] = lax.select(even, tile_low, tile_high)
        at += 1

    for b, block in enumerate(blocks):
        last = block.layers - 1
        rows, cols = block.rows, block.cols
        for rt in range(block.row_tiles):
            for ct in range(block.col_tiles):
                spot = (rows_of(rt), lanes_of(ct))
                for c in range(3):
                    send(sources[b]["u"][(c, 0) + spot], sources[b]["u"][(c, last) + spot])
                for kind in (XZ, YZ, ZZ):
                    send(stresses[b][(kind, 0) + spot], stresses[b][(kind, last) + spot])
                for i in range(3):
                    send(all_coefs[b][(0, i) + spot], all_coefs[b][(1, i) + spot])
        for ct in range(block.col_tiles):
            for c in range(3):
                low = block.index["u", c, 0]
                high = block.index["u", c, last]
                for edge, to in ((rows, c), (rows + SUB - 1, 4 + c)):
                    one = wides[b][low, edge : edge + 1, lanes_of(ct)]
                    two = wides[b][high, edge : edge + 1, lanes_of(ct)]
                    first[at, to : to + 1] = lax.select(even, two, one)
                    second[at, to : to + 1] = lax.select(even, one, two)
            at += 1
        for rt in range(block.row_tiles):
            pair = [jnp.zeros((SUB, LANE), jnp.float32)] * 2
            for c in range(3):
                for side, layer in enumerate((0, last)):
                    halo = wides[b][block.index["u", c, layer], rows_of(rt), cols:]
                    pair[side] = jnp.where(
                        jnp.right_shift(lane, 1) == c, pltpu.roll(halo, 1 + 2 * c, 1), pair[side]
                    )
            send(*pair)

    @pl.when(spot_z == count_z - 1)
    def _():
        at = 0
        down = restrict([starts[0][c] for c in range(3)], fine, coarse)
        for plane in down:
            at = put(second, at, plane)
        down = restrict([keep[c] for c in range(3)], fine, coarse)
        for plane in down:
            at = put(second, at, plane[: coarse.rows, : coarse.cols])
        for c in range(3):
            at = put(second, at, keep[3 + c][: fine.rows, : fine.cols])

    @pl.when(spot_z == 0)
    def _():
        wide, _ = interface_sizes(fine, coarse)
        for i, c in enumerate((4, 3, 2)):
            k = wides[1][coarse.index["k", c, 0]]
            start, below = starts[1][i], starts[1][3 + i]
            put(second, wide * i, k * (below - start) * 0.25)
            put(second, wide * (3 + i), k * (below - 0.5 * start) * 0.25)
            put(second, wide * (6 + i), k * 0.125)


def last_kernel(blocks, *refs):
    (step_f, step_c, coef_f, coef_c, got_first, got_second, sent, keep) = refs[:8]
    now_f, now_c, metric, density_f, density_c = refs[8:13]
    outs = refs[13:15]
    fine, coarse = blocks
    spot_z, count_z = lax.axis_index("gz"), lax.axis_size("gz")
    even = is_even("gz")
    inside = (spot_z > 0, spot_z < count_z - 1)
    lane = iota((SUB, LANE), 1)

    def reader(side):
        def read(at):
            one, two = got_first[at], got_second[at]
            value = lax.select(even, two, one) if side == 0 else lax.select(even, one, two)
            return lax.select(inside[side], value, jnp.zeros_like(value))

        return read

    start = 0
    for b, block in enumerate(blocks):
        rows, cols, layers, inverse = block.rows, block.cols, block.layers, block.inverse_step
        half = count_z * layers // 2
        now = (now_f, now_c)[b]
        step = (step_f, step_c)[b]
        density = (density_f, density_c)[b]
        coef = (coef_f, coef_c)[b]
        out = outs[b]
        extra = {}

        def add(c, layer, value):
            extra[c, layer] = extra[c, layer] + value if (c, layer) in extra else value

        def stretched(layer, value):
            value = value * inverse
            if not block.fine:
                return value
            factor = metric[layer]
            factor = lax.select(
                spot_z * layers + layer < half, factor, jnp.ones_like(factor)
            )
            return value * factor

        for side, layer, inner in ((0, 0, 1), (1, layers - 1, layers - 2)):
            read = reader(side)
            sign = -1.0 if side == 0 else 1.0
            tiles = block.row_tiles * block.col_tiles

            def plane(k):
                return jnp.concatenate(
                    [
                        jnp.concatenate(
                            [
                                read(start + 9 * (rt * block.col_tiles + ct) + k)
                                for ct in range(block.col_tiles)
                            ],
                            axis=1,
                        )
                        for rt in range(block.row_tiles)
                    ],
                    axis=0,
                )

            row = iota((SUB, LANE), 0)
            beyond = []
            for c in range(3):
                edges = []
                for ct in range(block.col_tiles):
                    tile = read(start + 9 * tiles + ct)
                    ahead = pltpu.roll(tile, (SUB - c) % SUB, 0)
                    behind = pltpu.roll(tile, 3 - c, 0)
                    edges.append(
                        jnp.where(row == 0, ahead, jnp.where(row == SUB - 1, behind, 0.0))
                    )
                sides = []
                for rt in range(block.row_tiles):
                    tile = read(start + 9 * tiles + block.col_tiles + rt)
                    tile = pltpu.roll(tile, LANE - 1 - 2 * c, 1)
                    sides.append(jnp.where((lane == 0) | (lane == LANE - 1), tile, 0.0))
                sides.append(jnp.zeros((SUB, LANE), jnp.float32))
                left = jnp.concatenate(
                    [plane(c), jnp.concatenate(edges, axis=1)], axis=0
                )
                beyond.append(
                    sign * jnp.concatenate([left, jnp.concatenate(sides, axis=0)], axis=1)
                )
            d_xz = coef[side, 0] * beyond[0]
            d_yz = coef[side, 1] * beyond[1]
            d_zz = coef[side, 2] * beyond[2]
            d_xx = coef[side, 3] * beyond[2]
            d_yy = coef[side, 4] * beyond[2]
            add(0, layer, slope(d_xx, 1)[:rows, :cols] * inverse)
            add(1, layer, slope(d_yy, 0)[:rows, :cols] * inverse)
            add(2, layer, (slope(d_xz, 1) + slope(d_yz, 0))[:rows, :cols] * inverse)
            for c, change in enumerate((d_xz, d_yz, d_zz)):
                there = plane(3 + c) - sign * plane(6 + c) * now[c, layer]
                add(c, layer, stretched(layer, sign * there))
                add(c, inner, stretched(inner, sign * change[:rows, :cols]))
        for layer in range(layers):
            for c in range(3):
                value = step[c, layer]
                if (c, layer) in extra:
                    value = value + ALPHA * extra[c, layer] / density[layer]
                out[c, layer] = value
        start += 9 * block.row_tiles * block.col_tiles + block.row_tiles + block.col_tiles

    wide, inner = interface_sizes(fine, coarse)
    height, width = coarse.wide

    @pl.when(spot_z == count_z - 1)
    def _():
        read = lambda at: got_second[at]
        part = [take(read, wide * i, height, width)[0] for i in range(9)]
        above = [keep[c] for c in range(3)]
        k = [jnp.where(keep[3 + c] > 0, keep[3 + c], 1.0) for c in range(3)]
        raised = prolong([clamp(part[c], coarse) for c in range(3)], fine, coarse)
        down = restrict([above[c] + raised[c] / k[c] for c in range(3)], fine, coarse)
        tractions = [clamp(part[3 + c] - part[6 + c] * down[c], coarse) for c in range(3)]
        raised = prolong(tractions, fine, coarse)
        for c in range(3):
            value = above[c] + raised[c] / k[c]
            outs[0][c, fine.layers - 1] = value[: fine.rows, : fine.cols]

    @pl.when(spot_z == 0)
    def _():
        read = lambda at: got_second[at]
        mine = lambda at: sent[at]
        tractions = []
        for c in range(3):
            down = take(read, wide * c, height, width)[0]
            part = take(mine, wide * (3 + c), height, width)[0]
            k = take(mine, wide * (6 + c), height, width)[0]
            tractions.append(clamp(part - k * down, coarse))
        raised = prolong(tractions, fine, coarse)
        at = 3 * wide + 3 * inner
        shares = []
        for c in range(3):
            k, at = take(read, at, fine.rows, fine.cols)
            share = raised[c][: fine.rows, : fine.cols] / k
            share = jnp.concatenate(
                [share, jnp.zeros((SUB, fine.cols), jnp.float32)], axis=0
            )
            shares.append(
                jnp.concatenate(
                    [share, jnp.zeros((fine.wide[0], LANE), jnp.float32)], axis=1
                )
            )
        down = restrict(shares, fine, coarse)
        for c in range(3):
            above = take(read, 3 * wide + inner * c, coarse.rows, coarse.cols)[0]
            total = above + down[c][: coarse.rows, : coarse.cols]
            outs[1][c, 0] = 0.5 * (step_c[c, 0] + total)


def pair_tables(count):
    even = [(i, i + 1) for i in range(0, count - 1, 2)]
    odd = [(i, i + 1) for i in range(1, count - 1, 2)]
    both = lambda some: some + [(b, a) for a, b in some]
    return both(even), both(odd)


def f32(*shape):
    return jax.ShapeDtypeStruct(shape, jnp.float32)


def kernel(body, out_shape, count, scratch=()):
    space = pl.BlockSpec(memory_space=pltpu.VMEM)
    return pl.pallas_call(
        body,
        out_shape=out_shape,
        in_specs=[space] * count,
        out_specs=[space] * len(out_shape),
        scratch_shapes=[pltpu.VMEM(shape, jnp.float32) for shape in scratch],
    )


def per_device(
    fine_now,
    fine_prev,
    stiffness,
    metric,
    density,
    coarse_now,
    coarse_prev,
    coarse_stiffness,
    coarse_density,
):
    blocks = fine, coarse = (
        Block(fine_now.shape[1:], True),
        Block(coarse_now.shape[1:], False),
    )
    arrays = [
        fine_now, stiffness, metric, fine_prev, density,
        coarse_now, coarse_stiffness, coarse_prev, coarse_density,
    ]
    count_z = lax.axis_size("gz")
    assert count_z % 2 == 0

    _, row_count = row_table(blocks)
    sent = kernel(functools.partial(rows_kernel, blocks), [f32(row_count, LANE)] * 2, 9)(*arrays)
    by_row = [
        lax.ppermute(buffer, "gy", pairs) if pairs else jnp.zeros_like(buffer)
        for buffer, pairs in zip(sent, pair_tables(lax.axis_size("gy")))
    ]

    tables = [pairs for pairs in pair_tables(lax.axis_size("gx")) if pairs]
    tiles = sum(block.x_tiles() for block in blocks)
    halo_shapes = [f32(len(block.planes), SUB, block.cols) for block in blocks]
    made = kernel(
        functools.partial(columns_kernel, blocks, len(tables)),
        halo_shapes + [f32(tiles, SUB, LANE)] * len(tables),
        11,
    )(*arrays, *by_row)
    halos = made[:2]
    by_column = [
        lax.ppermute(buffer, "gx", pairs) for buffer, pairs in zip(made[2:], tables)
    ]

    z_shape = f32(z_tiles(blocks), SUB, LANE)
    step_f, step_c, first, second, coef_f, coef_c, keep = kernel(
        functools.partial(step_kernel, blocks, len(tables)),
        [f32(*fine_now.shape), f32(*coarse_now.shape), z_shape, z_shape]
        + [f32(2, 5, *block.wide) for block in blocks]
        + [f32(6, *fine.wide)],
        11 + len(tables),
        [(len(block.planes), *block.wide) for block in blocks]
        + [(6, block.layers, *block.wide) for block in blocks]
        + [(3, *fine.wide), (6, *coarse.wide)],
    )(*arrays, *halos, *by_column)
    even_pairs, odd_pairs = pair_tables(count_z)
    odd_pairs = odd_pairs + [(0, count_z - 1), (count_z - 1, 0)]
    got_first = lax.ppermute(first, "gz", even_pairs)
    got_second = lax.ppermute(second, "gz", odd_pairs)

    return tuple(
        kernel(
            functools.partial(last_kernel, blocks),
            [f32(*fine_now.shape), f32(*coarse_now.shape)],
            13,
        )(
            step_f, step_c, coef_f, coef_c, got_first, got_second, second, keep,
            fine_now, coarse_now, metric, density, coarse_density,
        )
    )


def solution(mesh):
    block = P(None, "gz", "gy", "gx")
    field = P("gz", "gy", "gx")
    return jax.shard_map(
        per_device,
        mesh=mesh,
        in_specs=(block, block, block, field, field, block, block, block, field),
        out_specs=(block, block),
        check_vma=False,
    )
```

time: 59.5 us -> 46.5 us (0.78)
  the two profiles are of different devices: /device:TPU:0 before, /device:TPU:2 now
where the time goes in v2:
time: 46.5 us; the launch traced here: 46.2 us
  waiting for transfers between devices  20 us (43%)
  Pallas kernels  13.2 us (28%)
  starting transfers between devices  10.3 us (22%)
  local copies, waits for them, and re-layouts  2.02 us (4%)
  between operations  0.65 us (1%)
    ppermute x2, waiting for transfers between devices, per_device(): lax.ppermute(buffer, 'gy', pairs)  8.36 us
    ppermute x1, waiting for transfers between devices, per_device(): got_second = lax.ppermute(second, 'gz', odd_pairs)  8.23 us
    ppermute x2, starting transfers between devices, per_device(): lax.ppermute(buffer, 'gy', pairs)  4.88 us
    pallas_call x1, Pallas kernels, per_device(): kernel(functools.partial(step_kernel, blocks, len(tables)), [f32(*fine_no...  4.27 us
    ppermute x1, starting transfers between devices, per_device(): got_second = lax.ppermute(second, 'gz', odd_pairs)  3.9 us
    pallas_call x1, Pallas kernels, per_device(): kernel(functools.partial(last_kernel, blocks), [f32(*fine_now.shape), f32...  3.76 us
    pallas_call x1, Pallas kernels, per_device(): kernel(functools.partial(columns_kernel, blocks, len(tables)), halo_shape...  2.87 us
    pallas_call x1, Pallas kernels, per_device(): kernel(functools.partial(rows_kernel, blocks), [f32(row_count, LANE)] * 2...  2.31 us
  transfers between devices with their start and end apart: 5, of which 5 were waited for; matrix products, arithmetic and copies ran while one was open for 0% of the time, Pallas kernels for 0%

profile of v2, /device:TPU:2, one launch (start us, length us, event | category | flops | bytes accessed | tf_op | source)
XLA Modules:
  0.0 46.2 jit_solution(17424106247125645725)
XLA Ops:
  0.6 2.3 %shard_map.104 = (f32[440,128]{1,0:T(8,128)}, f32[440,128]{1,0:T(8,128)}) custom-call(f32[3,4,16,256]{3,2,1,0:T(8,128)} %refs_8_.7, f32[9,4,16,256]{3,2,1,0:T(8,128)} %refs_1_.5, f32[4,16,256]{2,1,0:T(8,128)} %refs_10_.1, f32[3,4,16,256]{3,2,1,0:T(8,128)} %refs_3_.5, f32[4,16,256]{2,1,0:T(8,128)} %refs_11_.1, f32[3,8,8,128]{3,2,1,0:T(8,128)} %refs_9_.1, ...), custom_call_target="tpu_custom_call" | custom-call | tf_op jit(solution)/shard_map/pallas_call | solution.py:641
  2.9 0.0 collective-permute-start
  2.9 4.9 %collective-permute-start.1 = (f32[440,128]{1,0:T(8,128)}, f32[440,128]{1,0:T(8,128)S(1)}, u32[]{:S(2)}, u32[]{:S(2)}) collective-permute-start(f32[440,128]{1,0:T(8,128)} %get-tuple-element.15), channel_id=1, source_target_pairs={{2,4},{4,2},{3,5},{5,3},{10,12},{12,10},{11,13},{13,11},{18,20},{2... | collective-permute-start | bytes 675848 | tf_op jit(solution)/shard_map/ppermute | solution.py:643
  7.8 2.6 %collective-permute-done.refs_9_ = f32[440,128]{1,0:T(8,128)S(1)} collective-permute-done((f32[440,128]{1,0:T(8,128)}, f32[440,128]{1,0:T(8,128)S(1)}, u32[]{:S(2)}, u32[]{:S(2)}) %collective-permute-start) | collective-permute-done | bytes 225312 | tf_op jit(solution)/shard_map/ppermute | solution.py:643
  10.4 0.0 copy-start
  10.4 5.8 %collective-permute-done.1.refs_10_ = f32[440,128]{1,0:T(8,128)S(1)} collective-permute-done((f32[440,128]{1,0:T(8,128)}, f32[440,128]{1,0:T(8,128)S(1)}, u32[]{:S(2)}, u32[]{:S(2)}) %collective-permute-start.1) | collective-permute-done | bytes 225312 | tf_op jit(solution)/shard_map/ppermute | solution.py:643
  16.2 0.0 copy-done
  16.2 0.0 copy-start.1
  16.2 0.7 %copy-done.1 = f32[440,128]{1,0:T(8,128)} copy-done((f32[440,128]{1,0:T(8,128)}, f32[440,128]{1,0:T(8,128)S(1)}, u32[]{:S(2)}) %copy-start.1) | copy-done | bytes 225304
  16.9 2.9 %shard_map.105 = (f32[60,8,256]{2,1,0:T(8,128)}, f32[104,8,128]{2,1,0:T(8,128)}, f32[14,8,128]{2,1,0:T(8,128)}) custom-call(f32[3,4,16,256]{3,2,1,0:T(8,128)} %refs_8_.7, f32[9,4,16,256]{3,2,1,0:T(8,128)} %refs_1_.5, f32[4,16,256]{2,1,0:T(8,128)} %refs_10_.1, f32[3,4,16,256]{3,2,1,0:T(8,128)} %refs_3_.5, f32[4,16,256]{2,1,0:T(8,128)} %refs_11_.1, ...), custom_call_target="tpu_custom_call" | custom-call | tf_op jit(solution)/shard_map/pallas_call | solution.py:650
  19.8 0.0 collective-permute-start.2
  19.8 1.4 %collective-permute-done.2.refs_11_ = f32[14,8,128]{2,1,0:T(8,128)S(1)} collective-permute-done((f32[14,8,128]{2,1,0:T(8,128)}, f32[14,8,128]{2,1,0:T(8,128)S(1)}, u32[]{:S(2)}, u32[]{:S(2)}) %collective-permute-start.2) | collective-permute-done | bytes 57376 | tf_op jit(solution)/shard_map/ppermute | solution.py:657
  21.2 0.0 copy-start.4
  21.2 0.6 %copy-done.4 = f32[14,8,128]{2,1,0:T(8,128)} copy-done((f32[14,8,128]{2,1,0:T(8,128)}, f32[14,8,128]{2,1,0:T(8,128)S(1)}, u32[]{:S(2)}) %copy-start.4) | copy-done | bytes 57368
  21.8 4.3 %shard_map.106 = (f32[3,4,16,256]{3,2,1,0:T(8,128)}, f32[3,8,8,128]{3,2,1,0:T(8,128)}, f32[51,8,128]{2,1,0:T(8,128)}, f32[51,8,128]{2,1,0:T(8,128)}, f32[2,5,24,...) custom-call(f32[3,4,16,256]{3,2,1,0:T(8,128)} %refs_8_.7, f32[9,4,16,256]{3,2,1,0:T(8,128)} %refs_1_.5, ...), custom_call_target="tpu_custom_call" | custom-call | tf_op jit(solution)/shard_map/pallas_call | solution.py:661
  26.1 1.6 %collective-permute-start.3 = (f32[51,8,128]{2,1,0:T(8,128)}, f32[51,8,128]{2,1,0:T(8,128)S(1)}, u32[]{:S(2)}, u32[]{:S(2)}) collective-permute-start(f32[51,8,128]{2,1,0:T(8,128)} %get-tuple-element.23), channel_id=1, source_target_pairs={{0,8},{16,24},{8,0},{24,16},{1,9},{17,25},{9,1},{25,17},{2,10},{18... | collective-permute-start | bytes 626696 | tf_op jit(solution)/shard_map/ppermute | solution.py:673
  27.7 3.9 %collective-permute-start.4 = (f32[51,8,128]{2,1,0:T(8,128)}, f32[51,8,128]{2,1,0:T(8,128)S(1)}, u32[]{:S(2)}, u32[]{:S(2)}) collective-permute-start(f32[51,8,128]{2,1,0:T(8,128)} %get-tuple-element.24.refs_6_), channel_id=1, source_target_pairs={{8,16},{16,8},{0,24},{24,0},{9,17},{17,9},{1,25},{25,1},{10,18},{1... | collective-permute-start | bytes 626696 | tf_op jit(solution)/shard_map/ppermute | solution.py:674
  31.6 2.0 %collective-permute-done.3.refs_4_ = f32[51,8,128]{2,1,0:T(8,128)S(1)} collective-permute-done((f32[51,8,128]{2,1,0:T(8,128)}, f32[51,8,128]{2,1,0:T(8,128)S(1)}, u32[]{:S(2)}, u32[]{:S(2)}) %collective-permute-start.3) | collective-permute-done | bytes 208928 | tf_op jit(solution)/shard_map/ppermute | solution.py:673
  33.6 0.0 copy-start.2
  33.6 8.2 %collective-permute-done.4.refs_5_ = f32[51,8,128]{2,1,0:T(8,128)S(1)} collective-permute-done((f32[51,8,128]{2,1,0:T(8,128)}, f32[51,8,128]{2,1,0:T(8,128)S(1)}, u32[]{:S(2)}, u32[]{:S(2)}) %collective-permute-start.4) | collective-permute-done | bytes 208928 | tf_op jit(solution)/shard_map/ppermute | solution.py:674
  41.8 0.0 copy-start.3
  41.8 0.0 copy-done.2
  41.8 0.7 %copy-done.3 = f32[51,8,128]{2,1,0:T(8,128)} copy-done((f32[51,8,128]{2,1,0:T(8,128)}, f32[51,8,128]{2,1,0:T(8,128)S(1)}, u32[]{:S(2)}) %copy-start.3) | copy-done | bytes 208920
  42.5 3.8 %shard_map.107 = (f32[3,4,16,256]{3,2,1,0:T(8,128)}, f32[3,8,8,128]{3,2,1,0:T(8,128)}) custom-call(f32[3,4,16,256]{3,2,1,0:T(8,128)} %get-tuple-element.19.refs_0_, f32[3,8,8,128]{3,2,1,0:T(8,128)} %get-tuple-element.20.refs_1_, f32[2,5,24,384]{3,2,1,0:T(8,128)} %get-tuple-element.21.refs_2_, f32[2,5,16,256]{3,2,1,0:T(8,128)} %get-tuple-element.22.refs_3_, ...), custom_call_target="tpu_custom_call" | custom-call | tf_op jit(solution)/shard_map/pallas_call | solution.py:677
Async XLA Ops:
  2.9 7.5 %collective-permute-start = (f32[440,128]{1,0:T(8,128)}, f32[440,128]{1,0:T(8,128)S(1)}, u32[]{:S(2)}, u32[]{:S(2)}) collective-permute-start(f32[440,128]{1,0:T(8,128)} %get-tuple-element.14), channel_id=1, source_target_pairs={{0,2},{4,6},{2,0},{6,4},{1,3},{5,7},{3,1},{7,5},{8,10},{12,14},{10... | collective-permute-start | bytes 675848 | tf_op jit(solution)/shard_map/ppermute | solution.py:643
  2.9 13.2 %collective-permute-start.1 = (f32[440,128]{1,0:T(8,128)}, f32[440,128]{1,0:T(8,128)S(1)}, u32[]{:S(2)}, u32[]{:S(2)}) collective-permute-start(f32[440,128]{1,0:T(8,128)} %get-tuple-element.15), channel_id=1, source_target_pairs={{2,4},{4,2},{3,5},{5,3},{10,12},{12,10},{11,13},{13,11},{18,20},{2... | collective-permute-start | bytes 675848 | tf_op jit(solution)/shard_map/ppermute | solution.py:643
  10.4 5.8 %copy-start = (f32[440,128]{1,0:T(8,128)}, f32[440,128]{1,0:T(8,128)S(1)}, u32[]{:S(2)}) copy-start(f32[440,128]{1,0:T(8,128)S(1)} %collective-permute-done.refs_9_) | copy-start | bytes 675844
  16.2 0.7 %copy-start.1 = (f32[440,128]{1,0:T(8,128)}, f32[440,128]{1,0:T(8,128)S(1)}, u32[]{:S(2)}) copy-start(f32[440,128]{1,0:T(8,128)S(1)} %collective-permute-done.1.refs_10_) | copy-start | bytes 675844
  19.8 1.5 %collective-permute-start.2 = (f32[14,8,128]{2,1,0:T(8,128)}, f32[14,8,128]{2,1,0:T(8,128)S(1)}, u32[]{:S(2)}, u32[]{:S(2)}) collective-permute-start(f32[14,8,128]{2,1,0:T(8,128)} %get-tuple-element.18), channel_id=1, source_target_pairs={{0,1},{1,0},{2,3},{3,2},{4,5},{5,4},{6,7},{7,6},{8,9},{9,8},{10,11... | collective-permute-start | bytes 172040 | tf_op jit(solution)/shard_map/ppermute | solution.py:657
  21.2 0.6 %copy-start.4 = (f32[14,8,128]{2,1,0:T(8,128)}, f32[14,8,128]{2,1,0:T(8,128)S(1)}, u32[]{:S(2)}) copy-start(f32[14,8,128]{2,1,0:T(8,128)S(1)} %collective-permute-done.2.refs_11_) | copy-start | bytes 172036
  26.1 7.4 %collective-permute-start.3 = (f32[51,8,128]{2,1,0:T(8,128)}, f32[51,8,128]{2,1,0:T(8,128)S(1)}, u32[]{:S(2)}, u32[]{:S(2)}) collective-permute-start(f32[51,8,128]{2,1,0:T(8,128)} %get-tuple-element.23), channel_id=1, source_target_pairs={{0,8},{16,24},{8,0},{24,16},{1,9},{17,25},{9,1},{25,17},{2,10},{18... | collective-permute-start | bytes 626696 | tf_op jit(solution)/shard_map/ppermute | solution.py:673
  27.7 14.1 %collective-permute-start.4 = (f32[51,8,128]{2,1,0:T(8,128)}, f32[51,8,128]{2,1,0:T(8,128)S(1)}, u32[]{:S(2)}, u32[]{:S(2)}) collective-permute-start(f32[51,8,128]{2,1,0:T(8,128)} %get-tuple-element.24.refs_6_), channel_id=1, source_target_pairs={{8,16},{16,8},{0,24},{24,0},{9,17},{17,9},{1,25},{25,1},{10,18},{1... | collective-permute-start | bytes 626696 | tf_op jit(solution)/shard_map/ppermute | solution.py:674
  33.6 8.2 %copy-start.2 = (f32[51,8,128]{2,1,0:T(8,128)}, f32[51,8,128]{2,1,0:T(8,128)S(1)}, u32[]{:S(2)}) copy-start(f32[51,8,128]{2,1,0:T(8,128)S(1)} %collective-permute-done.3.refs_4_) | copy-start | bytes 626692
  41.8 0.7 %copy-start.3 = (f32[51,8,128]{2,1,0:T(8,128)}, f32[51,8,128]{2,1,0:T(8,128)S(1)}, u32[]{:S(2)}) copy-start(f32[51,8,128]{2,1,0:T(8,128)S(1)} %collective-permute-done.4.refs_5_) | copy-start | bytes 626692

commit v3 on v2

--- a/solution.py
+++ b/solution.py
@@ -12,6 +12,7 @@
 TIME_STEP = 0.2
 ALPHA = TIME_STEP * TIME_STEP
 SUB = 8
+VMEM_BYTES = 16 * 2**20
 LANE = 128
 COLS = 4
 SLOTS = LANE // COLS
@@ -31,22 +32,17 @@
         for layer in range(self.layers):
             depth = self.depth(layer)
             for c in range(3):
-                self.planes.append(("u", c, layer, 4 if depth < 4 else 2))
+                self.planes.append(("u", c, layer, 2, (2, 2, 1)[depth] if depth < 3 else 0))
             for c in range(9):
-                in_y, in_z = c in Y_CHANNELS, c in Z_CHANNELS
-                if depth < 2:
-                    count = 3 if in_y else 2
-                elif depth == 2 and in_z:
-                    count = 2
-                else:
-                    count = 1 if in_y else 0
-                self.planes.append(("k", c, layer, count))
+                base = 1 if c in Y_CHANNELS else 0
+                extra = 2 if depth < 2 else (2 - base if depth == 2 and c in Z_CHANNELS else 0)
+                self.planes.append(("k", c, layer, base, extra))
             if fine:
-                self.planes.append(("m", 0, layer, 1))
+                self.planes.append(("m", 0, layer, 1, 0))
             if depth < 2:
                 for c in range(3):
-                    self.planes.append(("p", c, layer, 2))
-                self.planes.append(("d", 0, layer, 2))
+                    self.planes.append(("p", c, layer, 0, 2))
+                self.planes.append(("d", 0, layer, 0, 2))
         self.index = {plane[:3]: i for i, plane in enumerate(self.planes)}
 
     def depth(self, layer):
@@ -57,15 +53,25 @@
 
 
 def row_table(blocks):
-    table, at = {}, 0
-    for count in (4, 2, 1, 3):
+    base, extra, at = {}, {}, 0
+    for count in (2, 1):
         for b, block in enumerate(blocks):
             for p, plane in enumerate(block.planes):
                 if plane[3] == count:
                     for t in range(block.col_tiles):
-                        table[b, p, t] = at
+                        base[b, p, t] = slice(at, at + count)
                         at += count
-    return table, -(-at // SUB) * SUB
+    start, ends = at, []
+    for b, block in enumerate(blocks):
+        at = start
+        for count in (2, 1):
+            for p, plane in enumerate(block.planes):
+                if plane[4] == count:
+                    for t in range(block.col_tiles):
+                        extra[b, p, t] = slice(at, at + count)
+                        at += count
+        ends.append(at)
+    return base, extra, -(-max(ends) // SUB) * SUB
 
 
 def lanes_of(t):
@@ -98,18 +104,39 @@
 
 
 def rows_kernel(blocks, *refs):
-    sources, (first, second) = named(refs)
-    table, _ = row_table(blocks)
+    held, loaded, (first, second, done) = refs[:9], refs[9:18], refs[18:]
+    copies = [
+        pltpu.make_async_copy(source, target, done.at[i])
+        for i, (source, target) in enumerate(zip(held, loaded))
+    ]
+    for copy in copies:
+        copy.start()
+    for copy in copies:
+        copy.wait()
+    sources, _ = named(loaded)
+    base, extra, _ = row_table(blocks)
     even = is_even("gy")
+    is_low = lax.axis_index("gz") == 0
+
+    def move(b, block, plane, at, t, near, far):
+        high = own(sources[b], plane, slice(block.rows - far, block.rows - near), lanes_of(t))
+        low = own(sources[b], plane, slice(near, far), lanes_of(t))
+        first[at, :] = lax.select(even, high, low)
+        second[at, :] = lax.select(even, low, high)
+
     for b, block in enumerate(blocks):
         for p, plane in enumerate(block.planes):
-            count = plane[3]
-            for t in range(block.col_tiles if count else 0):
-                high = own(sources[b], plane, slice(block.rows - count, block.rows), lanes_of(t))
-                low = own(sources[b], plane, slice(0, count), lanes_of(t))
-                at = slice(table[b, p, t], table[b, p, t] + count)
-                first[at, :] = lax.select(even, high, low)
-                second[at, :] = lax.select(even, low, high)
+            for t in range(block.col_tiles):
+                if plane[3]:
+                    move(b, block, plane, base[b, p, t], t, 0, plane[3])
+    for b, block in enumerate(blocks):
+
+        @pl.when(is_low != block.fine)
+        def _():
+            for p, plane in enumerate(block.planes):
+                for t in range(block.col_tiles):
+                    if plane[4]:
+                        move(b, block, plane, extra[b, p, t], t, plane[3], plane[3] + plane[4])
 
 
 def columns_kernel(blocks, both, *refs):
@@ -117,17 +144,30 @@
     got_first, got_second = rest[:2]
     halos = rest[2:4]
     outs = rest[4:]
-    table, _ = row_table(blocks)
+    base, extra, _ = row_table(blocks)
     even = is_even("gy")
+    is_low = lax.axis_index("gz") == 0
+
+    def place(b, p, at, t, near, far):
+        one, two = got_first[at, :], got_second[at, :]
+        halos[b][p, near:far, lanes_of(t)] = lax.select(even, one, two)
+        halos[b][p, SUB - far : SUB - near, lanes_of(t)] = lax.select(even, two, one)
+
     for b, block in enumerate(blocks):
         for p, plane in enumerate(block.planes):
-            count = plane[3]
             halos[b][p] = jnp.zeros((SUB, block.cols), jnp.float32)
-            for t in range(block.col_tiles if count else 0):
-                at = slice(table[b, p, t], table[b, p, t] + count)
-                one, two = got_first[at, :], got_second[at, :]
-                halos[b][p, 0:count, lanes_of(t)] = lax.select(even, one, two)
-                halos[b][p, SUB - count : SUB, lanes_of(t)] = lax.select(even, two, one)
+            for t in range(block.col_tiles):
+                if plane[3]:
+                    place(b, p, base[b, p, t], t, 0, plane[3])
+    for b, block in enumerate(blocks):
+
+        @pl.when(is_low != block.fine)
+        def _():
+            for p, plane in enumerate(block.planes):
+                for t in range(block.col_tiles):
+                    if plane[4]:
+                        place(b, p, extra[b, p, t], t, plane[3], plane[3] + plane[4])
+
     even = is_even("gx")
     lane = iota((SUB, LANE), 1)
     slot = lax.shift_right_logical(lane, jnp.full((SUB, LANE), 2, jnp.int32))
@@ -142,7 +182,7 @@
                     if rt < block.row_tiles:
                         left = own(sources[b], plane, rows_of(rt), lanes_of(0))
                         right = own(sources[b], plane, rows_of(rt), lanes_of(block.col_tiles - 1))
-                    elif plane[3]:
+                    elif plane[3] + plane[4]:
                         left = halos[b][group + s, :, lanes_of(0)]
                         right = halos[b][group + s, :, lanes_of(block.col_tiles - 1)]
                     else:
@@ -233,17 +273,67 @@
     return plane
 
 
-def interface_sizes(fine, coarse):
-    wide = (coarse.wide[0] // SUB) * (coarse.wide[1] // LANE)
+def wide_tiles(count, coarse):
     inner = coarse.row_tiles * coarse.col_tiles
-    return wide, inner
-
-
-def z_tiles(blocks):
-    faces = sum(b.row_tiles * b.col_tiles * 9 + b.row_tiles + b.col_tiles for b in blocks)
-    wide, inner = interface_sizes(*blocks)
-    top = 3 * wide + 3 * inner + 3 * blocks[0].row_tiles * blocks[0].col_tiles
-    return max(faces, top, 9 * wide)
+    return count * inner + -(-count // 2) * coarse.col_tiles + coarse.row_tiles + 1
+
+
+def put_wide(buffer, at, planes, coarse):
+    rows, cols = coarse.rows, coarse.cols
+    for value in planes:
+        at = put(buffer, at, value[:rows, :cols])
+    for ct in range(coarse.col_tiles):
+        for i, value in enumerate(planes):
+            to = 4 * (i % 2)
+            buffer[at + i // 2, to : to + 2] = value[rows : rows + 2, lanes_of(ct)]
+            buffer[at + i // 2, to + 2 : to + 4] = value[rows + SUB - 2 :, lanes_of(ct)]
+        at += -(-len(planes) // 2)
+    slot = jnp.right_shift(iota((SUB, LANE), 1), 2)
+    for rt in range(coarse.row_tiles + 1):
+        tile = jnp.zeros((SUB, LANE), jnp.float32)
+        for i, value in enumerate(planes):
+            tile = jnp.where(slot == i, pltpu.roll(value[rows_of(rt), cols:], 2 + 4 * i, 1), tile)
+        buffer[at] = tile
+        at += 1
+    return at
+
+
+def take_wide(buffer, at, count, coarse):
+    row, lane = iota((SUB, LANE), 0), iota((SUB, LANE), 1)
+    read = lambda spot: buffer[spot]
+    inner = []
+    for _ in range(count):
+        value, at = take(read, at, coarse.rows, coarse.cols)
+        inner.append(value)
+    ends = [[] for _ in range(count)]
+    for ct in range(coarse.col_tiles):
+        for i in range(count):
+            tile = buffer[at + i // 2]
+            start = 4 * (i % 2)
+            ahead = pltpu.roll(tile, (SUB - start) % SUB, 0)
+            behind = pltpu.roll(tile, 4 - start, 0)
+            ends[i].append(jnp.where(row < 2, ahead, jnp.where(row >= SUB - 2, behind, 0.0)))
+        at += -(-count // 2)
+    sides = [[] for _ in range(count)]
+    for rt in range(coarse.row_tiles + 1):
+        for i in range(count):
+            tile = pltpu.roll(buffer[at], LANE - 2 - 4 * i, 1)
+            sides[i].append(jnp.where((lane < 2) | (lane >= LANE - 2), tile, 0.0))
+        at += 1
+    planes = []
+    for i in range(count):
+        left = jnp.concatenate([inner[i], jnp.concatenate(ends[i], axis=1)], axis=0)
+        planes.append(jnp.concatenate([left, jnp.concatenate(sides[i], axis=0)], axis=1))
+    return planes, at
+
+
+def interface_tiles(fine, coarse):
+    top = wide_tiles(3, coarse) + 3 * coarse.row_tiles * coarse.col_tiles
+    return max(top + 3 * fine.row_tiles * fine.col_tiles, wide_tiles(9, coarse))
+
+
+def face_tiles(blocks):
+    return sum(b.row_tiles * b.col_tiles * 9 + b.row_tiles + b.col_tiles for b in blocks)
 
 
 def widen(blocks, sources, halos, got, wides):
@@ -278,10 +368,10 @@
     halos = rest[:2]
     got = rest[2 : 2 + x_count]
     steps_out = rest[2 + x_count : 4 + x_count]
-    first, second, coefs, coefs_coarse, keep = rest[4 + x_count : 9 + x_count]
-    wides = rest[9 + x_count : 11 + x_count]
-    stresses = rest[11 + x_count : 13 + x_count]
-    starts = rest[13 + x_count : 15 + x_count]
+    first, second, third, coefs, coefs_coarse, keep = rest[4 + x_count : 10 + x_count]
+    wides = rest[10 + x_count : 12 + x_count]
+    stresses = rest[12 + x_count : 14 + x_count]
+    starts = rest[14 + x_count : 16 + x_count]
     all_coefs = (coefs, coefs_coarse)
     spot_z, count_z = lax.axis_index("gz"), lax.axis_size("gz")
     even = is_even("gz")
@@ -419,31 +509,30 @@
 
     @pl.when(spot_z == count_z - 1)
     def _():
-        at = 0
         down = restrict([starts[0][c] for c in range(3)], fine, coarse)
-        for plane in down:
-            at = put(second, at, plane)
+        at = put_wide(third, 0, down, coarse)
         down = restrict([keep[c] for c in range(3)], fine, coarse)
         for plane in down:
-            at = put(second, at, plane[: coarse.rows, : coarse.cols])
+            at = put(third, at, plane[: coarse.rows, : coarse.cols])
         for c in range(3):
-            at = put(second, at, keep[3 + c][: fine.rows, : fine.cols])
+            at = put(third, at, keep[3 + c][: fine.rows, : fine.cols])
 
     @pl.when(spot_z == 0)
     def _():
-        wide, _ = interface_sizes(fine, coarse)
+        planes = [[], [], []]
         for i, c in enumerate((4, 3, 2)):
             k = wides[1][coarse.index["k", c, 0]]
             start, below = starts[1][i], starts[1][3 + i]
-            put(second, wide * i, k * (below - start) * 0.25)
-            put(second, wide * (3 + i), k * (below - 0.5 * start) * 0.25)
-            put(second, wide * (6 + i), k * 0.125)
+            planes[0].append(k * (below - start) * 0.25)
+            planes[1].append(k * (below - 0.5 * start) * 0.25)
+            planes[2].append(k * 0.125)
+        put_wide(third, 0, sum(planes, []), coarse)
 
 
 def last_kernel(blocks, *refs):
-    (step_f, step_c, coef_f, coef_c, got_first, got_second, sent, keep) = refs[:8]
-    now_f, now_c, metric, density_f, density_c = refs[8:13]
-    outs = refs[13:15]
+    (step_f, step_c, coef_f, coef_c, got_first, got_second, got_third, sent, keep) = refs[:9]
+    now_f, now_c, metric, density_f, density_c = refs[9:14]
+    outs = refs[14:16]
     fine, coarse = blocks
     spot_z, count_z = lax.axis_index("gz"), lax.axis_size("gz")
     even = is_even("gz")
@@ -545,13 +634,9 @@
                 out[c, layer] = value
         start += 9 * block.row_tiles * block.col_tiles + block.row_tiles + block.col_tiles
 
-    wide, inner = interface_sizes(fine, coarse)
-    height, width = coarse.wide
-
     @pl.when(spot_z == count_z - 1)
     def _():
-        read = lambda at: got_second[at]
-        part = [take(read, wide * i, height, width)[0] for i in range(9)]
+        part, _ = take_wide(got_third, 0, 9, coarse)
         above = [keep[c] for c in range(3)]
         k = [jnp.where(keep[3 + c] > 0, keep[3 + c], 1.0) for c in range(3)]
         raised = prolong([clamp(part[c], coarse) for c in range(3)], fine, coarse)
@@ -564,16 +649,15 @@
 
     @pl.when(spot_z == 0)
     def _():
-        read = lambda at: got_second[at]
-        mine = lambda at: sent[at]
-        tractions = []
+        read = lambda spot: got_third[spot]
+        down, at = take_wide(got_third, 0, 3, coarse)
+        part, _ = take_wide(sent, 0, 9, coarse)
+        tractions = [clamp(part[3 + c] - part[6 + c] * down[c], coarse) for c in range(3)]
+        raised = prolong(tractions, fine, coarse)
+        above = []
         for c in range(3):
-            down = take(read, wide * c, height, width)[0]
-            part = take(mine, wide * (3 + c), height, width)[0]
-            k = take(mine, wide * (6 + c), height, width)[0]
-            tractions.append(clamp(part - k * down, coarse))
-        raised = prolong(tractions, fine, coarse)
-        at = 3 * wide + 3 * inner
+            value, at = take(read, at, coarse.rows, coarse.cols)
+            above.append(value)
         shares = []
         for c in range(3):
             k, at = take(read, at, fine.rows, fine.cols)
@@ -588,8 +672,7 @@
             )
         down = restrict(shares, fine, coarse)
         for c in range(3):
-            above = take(read, 3 * wide + inner * c, coarse.rows, coarse.cols)[0]
-            total = above + down[c][: coarse.rows, : coarse.cols]
+            total = above[c] + down[c][: coarse.rows, : coarse.cols]
             outs[1][c, 0] = 0.5 * (step_c[c, 0] + total)
 
 
@@ -604,14 +687,19 @@
     return jax.ShapeDtypeStruct(shape, jnp.float32)
 
 
-def kernel(body, out_shape, count, scratch=()):
+def kernel(body, out_shape, count, scratch=(), held=False):
     space = pl.BlockSpec(memory_space=pltpu.VMEM)
+    outside = pl.BlockSpec(memory_space=pltpu.HBM) if held else space
+    scratches = [pltpu.VMEM(shape, jnp.float32) for shape in scratch]
+    if held:
+        scratches = [pltpu.SemaphoreType.DMA((count,))]
     return pl.pallas_call(
         body,
         out_shape=out_shape,
-        in_specs=[space] * count,
+        in_specs=[outside] * count,
         out_specs=[space] * len(out_shape),
-        scratch_shapes=[pltpu.VMEM(shape, jnp.float32) for shape in scratch],
+        scratch_shapes=scratches,
+        compiler_params=pltpu.CompilerParams(vmem_limit_bytes=VMEM_BYTES),
     )
 
 
@@ -637,11 +725,16 @@
     count_z = lax.axis_size("gz")
     assert count_z % 2 == 0
 
-    _, row_count = row_table(blocks)
-    sent = kernel(functools.partial(rows_kernel, blocks), [f32(row_count, LANE)] * 2, 9)(*arrays)
+    _, _, row_count = row_table(blocks)
+    *arrays, first, second = kernel(
+        functools.partial(rows_kernel, blocks),
+        [f32(*array.shape) for array in arrays] + [f32(row_count, LANE)] * 2,
+        len(arrays),
+        held=True,
+    )(*[pltpu.with_memory_space_constraint(array, pltpu.HBM) for array in arrays])
     by_row = [
         lax.ppermute(buffer, "gy", pairs) if pairs else jnp.zeros_like(buffer)
-        for buffer, pairs in zip(sent, pair_tables(lax.axis_size("gy")))
+        for buffer, pairs in zip((first, second), pair_tables(lax.axis_size("gy")))
     ]
 
     tables = [pairs for pairs in pair_tables(lax.axis_size("gx")) if pairs]
@@ -657,10 +750,11 @@
         lax.ppermute(buffer, "gx", pairs) for buffer, pairs in zip(made[2:], tables)
     ]
 
-    z_shape = f32(z_tiles(blocks), SUB, LANE)
-    step_f, step_c, first, second, coef_f, coef_c, keep = kernel(
+    z_shape = f32(face_tiles(blocks), SUB, LANE)
+    step_f, step_c, first, second, third, coef_f, coef_c, keep = kernel(
         functools.partial(step_kernel, blocks, len(tables)),
         [f32(*fine_now.shape), f32(*coarse_now.shape), z_shape, z_shape]
+        + [f32(interface_tiles(*blocks), SUB, LANE)]
         + [f32(2, 5, *block.wide) for block in blocks]
         + [f32(6, *fine.wide)],
         11 + len(tables),
@@ -669,18 +763,20 @@
         + [(3, *fine.wide), (6, *coarse.wide)],
     )(*arrays, *halos, *by_column)
     even_pairs, odd_pairs = pair_tables(count_z)
-    odd_pairs = odd_pairs + [(0, count_z - 1), (count_z - 1, 0)]
     got_first = lax.ppermute(first, "gz", even_pairs)
-    got_second = lax.ppermute(second, "gz", odd_pairs)
-
+    got_second = lax.ppermute(second, "gz", odd_pairs) if odd_pairs else jnp.zeros_like(second)
+    got_third = lax.ppermute(third, "gz", [(0, count_z - 1), (count_z - 1, 0)])
+
+    now_f, _, metric, _, density = arrays[:5]
+    now_c, _, _, density_c = arrays[5:]
     return tuple(
         kernel(
             functools.partial(last_kernel, blocks),
             [f32(*fine_now.shape), f32(*coarse_now.shape)],
-            13,
+            14,
         )(
-            step_f, step_c, coef_f, coef_c, got_first, got_second, second, keep,
-            fine_now, coarse_now, metric, density, coarse_density,
+            step_f, step_c, coef_f, coef_c, got_first, got_second, got_third, third, keep,
+            now_f, now_c, metric, density, density_c,
         )
     )
 

time: 46.5 us -> 31.9 us (0.69)
  waiting for transfers between devices: 20 us -> 12 us
  Pallas kernels: 13.2 us -> 5.97 us
  starting transfers between devices: 10.3 us -> 13.1 us
  local copies, waits for them, and re-layouts: 2.02 us -> 0 us
    ppermute x1 -> x2, waiting for transfers between devices: 8.23 us -> 4.91 us  [the longest x1 4.91 us: per_device(): got_third = lax.ppermute(third, 'gz', [(0, count_z - 1), (count_z - 1, 0)])]
    pallas_call x1, Pallas kernels: 4.27 us -> 1.55 us  [per_device(): kernel(functools.partial(step_kernel, blocks, len(tables)), [f32(*fine_no...]
    ppermute x1 -> x2, starting transfers between devices: 3.9 us -> 6.41 us  [the longest x1 5.75 us: per_device(): got_third = lax.ppermute(third, 'gz', [(0, count_z - 1), (count_z - 1, 0)])]
    ppermute x2, waiting for transfers between devices: 8.36 us -> 5.87 us  [per_device(): lax.ppermute(buffer, 'gy', pairs)]
    pallas_call x1, Pallas kernels: 2.87 us -> 0.64 us  [per_device(): kernel(functools.partial(columns_kernel, blocks, len(tables)), halo_shape...]
    unnamed x10 -> x0, local copies, waits for them, and re-layouts: 2.02 us -> none
    ppermute x1, waiting for transfers between devices: 1.97 us -> 0.01 us  [per_device(): got_first = lax.ppermute(first, 'gz', even_pairs)]
    pallas_call x1, Pallas kernels: 3.76 us -> 2.16 us  [per_device(): kernel(functools.partial(last_kernel, blocks), [f32(*fine_now.shape), f32...]
  transfers between devices with their start and end apart: 5 -> 6, of which waited for: 5 -> 4; matrix products, arithmetic and copies ran while one was open for 0% -> 0% of each run, Pallas kernels for 0% -> 0%
where the time goes in v3:
time: 31.9 us; the launch traced here: 31.7 us
  starting transfers between devices  13.1 us (41%)
  waiting for transfers between devices  12 us (38%)
  Pallas kernels  5.97 us (19%)
  between operations  0.7 us (2%)
    ppermute x2, waiting for transfers between devices, per_device(): lax.ppermute(buffer, 'gy', pairs)  5.87 us
    ppermute x1, starting transfers between devices, per_device(): got_third = lax.ppermute(third, 'gz', [(0, count_z - 1), (count_z - 1, 0)])  5.75 us
    ppermute x2, starting transfers between devices, per_device(): lax.ppermute(buffer, 'gy', pairs)  4.94 us
    ppermute x1, waiting for transfers between devices, per_device(): got_third = lax.ppermute(third, 'gz', [(0, count_z - 1), (count_z - 1, 0)])  4.91 us
    pallas_call x1, Pallas kernels, per_device(): kernel(functools.partial(last_kernel, blocks), [f32(*fine_now.shape), f32...  2.16 us
    ppermute x1, starting transfers between devices, per_device(): got_first = lax.ppermute(first, 'gz', even_pairs)  1.64 us
    pallas_call x1, Pallas kernels, per_device(): kernel(functools.partial(rows_kernel, blocks), [f32(*array.shape) for arr...  1.61 us
    pallas_call x1, Pallas kernels, per_device(): kernel(functools.partial(step_kernel, blocks, len(tables)), [f32(*fine_no...  1.55 us
  transfers between devices with their start and end apart: 6, of which 4 were waited for; matrix products, arithmetic and copies ran while one was open for 0% of the time, Pallas kernels for 0%

profile of v3, /device:TPU:2, one launch (start us, length us, event | category | flops | bytes accessed | tf_op | source)
XLA Modules:
  0.0 31.7 jit_solution(15784751156921359070)
XLA Ops:
  0.6 1.6 %shard_map.104 = (f32[3,4,16,256]{3,2,1,0:T(8,128)S(1)}, f32[9,4,16,256]{3,2,1,0:T(8,128)S(1)}, f32[4,16,256]{2,1,0:T(8,128)S(1)}, f32[3,4,16,256]{3,2,1,0:T(8,1...) custom-call(f32[3,4,16,256]{3,2,1,0:T(8,128)} %refs_0_.1, ...), custom_call_target="tpu_custom_call" | custom-call | tf_op jit(solution)/shard_map/pallas_call | solution.py:729
  2.3 0.1 collective-permute-start
  2.3 4.9 %collective-permute-start.1 = (f32[336,128]{1,0:T(8,128)S(1)}, f32[336,128]{1,0:T(8,128)S(1)}, u32[]{:S(2)}, u32[]{:S(2)}) collective-permute-start(f32[336,128]{1,0:T(8,128)S(1)} %get-tuple-element.34), channel_id=1, source_target_pairs={{2,4},{4,2},{3,5},{5,3},{10,12},{12,10},{11,13},{13,11},{18,20},{2... | collective-permute-start | bytes 516104 | tf_op jit(solution)/shard_map/ppermute | solution.py:736
  7.2 1.2 %collective-permute-done.refs_9_ = f32[336,128]{1,0:T(8,128)S(1)} collective-permute-done((f32[336,128]{1,0:T(8,128)S(1)}, f32[336,128]{1,0:T(8,128)S(1)}, u32[]{:S(2)}, u32[]{:S(2)}) %collective-permute-start) | collective-permute-done | bytes 172064 | tf_op jit(solution)/shard_map/ppermute | solution.py:736
  8.4 4.6 %collective-permute-done.1.refs_10_ = f32[336,128]{1,0:T(8,128)S(1)} collective-permute-done((f32[336,128]{1,0:T(8,128)S(1)}, f32[336,128]{1,0:T(8,128)S(1)}, u32[]{:S(2)}, u32[]{:S(2)}) %collective-permute-start.1) | collective-permute-done | bytes 172064 | tf_op jit(solution)/shard_map/ppermute | solution.py:736
  13.1 0.6 %shard_map.105 = (f32[60,8,256]{2,1,0:T(8,128)S(1)}, f32[104,8,128]{2,1,0:T(8,128)S(1)}, f32[14,8,128]{2,1,0:T(8,128)S(1)}) custom-call(f32[3,4,16,256]{3,2,1,0:T(8,128)S(1)} %get-tuple-element.24.refs_0_.refs_9_, f32[9,4,16,256]{3,2,1,0:T(8,128)S(1)} %get-tuple-element.25.refs_1_, f32[4,16,256]{2,1,0:T(8,128)S(1)} %get-tuple-element.26.refs_2_.refs_11_, ...), custom_call_target="tpu_custom_call" | custom-call | tf_op jit(solution)/shard_map/pallas_call | solution.py:743
  13.7 0.1 collective-permute-start.2
  13.8 1.2 %collective-permute-done.2.refs_11_ = f32[14,8,128]{2,1,0:T(8,128)S(1)} collective-permute-done((f32[14,8,128]{2,1,0:T(8,128)S(1)}, f32[14,8,128]{2,1,0:T(8,128)S(1)}, u32[]{:S(2)}, u32[]{:S(2)}) %collective-permute-start.2) | collective-permute-done | bytes 57376 | tf_op jit(solution)/shard_map/ppermute | solution.py:750
  15.0 1.6 %shard_map.106 = (f32[3,4,16,256]{3,2,1,0:T(8,128)S(1)}, f32[3,8,8,128]{3,2,1,0:T(8,128)S(1)}, f32[51,8,128]{2,1,0:T(8,128)S(1)}, f32[51,8,128]{2,1,0:T(8,128)S(...) custom-call(f32[3,4,16,256]{3,2,1,0:T(8,128)S(1)} %get-tuple-element, ...), custom_call_target="tpu_custom_call" | custom-call | tf_op jit(solution)/shard_map/pallas_call | solution.py:754
  16.6 1.6 %collective-permute-start.3 = (f32[51,8,128]{2,1,0:T(8,128)S(1)}, f32[51,8,128]{2,1,0:T(8,128)S(1)}, u32[]{:S(2)}, u32[]{:S(2)}) collective-permute-start(f32[51,8,128]{2,1,0:T(8,128)S(1)} %get-tuple-element.42), channel_id=1, source_target_pairs={{0,8},{16,24},{8,0},{24,16},{1,9},{17,25},{9,1},{25,17},{2,10},{18... | collective-permute-start | bytes 626696 | tf_op jit(solution)/shard_map/ppermute | solution.py:766
  18.2 0.7 %collective-permute-start.4 = (f32[51,8,128]{2,1,0:T(8,128)S(1)}, f32[51,8,128]{2,1,0:T(8,128)S(1)}, u32[]{:S(2)}, u32[]{:S(2)}) collective-permute-start(f32[51,8,128]{2,1,0:T(8,128)S(1)} %get-tuple-element.43), channel_id=1, source_target_pairs={{8,16},{16,8},{9,17},{17,9},{10,18},{18,10},{11,19},{19,11},{12,20... | collective-permute-start | bytes 626696 | tf_op jit(solution)/shard_map/ppermute | solution.py:767
  18.9 5.7 %collective-permute-start.5 = (f32[22,8,128]{2,1,0:T(8,128)S(1)}, f32[22,8,128]{2,1,0:T(8,128)S(1)}, u32[]{:S(2)}, u32[]{:S(2)}) collective-permute-start(f32[22,8,128]{2,1,0:T(8,128)S(1)} %get-tuple-element.44.refs_7_), channel_id=1, source_target_pairs={{0,24},{24,0},{1,25},{25,1},{2,26},{26,2},{3,27},{27,3},{4,28},{28... | collective-permute-start | bytes 270344 | tf_op jit(solution)/shard_map/ppermute | solution.py:768
  24.7 4.9 %collective-permute-done.5.refs_6_ = f32[22,8,128]{2,1,0:T(8,128)S(1)} collective-permute-done((f32[22,8,128]{2,1,0:T(8,128)S(1)}, f32[22,8,128]{2,1,0:T(8,128)S(1)}, u32[]{:S(2)}, u32[]{:S(2)}) %collective-permute-start.5) | collective-permute-done | bytes 90144 | tf_op jit(solution)/shard_map/ppermute | solution.py:768
  29.6 0.0 collective-permute-done.3.refs_4_
  29.6 0.0 collective-permute-done.4.refs_5_
  29.6 2.2 %shard_map.107 = (f32[3,4,16,256]{3,2,1,0:T(8,128)}, f32[3,8,8,128]{3,2,1,0:T(8,128)}) custom-call(f32[3,4,16,256]{3,2,1,0:T(8,128)S(1)} %get-tuple-element.38.refs_0_, f32[3,8,8,128]{3,2,1,0:T(8,128)S(1)} %get-tuple-element.39.refs_1_, f32[2,5,24,384]{3,2,1,0:T(8,128)S(1)} %get-tuple-element.40.refs_2_, f32[2,5,16,256]{3,2,1,0:T(8,128)S(1)} %get-tuple-element.41.refs_3_, ...), custom_call_target="tpu_custom_call" | custom-call | tf_op jit(solution)/shard_map/pallas_call | solution.py:773
Async XLA Ops:
  2.3 6.2 %collective-permute-start = (f32[336,128]{1,0:T(8,128)S(1)}, f32[336,128]{1,0:T(8,128)S(1)}, u32[]{:S(2)}, u32[]{:S(2)}) collective-permute-start(f32[336,128]{1,0:T(8,128)S(1)} %get-tuple-element.33), channel_id=1, source_target_pairs={{0,2},{4,6},{2,0},{6,4},{1,3},{5,7},{3,1},{7,5},{8,10},{12,14},{10... | collective-permute-start | bytes 516104 | tf_op jit(solution)/shard_map/ppermute | solution.py:736
  2.3 10.7 %collective-permute-start.1 = (f32[336,128]{1,0:T(8,128)S(1)}, f32[336,128]{1,0:T(8,128)S(1)}, u32[]{:S(2)}, u32[]{:S(2)}) collective-permute-start(f32[336,128]{1,0:T(8,128)S(1)} %get-tuple-element.34), channel_id=1, source_target_pairs={{2,4},{4,2},{3,5},{5,3},{10,12},{12,10},{11,13},{13,11},{18,20},{2... | collective-permute-start | bytes 516104 | tf_op jit(solution)/shard_map/ppermute | solution.py:736
  13.7 1.3 %collective-permute-start.2 = (f32[14,8,128]{2,1,0:T(8,128)S(1)}, f32[14,8,128]{2,1,0:T(8,128)S(1)}, u32[]{:S(2)}, u32[]{:S(2)}) collective-permute-start(f32[14,8,128]{2,1,0:T(8,128)S(1)} %get-tuple-element.37), channel_id=1, source_target_pairs={{0,1},{1,0},{2,3},{3,2},{4,5},{5,4},{6,7},{7,6},{8,9},{9,8},{10,11... | collective-permute-start | bytes 172040 | tf_op jit(solution)/shard_map/ppermute | solution.py:750
  16.6 13.0 %collective-permute-start.3 = (f32[51,8,128]{2,1,0:T(8,128)S(1)}, f32[51,8,128]{2,1,0:T(8,128)S(1)}, u32[]{:S(2)}, u32[]{:S(2)}) collective-permute-start(f32[51,8,128]{2,1,0:T(8,128)S(1)} %get-tuple-element.42), channel_id=1, source_target_pairs={{0,8},{16,24},{8,0},{24,16},{1,9},{17,25},{9,1},{25,17},{2,10},{18... | collective-permute-start | bytes 626696 | tf_op jit(solution)/shard_map/ppermute | solution.py:766
  18.2 11.3 %collective-permute-start.4 = (f32[51,8,128]{2,1,0:T(8,128)S(1)}, f32[51,8,128]{2,1,0:T(8,128)S(1)}, u32[]{:S(2)}, u32[]{:S(2)}) collective-permute-start(f32[51,8,128]{2,1,0:T(8,128)S(1)} %get-tuple-element.43), channel_id=1, source_target_pairs={{8,16},{16,8},{9,17},{17,9},{10,18},{18,10},{11,19},{19,11},{12,20... | collective-permute-start | bytes 626696 | tf_op jit(solution)/shard_map/ppermute | solution.py:767
  18.9 10.7 %collective-permute-start.5 = (f32[22,8,128]{2,1,0:T(8,128)S(1)}, f32[22,8,128]{2,1,0:T(8,128)S(1)}, u32[]{:S(2)}, u32[]{:S(2)}) collective-permute-start(f32[22,8,128]{2,1,0:T(8,128)S(1)} %get-tuple-element.44.refs_7_), channel_id=1, source_target_pairs={{0,24},{24,0},{1,25},{25,1},{2,26},{26,2},{3,27},{27,3},{4,28},{28... | collective-permute-start | bytes 270344 | tf_op jit(solution)/shard_map/ppermute | solution.py:768

commit v4 on v3

--- a/solution.py
+++ b/solution.py
@@ -104,7 +104,8 @@
 
 
 def rows_kernel(blocks, *refs):
-    held, loaded, (first, second, done) = refs[:9], refs[9:18], refs[18:]
+    held, loaded = refs[:9], refs[9:18]
+    first, second, face_first, face_second, done = refs[18:]
     copies = [
         pltpu.make_async_copy(source, target, done.at[i])
         for i, (source, target) in enumerate(zip(held, loaded))
@@ -137,6 +138,18 @@
                 for t in range(block.col_tiles):
                     if plane[4]:
                         move(b, block, plane, extra[b, p, t], t, plane[3], plane[3] + plane[4])
+
+    even = is_even("gz")
+    at = 0
+    for b, block in enumerate(blocks):
+        for c in range(3):
+            for rt in range(block.row_tiles):
+                for ct in range(block.col_tiles):
+                    low = sources[b]["u"][c, 0, rows_of(rt), lanes_of(ct)]
+                    high = sources[b]["u"][c, block.layers - 1, rows_of(rt), lanes_of(ct)]
+                    face_first[at] = lax.select(even, high, low)
+                    face_second[at] = lax.select(even, low, high)
+                    at += 1
 
 
 def columns_kernel(blocks, both, *refs):
@@ -224,41 +237,78 @@
     return jnp.where(index < (inner + total) // 2, index, index - total)
 
 
-def transfer(fine, coarse, halo, down):
-    shape = (coarse + halo, fine + halo)
-    c = signed(iota(shape, 0), coarse, coarse + halo)
-    f = signed(iota(shape, 1), fine, fine + halo)
+def split_dot(value, matrix):
+    high = value.astype(jnp.bfloat16)
+    rest = value - high.astype(jnp.float32)
+    middle = rest.astype(jnp.bfloat16)
+    low = (rest - middle.astype(jnp.float32)).astype(jnp.bfloat16)
+    parts = jnp.concatenate([high, middle, low], axis=0)
+    out = jnp.dot(parts, matrix.astype(jnp.bfloat16), preferred_element_type=jnp.float32)
+    rows = value.shape[0]
+    return out[:rows] + (out[rows : 2 * rows] + out[2 * rows :])
+
+
+def restrict(planes, spare, fine, coarse):
+    rows, cols = fine.rows, fine.cols
+    row = iota((SUB, fine.wide[1]), 0)
+    stacked = []
+    for i, plane in enumerate(planes):
+        inner = []
+        for t in range(fine.col_tiles + 1):
+            at = (i * (fine.col_tiles + 1) + t) * rows
+            spare[at : at + rows, :] = plane[:rows, lanes_of(t)]
+            even = spare[pl.ds(at, coarse.rows, 2), :]
+            inner.append(even + spare[pl.ds(at + 1, coarse.rows, 2), :])
+        inner = jnp.concatenate(inner, axis=1)
+        pair = plane[rows:]
+        pair = pair + pltpu.roll(pair, SUB - 1, 0)
+        outer = jnp.where(row == 0, pair, 0.0)
+        for to, by in ((1, SUB - 1), (6, 2), (7, 1)):
+            outer = jnp.where(row == to, pltpu.roll(pair, by, 0), outer)
+        stacked += [inner, outer]
+    stacked = 0.25 * jnp.concatenate(stacked, axis=0)
+    inner = jnp.right_shift(iota((cols, coarse.cols), 0), 1) == iota((cols, coarse.cols), 1)
+    f = signed(iota((LANE, LANE), 0), 0, LANE)
+    outer = jnp.right_shift(f, 1) == signed(iota((LANE, LANE), 1), 0, LANE)
+    ones = lambda where: jnp.where(where, 1.0, 0.0)
+    out = jnp.concatenate(
+        [split_dot(stacked[:, :cols], ones(inner)), split_dot(stacked[:, cols:], ones(outer))],
+        axis=1,
+    )
+    height = coarse.wide[0]
+    return [out[i * height : i * height + height] for i in range(len(planes))]
+
+
+def prolong(planes, spare, fine, coarse):
+    shape = (coarse.wide[1], fine.wide[1])
+    c = signed(iota(shape, 0), coarse.cols, shape[0])
+    f = signed(iota(shape, 1), fine.cols, shape[1])
     half = jnp.right_shift(f, 1)
-    if down:
-        return jnp.where(half == c, 0.5, 0.0)
     other = half - 1 + 2 * jnp.bitwise_and(f, 1)
-    return jnp.where(half == c, 0.75, 0.0) + jnp.where(other == c, 0.25, 0.0)
-
-
-def exact_dot(a, b, dims):
-    return lax.dot_general(
-        a, b, (dims, ((), ())), precision=lax.Precision.HIGHEST, preferred_element_type=jnp.float32
-    )
-
-
-def restrict(planes, fine, coarse):
-    rows = fine.wide[0]
-    by_x = transfer(fine.cols, coarse.cols, LANE, True)
-    by_y = transfer(fine.rows, coarse.rows, SUB, True)
-    stacked = exact_dot(jnp.concatenate(planes, axis=0), by_x, ((1,), (1,)))
-    return [
-        exact_dot(by_y, stacked[i * rows : i * rows + rows], ((1,), (0,))) for i in range(3)
-    ]
-
-
-def prolong(planes, fine, coarse):
-    rows = coarse.wide[0]
-    by_x = transfer(fine.cols, coarse.cols, LANE, False)
-    by_y = transfer(fine.rows, coarse.rows, SUB, False)
-    stacked = exact_dot(jnp.concatenate(planes, axis=0), by_x, ((1,), (0,)))
-    return [
-        exact_dot(by_y, stacked[i * rows : i * rows + rows], ((0,), (0,))) for i in range(3)
-    ]
+    by_x = jnp.where(half == c, 0.75, jnp.where(other == c, 0.25, 0.0))
+    height, rows = coarse.wide[0], coarse.rows
+    stacked = split_dot(jnp.concatenate(planes, axis=0), by_x)
+    row = iota((SUB, shape[1]), 0)
+    out = []
+    for i in range(len(planes)):
+        value = stacked[i * height : i * height + height]
+        even = 0.75 * value + 0.25 * pltpu.roll(value, 1, 0)
+        odd = 0.75 * value + 0.25 * pltpu.roll(value, height - 1, 0)
+        inner = []
+        for t in range(fine.col_tiles + 1):
+            at = (i * (fine.col_tiles + 1) + t) * 2 * rows
+            spare[pl.ds(at, rows, 2), :] = even[:rows, lanes_of(t)]
+            spare[pl.ds(at + 1, rows, 2), :] = odd[:rows, lanes_of(t)]
+            inner.append(spare[at : at + 2 * rows, :])
+        inner = jnp.concatenate(inner, axis=1)
+        even, odd = even[rows:], odd[rows:]
+        outer = jnp.where(row == 0, even, odd)
+        for to, by, kind in (
+            (1, 1, odd), (2, 1, even), (3, 2, odd), (4, 6, even), (5, 7, odd), (6, 7, even)
+        ):
+            outer = jnp.where(row == to, pltpu.roll(kind, by, 0), outer)
+        out.append(jnp.concatenate([inner, outer], axis=0))
+    return out
 
 
 def clamp(plane, coarse):
@@ -333,7 +383,19 @@
 
 
 def face_tiles(blocks):
-    return sum(b.row_tiles * b.col_tiles * 9 + b.row_tiles + b.col_tiles for b in blocks)
+    return sum(3 * b.row_tiles * b.col_tiles for b in blocks)
+
+
+def edge_tiles(blocks):
+    return sum(b.row_tiles + b.col_tiles for b in blocks)
+
+
+def neighbours(first, second):
+    even = is_even("gz")
+    return (
+        lambda at: lax.select(even, second[at], first[at]),
+        lambda at: lax.select(even, first[at], second[at]),
+    )
 
 
 def widen(blocks, sources, halos, got, wides):
@@ -365,19 +427,30 @@
 
 def step_kernel(blocks, x_count, *refs):
     sources, rest = named(refs)
-    halos = rest[:2]
+    halos, face_first, face_second, rest = rest[:2], rest[2], rest[3], rest[2:]
     got = rest[2 : 2 + x_count]
     steps_out = rest[2 + x_count : 4 + x_count]
-    first, second, third, coefs, coefs_coarse, keep = rest[4 + x_count : 10 + x_count]
-    wides = rest[10 + x_count : 12 + x_count]
-    stresses = rest[12 + x_count : 14 + x_count]
-    starts = rest[14 + x_count : 16 + x_count]
+    first, second, coefs, coefs_coarse, keep = rest[4 + x_count : 9 + x_count]
+    wides = rest[9 + x_count : 11 + x_count]
+    stresses = rest[11 + x_count : 13 + x_count]
+    starts = rest[13 + x_count : 15 + x_count]
+    spare = rest[15 + x_count]
     all_coefs = (coefs, coefs_coarse)
     spot_z, count_z = lax.axis_index("gz"), lax.axis_size("gz")
     even = is_even("gz")
     widen(blocks, sources, halos, got, wides)
-
-    for b, block in enumerate(blocks):
+    before, after = neighbours(face_first, face_second)
+
+    start = 0
+    for b, block in enumerate(blocks):
+        beyond = [[], []]
+        for c in range(3):
+            for side, read in enumerate((before, after)):
+                plane, _ = take(read, start, block.rows, block.cols)
+                plane = jnp.concatenate([plane, jnp.zeros((SUB, block.cols), jnp.float32)], axis=0)
+                plane = jnp.concatenate([plane, jnp.zeros((block.wide[0], LANE), jnp.float32)], axis=1)
+                beyond[side].append(plane)
+            start += block.row_tiles * block.col_tiles
         wide, stress = wides[b], stresses[b]
         layers, rows, cols, inverse = block.layers, block.rows, block.cols, block.inverse_step
         half = count_z * layers // 2
@@ -409,8 +482,8 @@
             stretch = stretched(layer)
             dz = [
                 along_z(
-                    field("u", c, layer - 1) if layer else None,
-                    field("u", c, layer + 1) if layer < layers - 1 else None,
+                    field("u", c, layer - 1) if layer else beyond[0][c],
+                    field("u", c, layer + 1) if layer < layers - 1 else beyond[1][c],
                     stretch,
                 )
                 for c in range(3)
@@ -481,12 +554,8 @@
         for rt in range(block.row_tiles):
             for ct in range(block.col_tiles):
                 spot = (rows_of(rt), lanes_of(ct))
-                for c in range(3):
-                    send(sources[b]["u"][(c, 0) + spot], sources[b]["u"][(c, last) + spot])
                 for kind in (XZ, YZ, ZZ):
                     send(stresses[b][(kind, 0) + spot], stresses[b][(kind, last) + spot])
-                for i in range(3):
-                    send(all_coefs[b][(0, i) + spot], all_coefs[b][(1, i) + spot])
         for ct in range(block.col_tiles):
             for c in range(3):
                 low = block.index["u", c, 0]
@@ -509,13 +578,13 @@
 
     @pl.when(spot_z == count_z - 1)
     def _():
-        down = restrict([starts[0][c] for c in range(3)], fine, coarse)
-        at = put_wide(third, 0, down, coarse)
-        down = restrict([keep[c] for c in range(3)], fine, coarse)
-        for plane in down:
-            at = put(third, at, plane[: coarse.rows, : coarse.cols])
+        planes = [starts[0][c] for c in range(3)] + [keep[c] for c in range(3)]
+        down = restrict(planes, spare, fine, coarse)
+        at = put_wide(second, 0, down[:3], coarse)
+        for plane in down[3:]:
+            at = put(second, at, plane[: coarse.rows, : coarse.cols])
         for c in range(3):
-            at = put(third, at, keep[3 + c][: fine.rows, : fine.cols])
+            at = put(second, at, keep[3 + c][: fine.rows, : fine.cols])
 
     @pl.when(spot_z == 0)
     def _():
@@ -526,32 +595,31 @@
             planes[0].append(k * (below - start) * 0.25)
             planes[1].append(k * (below - 0.5 * start) * 0.25)
             planes[2].append(k * 0.125)
-        put_wide(third, 0, sum(planes, []), coarse)
+        put_wide(second, 0, sum(planes, []), coarse)
 
 
 def last_kernel(blocks, *refs):
-    (step_f, step_c, coef_f, coef_c, got_first, got_second, got_third, sent, keep) = refs[:9]
-    now_f, now_c, metric, density_f, density_c = refs[9:14]
-    outs = refs[14:16]
+    (step_f, step_c, coef_f, coef_c, got_first, got_second, sent, keep) = refs[:8]
+    metric, density_f, density_c = refs[8:11]
+    outs, spare = refs[11:13], refs[13]
     fine, coarse = blocks
     spot_z, count_z = lax.axis_index("gz"), lax.axis_size("gz")
-    even = is_even("gz")
-    inside = (spot_z > 0, spot_z < count_z - 1)
-    lane = iota((SUB, LANE), 1)
-
-    def reader(side):
-        def read(at):
-            one, two = got_first[at], got_second[at]
-            value = lax.select(even, two, one) if side == 0 else lax.select(even, one, two)
-            return lax.select(inside[side], value, jnp.zeros_like(value))
-
-        return read
+    lane, row = iota((SUB, LANE), 1), iota((SUB, LANE), 0)
+
+    def inside(read, there):
+        def masked(at):
+            value = read(at)
+            return lax.select(there, value, jnp.zeros_like(value))
+
+        return masked
+
+    before, after = neighbours(got_first, got_second)
+    readers = inside(before, spot_z > 0), inside(after, spot_z < count_z - 1)
 
     start = 0
     for b, block in enumerate(blocks):
         rows, cols, layers, inverse = block.rows, block.cols, block.layers, block.inverse_step
         half = count_z * layers // 2
-        now = (now_f, now_c)[b]
         step = (step_f, step_c)[b]
         density = (density_f, density_c)[b]
         coef = (coef_f, coef_c)[b]
@@ -571,17 +639,51 @@
             )
             return value * factor
 
-        for side, layer, inner in ((0, 0, 1), (1, layers - 1, layers - 2)):
-            read = reader(side)
+        for side, layer in enumerate((0, layers - 1)):
+            read = readers[side]
             sign = -1.0 if side == 0 else 1.0
             tiles = block.row_tiles * block.col_tiles
-
-            def plane(k):
-                return jnp.concatenate(
+            beyond = []
+            for c in range(3):
+                edges = []
+                for ct in range(block.col_tiles):
+                    tile = read(start + 3 * tiles + ct)
+                    ahead = pltpu.roll(tile, (SUB - c) % SUB, 0)
+                    behind = pltpu.roll(tile, 3 - c, 0)
+                    edges.append(
+                        jnp.where(row == 0, ahead, jnp.where(row == SUB - 1, behind, 0.0))
+                    )
+                sides = []
+                for rt in range(block.row_tiles):
+                    tile = read(start + 3 * tiles + block.col_tiles + rt)
+                    tile = pltpu.roll(tile, LANE - 1 - 2 * c, 1)
+                    sides.append(jnp.where((lane == 0) | (lane == LANE - 1), tile, 0.0))
+                beyond.append(
+                    (
+                        sign * jnp.concatenate(edges, axis=1),
+                        sign * jnp.concatenate(sides, axis=0),
+                    )
+                )
+
+            def over_x(k, value):
+                halo = coef[side, k, :rows, cols:] * value
+                left = jnp.zeros((rows, cols), jnp.float32)
+                return slope(jnp.concatenate([left, halo], axis=1), 1)[:, :cols] * inverse
+
+            def over_y(k, value):
+                halo = coef[side, k, rows:, :cols] * value
+                left = jnp.zeros((rows, cols), jnp.float32)
+                return slope(jnp.concatenate([left, halo], axis=0), 0)[:rows] * inverse
+
+            add(0, layer, over_x(3, beyond[2][1]))
+            add(1, layer, over_y(4, beyond[2][0]))
+            add(2, layer, over_x(0, beyond[0][1]) + over_y(1, beyond[1][0]))
+            for c in range(3):
+                there = jnp.concatenate(
                     [
                         jnp.concatenate(
                             [
-                                read(start + 9 * (rt * block.col_tiles + ct) + k)
+                                read(start + 3 * (rt * block.col_tiles + ct) + c)
                                 for ct in range(block.col_tiles)
                             ],
                             axis=1,
@@ -590,70 +692,35 @@
                     ],
                     axis=0,
                 )
-
-            row = iota((SUB, LANE), 0)
-            beyond = []
-            for c in range(3):
-                edges = []
-                for ct in range(block.col_tiles):
-                    tile = read(start + 9 * tiles + ct)
-                    ahead = pltpu.roll(tile, (SUB - c) % SUB, 0)
-                    behind = pltpu.roll(tile, 3 - c, 0)
-                    edges.append(
-                        jnp.where(row == 0, ahead, jnp.where(row == SUB - 1, behind, 0.0))
-                    )
-                sides = []
-                for rt in range(block.row_tiles):
-                    tile = read(start + 9 * tiles + block.col_tiles + rt)
-                    tile = pltpu.roll(tile, LANE - 1 - 2 * c, 1)
-                    sides.append(jnp.where((lane == 0) | (lane == LANE - 1), tile, 0.0))
-                sides.append(jnp.zeros((SUB, LANE), jnp.float32))
-                left = jnp.concatenate(
-                    [plane(c), jnp.concatenate(edges, axis=1)], axis=0
-                )
-                beyond.append(
-                    sign * jnp.concatenate([left, jnp.concatenate(sides, axis=0)], axis=1)
-                )
-            d_xz = coef[side, 0] * beyond[0]
-            d_yz = coef[side, 1] * beyond[1]
-            d_zz = coef[side, 2] * beyond[2]
-            d_xx = coef[side, 3] * beyond[2]
-            d_yy = coef[side, 4] * beyond[2]
-            add(0, layer, slope(d_xx, 1)[:rows, :cols] * inverse)
-            add(1, layer, slope(d_yy, 0)[:rows, :cols] * inverse)
-            add(2, layer, (slope(d_xz, 1) + slope(d_yz, 0))[:rows, :cols] * inverse)
-            for c, change in enumerate((d_xz, d_yz, d_zz)):
-                there = plane(3 + c) - sign * plane(6 + c) * now[c, layer]
                 add(c, layer, stretched(layer, sign * there))
-                add(c, inner, stretched(inner, sign * change[:rows, :cols]))
         for layer in range(layers):
             for c in range(3):
                 value = step[c, layer]
                 if (c, layer) in extra:
                     value = value + ALPHA * extra[c, layer] / density[layer]
                 out[c, layer] = value
-        start += 9 * block.row_tiles * block.col_tiles + block.row_tiles + block.col_tiles
+        start += 3 * block.row_tiles * block.col_tiles + block.row_tiles + block.col_tiles
 
     @pl.when(spot_z == count_z - 1)
     def _():
-        part, _ = take_wide(got_third, 0, 9, coarse)
+        part, _ = take_wide(got_second, 0, 9, coarse)
         above = [keep[c] for c in range(3)]
         k = [jnp.where(keep[3 + c] > 0, keep[3 + c], 1.0) for c in range(3)]
-        raised = prolong([clamp(part[c], coarse) for c in range(3)], fine, coarse)
-        down = restrict([above[c] + raised[c] / k[c] for c in range(3)], fine, coarse)
+        raised = prolong([clamp(part[c], coarse) for c in range(3)], spare, fine, coarse)
+        down = restrict([above[c] + raised[c] / k[c] for c in range(3)], spare, fine, coarse)
         tractions = [clamp(part[3 + c] - part[6 + c] * down[c], coarse) for c in range(3)]
-        raised = prolong(tractions, fine, coarse)
+        raised = prolong(tractions, spare, fine, coarse)
         for c in range(3):
             value = above[c] + raised[c] / k[c]
             outs[0][c, fine.layers - 1] = value[: fine.rows, : fine.cols]
 
     @pl.when(spot_z == 0)
     def _():
-        read = lambda spot: got_third[spot]
-        down, at = take_wide(got_third, 0, 3, coarse)
+        read = lambda spot: got_second[spot]
+        down, at = take_wide(got_second, 0, 3, coarse)
         part, _ = take_wide(sent, 0, 9, coarse)
         tractions = [clamp(part[3 + c] - part[6 + c] * down[c], coarse) for c in range(3)]
-        raised = prolong(tractions, fine, coarse)
+        raised = prolong(tractions, spare, fine, coarse)
         above = []
         for c in range(3):
             value, at = take(read, at, coarse.rows, coarse.cols)
@@ -670,7 +737,7 @@
                     [share, jnp.zeros((fine.wide[0], LANE), jnp.float32)], axis=1
                 )
             )
-        down = restrict(shares, fine, coarse)
+        down = restrict(shares, spare, fine, coarse)
         for c in range(3):
             total = above[c] + down[c][: coarse.rows, : coarse.cols]
             outs[1][c, 0] = 0.5 * (step_c[c, 0] + total)
@@ -726,9 +793,12 @@
     assert count_z % 2 == 0
 
     _, _, row_count = row_table(blocks)
-    *arrays, first, second = kernel(
+    face_shape = f32(face_tiles(blocks), SUB, LANE)
+    *arrays, first, second, face_first, face_second = kernel(
         functools.partial(rows_kernel, blocks),
-        [f32(*array.shape) for array in arrays] + [f32(row_count, LANE)] * 2,
+        [f32(*array.shape) for array in arrays]
+        + [f32(row_count, LANE)] * 2
+        + [face_shape] * 2,
         len(arrays),
         held=True,
     )(*[pltpu.with_memory_space_constraint(array, pltpu.HBM) for array in arrays])
@@ -736,6 +806,17 @@
         lax.ppermute(buffer, "gy", pairs) if pairs else jnp.zeros_like(buffer)
         for buffer, pairs in zip((first, second), pair_tables(lax.axis_size("gy")))
     ]
+
+    even_pairs, odd_pairs = pair_tables(count_z)
+
+    def swap_z(first, second):
+        if odd_pairs:
+            got = lax.ppermute(second, "gz", odd_pairs)
+        else:
+            got = jnp.zeros_like(second)
+        return lax.ppermute(first, "gz", even_pairs), got
+
+    faces = swap_z(face_first, face_second)
 
     tables = [pairs for pairs in pair_tables(lax.axis_size("gx")) if pairs]
     tiles = sum(block.x_tiles() for block in blocks)
@@ -750,33 +831,36 @@
         lax.ppermute(buffer, "gx", pairs) for buffer, pairs in zip(made[2:], tables)
     ]
 
-    z_shape = f32(face_tiles(blocks), SUB, LANE)
-    step_f, step_c, first, second, third, coef_f, coef_c, keep = kernel(
+    count = max(face_tiles(blocks) + edge_tiles(blocks), interface_tiles(*blocks))
+    z_shape = f32(count, SUB, LANE)
+    step_f, step_c, first, second, coef_f, coef_c, keep = kernel(
         functools.partial(step_kernel, blocks, len(tables)),
         [f32(*fine_now.shape), f32(*coarse_now.shape), z_shape, z_shape]
-        + [f32(interface_tiles(*blocks), SUB, LANE)]
         + [f32(2, 5, *block.wide) for block in blocks]
         + [f32(6, *fine.wide)],
-        11 + len(tables),
+        13 + len(tables),
         [(len(block.planes), *block.wide) for block in blocks]
         + [(6, block.layers, *block.wide) for block in blocks]
-        + [(3, *fine.wide), (6, *coarse.wide)],
-    )(*arrays, *halos, *by_column)
-    even_pairs, odd_pairs = pair_tables(count_z)
-    got_first = lax.ppermute(first, "gz", even_pairs)
-    got_second = lax.ppermute(second, "gz", odd_pairs) if odd_pairs else jnp.zeros_like(second)
-    got_third = lax.ppermute(third, "gz", [(0, count_z - 1), (count_z - 1, 0)])
-
-    now_f, _, metric, _, density = arrays[:5]
-    now_c, _, _, density_c = arrays[5:]
+        + [(3, *fine.wide), (6, *coarse.wide)]
+        + [(6 * (fine.col_tiles + 1) * fine.rows, LANE)],
+    )(*arrays, *halos, *faces, *by_column)
+    with jax.named_scope("z_second"):
+        got_second = lax.ppermute(
+            second, "gz", odd_pairs + [(0, count_z - 1), (count_z - 1, 0)]
+        )
+    with jax.named_scope("z_first"):
+        got_first = lax.ppermute(first, "gz", even_pairs)
+
+    metric, density, density_c = arrays[2], arrays[4], arrays[8]
     return tuple(
         kernel(
             functools.partial(last_kernel, blocks),
             [f32(*fine_now.shape), f32(*coarse_now.shape)],
-            14,
+            11,
+            [(3 * (fine.col_tiles + 1) * fine.rows, LANE)],
         )(
-            step_f, step_c, coef_f, coef_c, got_first, got_second, got_third, third, keep,
-            now_f, now_c, metric, density, density_c,
+            step_f, step_c, coef_f, coef_c, got_first, got_second, second, keep,
+            metric, density, density_c,
         )
     )
 

time: 31.9 us -> 26.9 us (0.84)
  waiting for transfers between devices: 12 us -> 9.48 us
  starting transfers between devices: 13.1 us -> 11.5 us
  Pallas kernels: 5.97 us -> 5.11 us
    ppermute x2, waiting for transfers between devices: 5.87 us -> 3.51 us  [per_device(): lax.ppermute(buffer, 'gy', pairs)]
    ppermute x2 -> x3, starting transfers between devices: 6.41 us -> 4.82 us  [the longest x1 2.47 us: per_device(): lax.ppermute(second, 'gz', odd_pairs + [(0, count_z - 1), (count_z - 1, 0)])]
    pallas_call x1, Pallas kernels: 2.16 us -> 1.33 us  [per_device(): kernel(functools.partial(last_kernel, blocks), [f32(*fine_now.shape), f32...]
    ppermute x2 -> x3, waiting for transfers between devices: 4.91 us -> 4.13 us  [the longest x1 4.13 us: per_device(): lax.ppermute(second, 'gz', odd_pairs + [(0, count_z - 1), (count_z - 1, 0)])]
    ppermute x1, waiting for transfers between devices: 0.01 us -> 0.63 us  [per_device(): got_first = lax.ppermute(first, 'gz', even_pairs)]
  transfers between devices with their start and end apart: 6 -> 7, of which waited for: 4 -> 4; matrix products, arithmetic and copies ran while one was open for 0% -> 0% of each run, Pallas kernels for 0% -> 2%
where the time goes in v4:
time: 26.9 us; the launch traced here: 26.8 us
  starting transfers between devices  11.5 us (43%)
  waiting for transfers between devices  9.48 us (35%)
  Pallas kernels  5.11 us (19%)
  between operations  0.71 us (3%)
    ppermute x2, starting transfers between devices, per_device(): lax.ppermute(buffer, 'gy', pairs)  4.94 us
    ppermute x1, waiting for transfers between devices, per_device(): lax.ppermute(second, 'gz', odd_pairs + [(0, count_z - 1), (count_z - 1, 0)])  4.13 us
    ppermute x2, waiting for transfers between devices, per_device(): lax.ppermute(buffer, 'gy', pairs)  3.51 us
    ppermute x1, starting transfers between devices, per_device(): lax.ppermute(second, 'gz', odd_pairs + [(0, count_z - 1), (count_z - 1, 0)])  2.47 us
    ppermute x1, starting transfers between devices, swap_z(): return (lax.ppermute(first, 'gz', even_pairs), got)  1.69 us
    ppermute x1, starting transfers between devices, per_device(): got_first = lax.ppermute(first, 'gz', even_pairs)  1.64 us
    pallas_call x1, Pallas kernels, per_device(): kernel(functools.partial(rows_kernel, blocks), [f32(*array.shape) for arr...  1.63 us
    pallas_call x1, Pallas kernels, per_device(): kernel(functools.partial(step_kernel, blocks, len(tables)), [f32(*fine_no...  1.52 us
  transfers between devices with their start and end apart: 7, of which 4 were waited for; matrix products, arithmetic and copies ran while one was open for 0% of the time, Pallas kernels for 2%

profile of v4, /device:TPU:2, one launch (start us, length us, event | category | flops | bytes accessed | tf_op | source)
XLA Modules:
  0.0 26.8 jit_solution(11146211695947257404)
XLA Ops:
  0.6 1.6 %shard_map.104 = (f32[3,4,16,256]{3,2,1,0:T(8,128)S(1)}, f32[9,4,16,256]{3,2,1,0:T(8,128)S(1)}, f32[4,16,256]{2,1,0:T(8,128)S(1)}, f32[3,4,16,256]{3,2,1,0:T(8,1...) custom-call(f32[3,4,16,256]{3,2,1,0:T(8,128)} %refs_0_.1, ...), custom_call_target="tpu_custom_call" | custom-call | tf_op jit(solution)/shard_map/pallas_call | solution.py:797
  2.3 0.1 collective-permute-start
  2.3 4.9 %collective-permute-start.1 = (f32[336,128]{1,0:T(8,128)S(1)}, f32[336,128]{1,0:T(8,128)S(1)}, u32[]{:S(2)}, u32[]{:S(2)}) collective-permute-start(f32[336,128]{1,0:T(8,128)S(1)} %get-tuple-element.35), channel_id=1, source_target_pairs={{2,4},{4,2},{3,5},{5,3},{10,12},{12,10},{11,13},{13,11},{18,20},{2... | collective-permute-start | bytes 516104 | tf_op jit(solution)/shard_map/ppermute | solution.py:806
  7.2 1.7 %collective-permute-start.2 = (f32[15,8,128]{2,1,0:T(8,128)S(1)}, f32[15,8,128]{2,1,0:T(8,128)S(1)}, u32[]{:S(2)}, u32[]{:S(2)}) collective-permute-start(f32[15,8,128]{2,1,0:T(8,128)S(1)} %get-tuple-element.38), channel_id=1, source_target_pairs={{0,8},{16,24},{8,0},{24,16},{1,9},{17,25},{9,1},{25,17},{2,10},{18... | collective-permute-start | bytes 184328 | tf_op jit(solution)/shard_map/ppermute | solution.py:817
  8.9 0.7 %collective-permute-start.3 = (f32[15,8,128]{2,1,0:T(8,128)S(1)}, f32[15,8,128]{2,1,0:T(8,128)S(1)}, u32[]{:S(2)}, u32[]{:S(2)}) collective-permute-start(f32[15,8,128]{2,1,0:T(8,128)S(1)} %get-tuple-element.39), channel_id=1, source_target_pairs={{8,16},{16,8},{9,17},{17,9},{10,18},{18,10},{11,19},{19,11},{12,20... | collective-permute-start | bytes 184328 | tf_op jit(solution)/shard_map/ppermute | solution.py:814
  9.6 0.0 collective-permute-done.refs_9_
  9.6 3.5 %collective-permute-done.1.refs_10_ = f32[336,128]{1,0:T(8,128)S(1)} collective-permute-done((f32[336,128]{1,0:T(8,128)S(1)}, f32[336,128]{1,0:T(8,128)S(1)}, u32[]{:S(2)}, u32[]{:S(2)}) %collective-permute-start.1) | collective-permute-done | bytes 172064 | tf_op jit(solution)/shard_map/ppermute | solution.py:806
  13.1 0.6 %shard_map.105 = (f32[60,8,256]{2,1,0:T(8,128)S(1)}, f32[104,8,128]{2,1,0:T(8,128)S(1)}, f32[14,8,128]{2,1,0:T(8,128)S(1)}) custom-call(f32[3,4,16,256]{3,2,1,0:T(8,128)S(1)} %get-tuple-element.25.refs_0_, f32[9,4,16,256]{3,2,1,0:T(8,128)S(1)} %get-tuple-element.26.refs_1_, f32[4,16,256]{2,1,0:T(8,128)S(1)} %get-tuple-element.27.refs_2_.refs_8_, ...), custom_call_target="tpu_custom_call" | custom-call | tf_op jit(solution)/shard_map/pallas_call | solution.py:824
  13.7 0.1 collective-permute-start.4
  13.8 0.0 collective-permute-done.2.refs_11_
  13.8 0.0 collective-permute-done.3.refs_12_
  13.8 1.2 %collective-permute-done.4.refs_13_ = f32[14,8,128]{2,1,0:T(8,128)S(1)} collective-permute-done((f32[14,8,128]{2,1,0:T(8,128)S(1)}, f32[14,8,128]{2,1,0:T(8,128)S(1)}, u32[]{:S(2)}, u32[]{:S(2)}) %collective-permute-start.4) | collective-permute-done | bytes 57376 | tf_op jit(solution)/shard_map/ppermute | solution.py:831
  15.0 1.5 %shard_map.106 = (f32[3,4,16,256]{3,2,1,0:T(8,128)S(1)}, f32[3,8,8,128]{3,2,1,0:T(8,128)S(1)}, f32[22,8,128]{2,1,0:T(8,128)S(1)}, f32[22,8,128]{2,1,0:T(8,128)S(...) custom-call(f32[3,4,16,256]{3,2,1,0:T(8,128)S(1)} %get-tuple-element.25.refs_0_, ...), custom_call_target="tpu_custom_call" | custom-call | tf_op jit(solution)/shard_map/pallas_call | solution.py:836
  16.6 1.6 %collective-permute-start.5 = (f32[22,8,128]{2,1,0:T(8,128)S(1)}, f32[22,8,128]{2,1,0:T(8,128)S(1)}, u32[]{:S(2)}, u32[]{:S(2)}) collective-permute-start(f32[22,8,128]{2,1,0:T(8,128)S(1)} %get-tuple-element.45), channel_id=1, source_target_pairs={{0,8},{16,24},{8,0},{24,16},{1,9},{17,25},{9,1},{25,17},{2,10},{18... | collective-permute-start | bytes 270344 | tf_op jit(solution)/shard_map/z_first/ppermute | solution.py:852
  18.2 2.5 %collective-permute-start.6 = (f32[22,8,128]{2,1,0:T(8,128)S(1)}, f32[22,8,128]{2,1,0:T(8,128)S(1)}, u32[]{:S(2)}, u32[]{:S(2)}) collective-permute-start(f32[22,8,128]{2,1,0:T(8,128)S(1)} %get-tuple-element.46.refs_6_), channel_id=1, source_target_pairs={{8,16},{16,8},{0,24},{24,0},{9,17},{17,9},{1,25},{25,1},{10,18},{1... | collective-permute-start | bytes 270344 | tf_op jit(solution)/shard_map/z_second/ppermute | solution.py:848
  20.7 0.6 %collective-permute-done.5.refs_4_ = f32[22,8,128]{2,1,0:T(8,128)S(1)} collective-permute-done((f32[22,8,128]{2,1,0:T(8,128)S(1)}, f32[22,8,128]{2,1,0:T(8,128)S(1)}, u32[]{:S(2)}, u32[]{:S(2)}) %collective-permute-start.5) | collective-permute-done | bytes 90144 | tf_op jit(solution)/shard_map/z_first/ppermute | solution.py:852
  21.3 4.1 %collective-permute-done.6.refs_5_ = f32[22,8,128]{2,1,0:T(8,128)S(1)} collective-permute-done((f32[22,8,128]{2,1,0:T(8,128)S(1)}, f32[22,8,128]{2,1,0:T(8,128)S(1)}, u32[]{:S(2)}, u32[]{:S(2)}) %collective-permute-start.6) | collective-permute-done | bytes 90144 | tf_op jit(solution)/shard_map/z_second/ppermute | solution.py:848
  25.5 1.3 %shard_map.107 = (f32[3,4,16,256]{3,2,1,0:T(8,128)}, f32[3,8,8,128]{3,2,1,0:T(8,128)}) custom-call(f32[3,4,16,256]{3,2,1,0:T(8,128)S(1)} %get-tuple-element.41.refs_0_, f32[3,8,8,128]{3,2,1,0:T(8,128)S(1)} %get-tuple-element.42.refs_1_, f32[2,5,24,384]{3,2,1,0:T(8,128)S(1)} %get-tuple-element.43.refs_2_, f32[2,5,16,256]{3,2,1,0:T(8,128)S(1)} %get-tuple-element.44.refs_3_, ...), custom_call_target="tpu_custom_call" | custom-call | tf_op jit(solution)/shard_map/pallas_call | solution.py:856
Async XLA Ops:
  2.3 7.3 %collective-permute-start = (f32[336,128]{1,0:T(8,128)S(1)}, f32[336,128]{1,0:T(8,128)S(1)}, u32[]{:S(2)}, u32[]{:S(2)}) collective-permute-start(f32[336,128]{1,0:T(8,128)S(1)} %get-tuple-element.34), channel_id=1, source_target_pairs={{0,2},{4,6},{2,0},{6,4},{1,3},{5,7},{3,1},{7,5},{8,10},{12,14},{10... | collective-permute-start | bytes 516104 | tf_op jit(solution)/shard_map/ppermute | solution.py:806
  2.3 10.7 %collective-permute-start.1 = (f32[336,128]{1,0:T(8,128)S(1)}, f32[336,128]{1,0:T(8,128)S(1)}, u32[]{:S(2)}, u32[]{:S(2)}) collective-permute-start(f32[336,128]{1,0:T(8,128)S(1)} %get-tuple-element.35), channel_id=1, source_target_pairs={{2,4},{4,2},{3,5},{5,3},{10,12},{12,10},{11,13},{13,11},{18,20},{2... | collective-permute-start | bytes 516104 | tf_op jit(solution)/shard_map/ppermute | solution.py:806
  7.2 6.6 %collective-permute-start.2 = (f32[15,8,128]{2,1,0:T(8,128)S(1)}, f32[15,8,128]{2,1,0:T(8,128)S(1)}, u32[]{:S(2)}, u32[]{:S(2)}) collective-permute-start(f32[15,8,128]{2,1,0:T(8,128)S(1)} %get-tuple-element.38), channel_id=1, source_target_pairs={{0,8},{16,24},{8,0},{24,16},{1,9},{17,25},{9,1},{25,17},{2,10},{18... | collective-permute-start | bytes 184328 | tf_op jit(solution)/shard_map/ppermute | solution.py:817
  8.9 4.9 %collective-permute-start.3 = (f32[15,8,128]{2,1,0:T(8,128)S(1)}, f32[15,8,128]{2,1,0:T(8,128)S(1)}, u32[]{:S(2)}, u32[]{:S(2)}) collective-permute-start(f32[15,8,128]{2,1,0:T(8,128)S(1)} %get-tuple-element.39), channel_id=1, source_target_pairs={{8,16},{16,8},{9,17},{17,9},{10,18},{18,10},{11,19},{19,11},{12,20... | collective-permute-start | bytes 184328 | tf_op jit(solution)/shard_map/ppermute | solution.py:814
  13.7 1.3 %collective-permute-start.4 = (f32[14,8,128]{2,1,0:T(8,128)S(1)}, f32[14,8,128]{2,1,0:T(8,128)S(1)}, u32[]{:S(2)}, u32[]{:S(2)}) collective-permute-start(f32[14,8,128]{2,1,0:T(8,128)S(1)} %get-tuple-element.40), channel_id=1, source_target_pairs={{0,1},{1,0},{2,3},{3,2},{4,5},{5,4},{6,7},{7,6},{8,9},{9,8},{10,11... | collective-permute-start | bytes 172040 | tf_op jit(solution)/shard_map/ppermute | solution.py:831
  16.6 4.7 %collective-permute-start.5 = (f32[22,8,128]{2,1,0:T(8,128)S(1)}, f32[22,8,128]{2,1,0:T(8,128)S(1)}, u32[]{:S(2)}, u32[]{:S(2)}) collective-permute-start(f32[22,8,128]{2,1,0:T(8,128)S(1)} %get-tuple-element.45), channel_id=1, source_target_pairs={{0,8},{16,24},{8,0},{24,16},{1,9},{17,25},{9,1},{25,17},{2,10},{18... | collective-permute-start | bytes 270344 | tf_op jit(solution)/shard_map/z_first/ppermute | solution.py:852
  18.2 7.2 %collective-permute-start.6 = (f32[22,8,128]{2,1,0:T(8,128)S(1)}, f32[22,8,128]{2,1,0:T(8,128)S(1)}, u32[]{:S(2)}, u32[]{:S(2)}) collective-permute-start(f32[22,8,128]{2,1,0:T(8,128)S(1)} %get-tuple-element.46.refs_6_), channel_id=1, source_target_pairs={{8,16},{16,8},{0,24},{24,0},{9,17},{17,9},{1,25},{25,1},{10,18},{1... | collective-permute-start | bytes 270344 | tf_op jit(solution)/shard_map/z_second/ppermute | solution.py:848
